TPU v7x, 512 devices: a 8x2x16 block of a 8x8x16 slice. The times are simulated.
512 devices in a mesh: groups: 2 (over y), seq: 16 (over z), vocab: 8 (over x), batch: 2 (over core).
Axes of the slice: x: 8, y: 2, z: 16, core: 2. Of those that a mesh axis runs over, the one named last changes fastest.
The devices are a block of a 8x8x16 slice.
Arguments:
- queries: bfloat16 [32, 3072, 3584], P(('groups', 'vocab', 'batch'), 'seq'), parts along dimension 0, may hold values from -300 to 300
- keys: bfloat16 [32, 3072, 512], P(('groups', 'vocab', 'batch'), 'seq'), parts along dimension 0, may hold values from -10 to 10
- values: bfloat16 [32, 3072, 512], P(('groups', 'vocab', 'batch'), 'seq'), parts along dimension 0, may hold values from -24 to 24
- residual: bfloat16 [32, 3072, 3584], P(('groups', 'vocab', 'batch'), 'seq'), parts along dimension 0, may hold values from -2048 to 2048
- norm_gain: float32 [3584], replicated, may hold values from 0.5 to 1.5
Outputs:
- normed: bfloat16 [32, 3072, 3584], P(('groups', 'vocab', 'batch'), 'seq'), parts along dimension 0
There are 2 independent parts, one for each index of `groups`. A program takes and returns all parts, laid end to end along the dimension named above; an argument that names none is the same for every part. Nothing has to cross between parts.
All inputs are finite; a program needn't handle non-finite values.
Results may differ from a plain program's by a relative error of at most 0.0049.
Values may be sent and summed in bfloat16 or wider, within the bound.
No kernel may reach another device: no remote copies, remote signals or barrier semaphores. Data moves between devices by JAX's collectives and lax.ppermute only.
A program may use at most 128 MiB of HBM per device.

v0:
```python
import math

import jax
import jax.numpy as jnp
from jax import lax
from jax.sharding import PartitionSpec as P

HEAD_WIDTH = 128


group_slots = 8
norm_eps = 1e-06


def attend_block(query_block, key_seen, value_seen, first_row):
    scores = jnp.einsum("qhd,kd->hqk", query_block, key_seen, preferred_element_type=jnp.float32)
    scores = scores * (1.0 / math.sqrt(query_block.shape[2]))
    query_pos = first_row + jnp.arange(query_block.shape[0])
    key_pos = jnp.arange(key_seen.shape[0])
    allowed = key_pos[None, :] <= query_pos[:, None]
    scores = jnp.where(allowed[None], scores, -jnp.inf)
    row_max = jnp.max(scores, axis=2, keepdims=True)
    weights = jnp.exp(scores - row_max)
    soft_probs = (weights / jnp.sum(weights, axis=2, keepdims=True)).astype(jnp.bfloat16)
    output = jnp.einsum("hqk,kd->qhd", soft_probs, value_seen, preferred_element_type=jnp.float32)
    return output.astype(jnp.bfloat16)


def body(queries, keys, values, residual, norm_gain):
    seq_count = lax.axis_size("seq")
    seq_rows = queries.shape[1]
    total_rows = seq_rows * seq_count
    kv_heads = keys.shape[2] // HEAD_WIDTH
    q_heads = queries.shape[2] // HEAD_WIDTH
    queries_per_group = q_heads // kv_heads
    padded = kv_heads * group_slots
    local_heads = padded // seq_count
    query_rows = queries[0].reshape(seq_rows, kv_heads, queries_per_group, HEAD_WIDTH)
    query_pad = jnp.pad(
        query_rows, ((0, 0), (0, 0), (0, group_slots - queries_per_group), (0, 0))
    ).reshape(seq_rows, padded * HEAD_WIDTH)
    key_rows = keys[0].reshape(seq_rows, kv_heads, HEAD_WIDTH)
    value_rows = values[0].reshape(seq_rows, kv_heads, HEAD_WIDTH)
    key_send = jnp.repeat(key_rows, seq_count // kv_heads, axis=1).reshape(
        seq_rows, seq_count * HEAD_WIDTH
    )
    value_send = jnp.repeat(value_rows, seq_count // kv_heads, axis=1).reshape(
        seq_rows, seq_count * HEAD_WIDTH
    )
    query_here, key_here, value_here = (
        lax.all_to_all(query_pad, "seq", split_axis=1, concat_axis=0, tiled=True),
        lax.all_to_all(key_send, "seq", split_axis=1, concat_axis=0, tiled=True),
        lax.all_to_all(value_send, "seq", split_axis=1, concat_axis=0, tiled=True),
    )
    query_here = query_here.reshape(total_rows, local_heads, HEAD_WIDTH)
    block_rows = 512
    outputs = []
    for block_index in range(total_rows // block_rows):
        first_row = block_index * block_rows
        last_row = first_row + block_rows
        outputs.append(
            attend_block(
                query_here[first_row:last_row],
                key_here[:last_row],
                value_here[:last_row],
                first_row,
            )
        )
    attended = jnp.concatenate(outputs, axis=0).reshape(total_rows, local_heads * HEAD_WIDTH)
    returned = lax.all_to_all(attended, "seq", split_axis=0, concat_axis=1, tiled=True)
    attention = returned.reshape(seq_rows, kv_heads, group_slots, HEAD_WIDTH)[
        :, :, :queries_per_group
    ].reshape(seq_rows, q_heads * HEAD_WIDTH)
    hidden = residual[0].astype(jnp.float32) + attention.astype(jnp.float32)
    inv_rms = lax.rsqrt(jnp.mean(hidden * hidden, axis=1, keepdims=True) + norm_eps)
    normed = (hidden * inv_rms * norm_gain).astype(jnp.bfloat16)
    return normed[None]


def solution(mesh):
    return jax.shard_map(
        body,
        mesh=mesh,
        in_specs=(
            P(("groups", "vocab", "batch"), "seq", None),
            P(("groups", "vocab", "batch"), "seq", None),
            P(("groups", "vocab", "batch"), "seq", None),
            P(("groups", "vocab", "batch"), "seq", None),
            P(),
        ),
        out_specs=P(("groups", "vocab", "batch"), "seq", None),
        check_vma=False,
    )
```

profile of v0, /device:TPU:72, one launch (start us, length us, event | category | flops | bytes accessed | tf_op | source)
XLA Modules:
  0.0 371.8 jit_solution(17336687048558871853)
XLA Ops:
  2.1 43.7 %all-to-all-start.1 = ((bf16[192,16,128]{2,0,1:T(8,128)(2,1)}), bf16[192,16,128]{2,0,1:T(8,128)(2,1)S(1)}, u32[]{:S(2)}, u32[]{:S(2)}) async-start(bf16[192,16,128]{2,0,1:T(8,128)(2,1)} %bitcast.1), calls=%async_computation.1 | async-start | bytes 1572864 | tf_op jit(solution)/shard_map/all_to_all | solution.py:52
  45.9 38.8 %all-to-all-done.1 = bf16[192,16,128]{2,0,1:T(8,128)(2,1)S(1)} async-done(((bf16[192,16,128]{2,0,1:T(8,128)(2,1)}), bf16[192,16,128]{2,0,1:T(8,128)(2,1)S(1)}, u32[]{:S(2)}, u32[]{:S(2)}) %all-to-all-start.1) | async-done | bytes 786464 | tf_op jit(solution)/shard_map/all_to_all | solution.py:52
  85.8 7.8 %all-to-all-start.2 = ((bf16[192,16,128]{2,0,1:T(8,128)(2,1)}), bf16[192,16,128]{2,0,1:T(8,128)(2,1)}, u32[]{:S(2)}, u32[]{:S(2)}) async-start(bf16[192,16,128]{2,0,1:T(8,128)(2,1)} %bitcast.6), calls=%async_computation.2 | async-start | bytes 1572864 | tf_op jit(solution)/shard_map/all_to_all | solution.py:53
  98.0 34.7 %all-to-all-done.2 = bf16[192,16,128]{2,0,1:T(8,128)(2,1)} async-done(((bf16[192,16,128]{2,0,1:T(8,128)(2,1)}), bf16[192,16,128]{2,0,1:T(8,128)(2,1)}, u32[]{:S(2)}, u32[]{:S(2)}) %all-to-all-start.2) | async-done | bytes 786464 | tf_op jit(solution)/shard_map/all_to_all | solution.py:53
  132.6 8.0 %all-to-all-start = ((bf16[192,16,256]{2,0,1:T(8,128)(2,1)}), bf16[192,16,256]{2,0,1:T(8,128)(2,1)S(1)}, u32[]{:S(2)}, u32[]{:S(2)}) async-start(bf16[192,16,256]{2,0,1:T(8,128)(2,1)} %copy.20), calls=%async_computation | async-start | bytes 3145728 | tf_op jit(solution)/shard_map/all_to_all | solution.py:51
  147.5 2.4 iota_compare_fusion
  151.7 63.1 %all-to-all-done = bf16[192,16,256]{2,0,1:T(8,128)(2,1)S(1)} async-done(((bf16[192,16,256]{2,0,1:T(8,128)(2,1)}), bf16[192,16,256]{2,0,1:T(8,128)(2,1)S(1)}, u32[]{:S(2)}, u32[]{:S(2)}) %all-to-all-start) | async-done | bytes 1572896 | tf_op jit(solution)/shard_map/all_to_all | solution.py:51
  215.2 2.0 fusion.124
  217.7 2.3 fusion.125
  220.0 3.6 fusion.126
  224.7 4.4 %fusion.131 = (f32[2,512]{1,0:T(2,128)S(1)}, f32[2,512,1536]{2,1,0:T(8,128)}) fusion(f32[512,2,1536]{2,0,1:T(8,128)S(1)} %fusion.86, pred[512,1536]{1,0:T(8,128)(4,1)S(1)} %copy-done.9), kind=kOutput, calls=%fused_computation.147 | output fusion | flops 9438719 | bytes 13373440 | tf_op jit(solution)/shard_map/sub | solution.py:23
  229.1 7.4 %fusion.132 = (f32[2,512]{1,0:T(2,128)S(1)}, f32[2,512,2048]{2,1,0:T(8,128)}) fusion(pred[512,2048]{1,0:T(8,128)(4,1)S(1)} %copy-done.8, bf16[3072,128]{1,0:T(8,128)(2,1)S(1)} %bitcast.179, bf16[512,2,128]{2,1,0:T(2,128)(2,1)} %get-tuple-element.7), kind=kOutput, calls=%fused_computation.148 | convolution fusion | flops 545261568 | bytes 10227712 | tf_op jit(solution)/shard_map/sub | solution.py:23
  236.6 6.0 %fusion.137 = (f32[2,512]{1,0:T(2,128)S(1)}, f32[2,512,2560]{2,1,0:T(8,128)}) fusion(pred[512,2560]{1,0:T(8,128)(4,1)S(1)} %copy-done.7, bf16[3072,128]{1,0:T(8,128)(2,1)S(1)} %bitcast.180, bf16[512,2,128]{2,1,0:T(2,128)(2,1)S(1)} %copy-done.13), kind=kOutput, calls=%fused_computation.149 | convolution fusion | flops 681576960 | bytes 12718080 | tf_op jit(solution)/shard_map/sub | solution.py:23
  242.6 3.0 fusion.64
  245.5 3.8 %fusion.74 = bf16[3072,2,128]{2,0,1:T(8,128)(2,1)} fusion(bf16[3072,2,128]{2,0,1:T(8,128)(2,1)} %fusion.64, f32[2,512,1024]{2,1,0:T(8,128)} %get-tuple-element.14, f32[2,512]{1,0:T(2,128)S(1)} %get-tuple-element.13, bf16[3072,128]{1,0:T(8,128)(2,1)} %bitcast.8), kind=kOutput, calls=%fused_computation.94 | convolution fusion | flops 270663680 | bytes 4722688 | tf_op jit(solution)/shard_map/hqk,kd->qhd/dot_general | solution.py:25
  251.8 3.9 %fusion.70 = bf16[3072,2,128]{2,0,1:T(8,128)(2,1)} fusion(bf16[3072,2,128]{2,0,1:T(8,128)(2,1)} %fusion.72, f32[2,512,2048]{2,1,0:T(8,128)S(1)} %bitcast.187, f32[2,512]{1,0:T(2,128)S(1)} %get-tuple-element.17, bf16[3072,128]{1,0:T(8,128)(2,1)} %bitcast.8), kind=kOutput, calls=%fused_computation.90 | convolution fusion | flops 541196288 | bytes 9179136 | tf_op jit(solution)/shard_map/hqk,kd->qhd/dot_general | solution.py:25
  255.7 3.5 fusion.68
  259.2 7.0 %fusion.142 = (f32[2,512]{1,0:T(2,128)S(1)}, f32[2,512,3072]{2,1,0:T(8,128)}) fusion(pred[512,3072]{1,0:T(8,128)(4,1)S(1)} %copy-done.5, bf16[3072,128,1]{1,0,2:T(8,128)(2,1)S(1)} %bitcast.181, bf16[512,2,128]{2,1,0:T(2,128)(2,1)S(1)} %copy-done.12), kind=kOutput, calls=%fused_computation.150 | convolution fusion | flops 817892352 | bytes 15208448 | tf_op jit(solution)/shard_map/sub | solution.py:23
  266.2 7.2 %fusion.66 = bf16[3072,2,128]{2,0,1:T(8,128)(2,1)} fusion(bf16[3072,2,128]{2,0,1:T(8,128)(2,1)} %fusion.68, bf16[3072,128,1]{1,0,2:T(8,128)(2,1)} %bitcast.33, f32[2,512,3072]{2,1,0:T(8,128)} %get-tuple-element.22, f32[2,512]{1,0:T(2,128)S(1)} %get-tuple-element.21), kind=kOutput, calls=%fused_computation.86 | convolution fusion | flops 811728896 | bytes 13635584 | tf_op jit(solution)/shard_map/hqk,kd->qhd/dot_general | solution.py:25
  273.4 3.9 %copy.30 = bf16[3072,2,128]{2,1,0:T(2,128)(2,1)S(1)} copy(bf16[3072,2,128]{2,0,1:T(8,128)(2,1)} %fusion.66) | data formatting | bytes 3145728 | tf_op jit(solution)/shard_map/concatenate | solution.py:69
  278.3 80.1 %all_to_all.70 = bf16[16,192,256]{2,1,0:T(8,128)(2,1)S(1)} all-to-all(bf16[16,192,256]{2,1,0:T(8,128)(2,1)S(1)} %all_to_all.63), channel_id=1, replica_groups=mesh['groups'=2,'seq'=16,'vocab'=8,'batch'=2] {'seq'}, dimensions={0} | all-to-all | bytes 3145728 | tf_op jit(solution)/shard_map/all_to_all | solution.py:70
  359.3 2.0 reshape.207
  363.2 1.9 reshape.210
  366.8 2.8 fusion.47
  (85 shorter events, 28.5 us)
Async XLA Ops:
  0.0 45.8 %copy-start.16 = (bf16[1,192,512]{2,1,0:T(8,128)(2,1)S(1)}, bf16[1,192,512]{2,1,0:T(8,128)(2,1)}, u32[]{:S(2)}) copy-start(bf16[1,192,512]{2,1,0:T(8,128)(2,1)} %param.7) | copy-start | bytes 589828
  1.0 92.6 %copy-start.6 = (bf16[1,192,3584]{2,1,0:T(8,128)(2,1)S(1)}, bf16[1,192,3584]{2,1,0:T(8,128)(2,1)}, u32[]{:S(2)}) copy-start(bf16[1,192,3584]{2,1,0:T(8,128)(2,1)} %param.5) | copy-start | bytes 4128772
  2.1 82.6 %all-to-all-start.1 = ((bf16[192,16,128]{2,0,1:T(8,128)(2,1)}), bf16[192,16,128]{2,0,1:T(8,128)(2,1)S(1)}, u32[]{:S(2)}, u32[]{:S(2)}) async-start(bf16[192,16,128]{2,0,1:T(8,128)(2,1)} %bitcast.1), calls=%async_computation.1 | async-start | bytes 1572864 | tf_op jit(solution)/shard_map/all_to_all | solution.py:52
  85.8 46.8 %all-to-all-start.2 = ((bf16[192,16,128]{2,0,1:T(8,128)(2,1)}), bf16[192,16,128]{2,0,1:T(8,128)(2,1)}, u32[]{:S(2)}, u32[]{:S(2)}) async-start(bf16[192,16,128]{2,0,1:T(8,128)(2,1)} %bitcast.6), calls=%async_computation.2 | async-start | bytes 1572864 | tf_op jit(solution)/shard_map/all_to_all | solution.py:53
  132.6 82.2 %all-to-all-start = ((bf16[192,16,256]{2,0,1:T(8,128)(2,1)}), bf16[192,16,256]{2,0,1:T(8,128)(2,1)S(1)}, u32[]{:S(2)}, u32[]{:S(2)}) async-start(bf16[192,16,256]{2,0,1:T(8,128)(2,1)} %copy.20), calls=%async_computation | async-start | bytes 3145728 | tf_op jit(solution)/shard_map/all_to_all | solution.py:51
  140.6 9.3 %copy-start.3 = (bf16[192,16,128]{2,0,1:T(8,128)(2,1)S(1)}, bf16[192,16,128]{2,0,1:T(8,128)(2,1)}, u32[]{:S(2)}) copy-start(bf16[192,16,128]{2,0,1:T(8,128)(2,1)} %copy-done.2) | copy-start | bytes 2359300
  215.2 2.4 copy-start.15
  217.7 2.3 copy-start.10
  224.7 4.4 %copy-start.8 = (pred[512,2048]{1,0:T(8,128)(4,1)S(1)}, pred[512,2048]{1,0:T(8,128)(4,1)}, u32[]{:S(2)}) copy-start(pred[512,2048]{1,0:T(8,128)(4,1)} %iota_compare_fusion.2) | copy-start | bytes 3145732
  229.1 7.4 %copy-start.7 = (pred[512,2560]{1,0:T(8,128)(4,1)S(1)}, pred[512,2560]{1,0:T(8,128)(4,1)}, u32[]{:S(2)}) copy-start(pred[512,2560]{1,0:T(8,128)(4,1)} %iota_compare_fusion.1) | copy-start | bytes 3932164
  229.1 7.4 %copy-start.13 = (bf16[512,2,128]{2,1,0:T(2,128)(2,1)S(1)}, bf16[512,2,128]{2,1,0:T(2,128)(2,1)}, u32[]{:S(2)}) copy-start(bf16[512,2,128]{2,1,0:T(2,128)(2,1)} %get-tuple-element.6) | copy-start | bytes 786436
  242.6 6.8 %slice-start = ((s8[6291456]{0:T(1024)(128)(4,1)}), s8[4194304]{0:T(1024)(128)(4,1)S(1)}, s32[]{:S(2)}) async-start(s8[6291456]{0:T(1024)(128)(4,1)} %bitcast.184), calls=%async_computation.4 | async-start | bytes 8388608
  245.5 3.8 %copy-start.11 = (bf16[8,192,128]{2,1,0:T(8,128)(2,1)S(1)}, bf16[8,192,128]{2,1,0:T(8,128)(2,1)}, u32[]{:S(2)}) copy-start(bf16[8,192,128]{2,1,0:T(8,128)(2,1)} %slice.84) | copy-start | bytes 1179652
  245.5 3.8 %slice-start.1 = ((s8[6291456]{0:T(1024)(128)(4,1)}), s8[2097152]{0:T(1024)(128)(4,1)S(1)}, s32[]{:S(2)}) async-start(s8[6291456]{0:T(1024)(128)(4,1)} %bitcast.184), calls=%async_computation.5 | async-start | bytes 4194304
  245.5 5.7 %slice-start.2 = ((s8[8388608]{0:T(1024)(128)(4,1)}), s8[4194304]{0:T(1024)(128)(4,1)S(1)}, s32[]{:S(2)}) async-start(s8[8388608]{0:T(1024)(128)(4,1)} %bitcast.186), calls=%async_computation.6 | async-start | bytes 8388608
  249.4 2.4 slice-start.3
  249.4 6.3 %slice-start.4 = ((s8[10485760]{0:T(1024)(128)(4,1)}), s8[4194304]{0:T(1024)(128)(4,1)S(1)}, s32[]{:S(2)}) async-start(s8[10485760]{0:T(1024)(128)(4,1)} %bitcast.188), calls=%async_computation.8 | async-start | bytes 8388608
  249.4 6.3 %slice-start.5 = ((s8[10485760]{0:T(1024)(128)(4,1)}), s8[4194304]{0:T(1024)(128)(4,1)S(1)}, s32[]{:S(2)}) async-start(s8[10485760]{0:T(1024)(128)(4,1)} %bitcast.188), calls=%async_computation.9 | async-start | bytes 8388608
  251.8 3.9 %slice-start.6 = ((s8[10485760]{0:T(1024)(128)(4,1)}), s8[2097152]{0:T(1024)(128)(4,1)S(1)}, s32[]{:S(2)}) async-start(s8[10485760]{0:T(1024)(128)(4,1)} %bitcast.188), calls=%async_computation.10 | async-start | bytes 4194304
  255.7 3.5 copy-start.5
  255.7 3.5 copy-start.12
  365.0 4.6 %copy-start.17 = (f32[3584]{0:T(1024)S(1)}, f32[3584]{0:T(1024)}, u32[]{:S(2)}) copy-start(f32[3584]{0:T(1024)} %param.9) | copy-start | bytes 43012
  366.8 3.0 copy-start
  366.8 3.4 copy-start.1
  (4 other events, 6.6 us)
where the time goes:
time: 372 us
  waiting for transfers between devices  137 us (37%)
  blocking collectives  80.1 us (22%)
  starting transfers between devices  59.5 us (16%)
  matrix products  48.5 us (13%)
  local copies, waits for them, and re-layouts  24.7 us (7%)
  other arithmetic  22.2 us (6%)
    all_to_all x1, blocking collectives, body(): lax.all_to_all(attended, 'seq', split_axis=0, concat_axis=1, tiled=True)  80.1 us
    all_to_all x1, waiting for transfers between devices, body(): lax.all_to_all(query_pad, 'seq', split_axis=1, concat_axis=0, tiled=True)  63.1 us
    all_to_all x1, starting transfers between devices, body(): lax.all_to_all(key_send, 'seq', split_axis=1, concat_axis=0, tiled=True)  43.7 us
    all_to_all x1, waiting for transfers between devices, body(): lax.all_to_all(key_send, 'seq', split_axis=1, concat_axis=0, tiled=True)  38.8 us
    all_to_all x1, waiting for transfers between devices, body(): lax.all_to_all(value_send, 'seq', split_axis=1, concat_axis=0, tiled=True)  34.7 us
    sub x4, matrix products, attend_block(): weights = jnp.exp(scores - row_max)  23.9 us
    dot_general x6, matrix products, attend_block(): jnp.einsum('hqk,kd->qhd', soft_probs, value_seen, preferred_element_type=...  23.2 us
    le x6, other arithmetic, attend_block(): allowed = key_pos[None, :] <= query_pos[:, None]  9.25 us
  transfers between devices with their start and end apart: 3, of which 3 were waited for; matrix products, arithmetic and copies ran while one was open for 4% of the time, Pallas kernels for 0%

commit v1 on v0

v1 whole, which is shorter than its diff:
```python
import functools
import math

import jax
import jax.numpy as jnp
from jax import lax
from jax.experimental import pallas as pl
from jax.experimental.pallas import tpu as pltpu
from jax.sharding import PartitionSpec as P


HEAD_WIDTH = 128
NORM_EPS = 1e-06
SCALE = math.log2(math.e) / math.sqrt(HEAD_WIDTH)
VMEM_LIMIT = 12 * 1024 * 1024


def lanes(col, width):
    reps = -(-width // HEAD_WIDTH)
    wide = jnp.concatenate([col] * reps, axis=1) if reps > 1 else col
    return wide[:, :width]


def attend(query, key, value_ones, old, causal):
    scores = lax.dot_general(query, key, (((1,), (1,)), ((), ())), preferred_element_type=jnp.float32)
    rows, width = scores.shape
    if causal:
        row = lax.broadcasted_iota(jnp.int32, scores.shape, 0)
        col = lax.broadcasted_iota(jnp.int32, scores.shape, 1)
        scores = jnp.where(col <= row, scores, -jnp.inf)
    top_here = jnp.max(scores, axis=1, keepdims=True) * SCALE
    if old is None:
        top = jnp.broadcast_to(top_here, (rows, HEAD_WIDTH))
    else:
        top = jnp.maximum(old[2], top_here)
    weights = jnp.exp2(scores * SCALE - lanes(top, width))
    summed = jnp.dot(weights.astype(jnp.bfloat16), value_ones, preferred_element_type=jnp.float32)
    acc, total = summed[:, :HEAD_WIDTH], summed[:, HEAD_WIDTH:]
    if old is not None:
        fade = jnp.exp2(old[2] - top)
        acc = old[0] * fade + acc
        total = old[1] * fade + total
    return acc, total, top


def group_key_value(blocks, group, kv_heads):
    key_at = pl.ds(pl.multiple_of(group * HEAD_WIDTH, HEAD_WIDTH), HEAD_WIDTH)
    value_at = pl.ds(pl.multiple_of((kv_heads + group) * HEAD_WIDTH, HEAD_WIDTH), HEAD_WIDTH)
    key = jnp.concatenate([b[:, key_at] for b in blocks], axis=0)
    value = jnp.concatenate([b[:, value_at] for b in blocks], axis=0)
    return key, jnp.concatenate([value, jnp.ones_like(value)], axis=1)


def each_head(q_ref, blocks, acc_ref, total_ref, top_ref, q_heads, kv_heads, first):
    per_group = q_heads // kv_heads

    def one_group(group, carry):
        key, value_ones = group_key_value(blocks, group, kv_heads)
        for i in range(per_group):
            head = group * per_group + i
            query = q_ref[:, pl.ds(pl.multiple_of(head * HEAD_WIDTH, HEAD_WIDTH), HEAD_WIDTH)]
            old = None if first else (acc_ref[head], total_ref[head], top_ref[head])
            acc, total, top = attend(query, key, value_ones, old, first)
            acc_ref[head] = acc
            total_ref[head] = total
            top_ref[head] = top
        return carry

    lax.fori_loop(0, kv_heads, one_group, 0)


def first_kernel(_place, q_ref, kv_ref, q_out, acc_ref, total_ref, top_ref, *, q_heads, kv_heads):
    q_out[...] = q_ref[...]
    each_head(q_ref, (kv_ref,), acc_ref, total_ref, top_ref, q_heads, kv_heads, True)


def step_kernel(place_ref, q_ref, f_ref, b_ref, _a, _t, _m, acc_ref, total_ref, top_ref, *, step, count, q_heads, kv_heads):
    place = place_ref[0]
    wrapped = place + step >= count

    @pl.when(wrapped)
    def _():
        each_head(q_ref, (f_ref, b_ref), acc_ref, total_ref, top_ref, q_heads, kv_heads, False)

    @pl.when(jnp.logical_and(place >= step, jnp.logical_not(wrapped)))
    def _():
        each_head(q_ref, (f_ref,), acc_ref, total_ref, top_ref, q_heads, kv_heads, False)


def last_kernel(
    place_ref, q_ref, f_ref, b_ref, residual_ref, gain_ref, _a, _t, _m, acc_ref, total_ref, top_ref, out_ref,
    *, step, q_heads, kv_heads,
):
    @pl.when(place_ref[0] >= step)
    def _():
        each_head(q_ref, (f_ref, b_ref), acc_ref, total_ref, top_ref, q_heads, kv_heads, False)

    rows, width = out_ref.shape
    square = jnp.zeros((rows, HEAD_WIDTH), jnp.float32)
    for head in range(q_heads):
        at = slice(head * HEAD_WIDTH, (head + 1) * HEAD_WIDTH)
        attended = (acc_ref[head] / total_ref[head]).astype(jnp.bfloat16).astype(jnp.float32)
        hidden = residual_ref[:, at].astype(jnp.float32) + attended
        acc_ref[head] = hidden
        square = square + hidden * hidden
    inv_rms = lax.rsqrt(jnp.sum(square, axis=1, keepdims=True) / width + NORM_EPS)
    inv_rms = jnp.broadcast_to(inv_rms, (rows, HEAD_WIDTH))
    for head in range(q_heads):
        at = slice(head * HEAD_WIDTH, (head + 1) * HEAD_WIDTH)
        out_ref[:, at] = (acc_ref[head] * inv_rms * gain_ref[:, at]).astype(jnp.bfloat16)


def shift(array, pairs):
    return lax.ppermute(array, "seq", pairs)


def layer(queries, keys, values, residual, norm_gain):
    count = lax.axis_size("seq")
    half = count // 2
    query = queries[0]
    rows, width = query.shape
    q_heads = width // HEAD_WIDTH
    kv_heads = keys.shape[2] // HEAD_WIDTH
    place = lax.axis_index("seq").astype(jnp.int32).reshape(1)
    own = jnp.concatenate([keys[0], values[0]], axis=1)
    right = [(i, (i + 1) % count) for i in range(count)]
    left = [(i, (i - 1) % count) for i in range(count)]
    state_shape = (q_heads, rows, HEAD_WIDTH)
    state = pltpu.VMEM(state_shape, jnp.float32)
    vmem = pl.BlockSpec(memory_space=pltpu.VMEM)
    smem = pl.BlockSpec(memory_space=pltpu.SMEM)
    params = pltpu.CompilerParams(vmem_limit_bytes=VMEM_LIMIT)

    def cost(keys_seen):
        return pl.CostEstimate(
            flops=4 * q_heads * rows * keys_seen * HEAD_WIDTH,
            transcendentals=q_heads * rows * keys_seen,
            bytes_accessed=4 * rows * width,
        )

    forward = shift(own, right)
    backward = shift(own, left)
    query, acc, total, top = pl.pallas_call(
        functools.partial(first_kernel, q_heads=q_heads, kv_heads=kv_heads),
        out_shape=(pltpu.VMEM(query.shape, query.dtype), state, state, state),
        in_specs=[smem, vmem, vmem],
        out_specs=(vmem, vmem, vmem, vmem),
        compiler_params=params,
        cost_estimate=cost(rows),
        name="first",
    )(place, query, own)
    for step in range(1, half):
        if step + 1 < half:
            forward_next = shift(forward, right)
            backward_next = shift(backward, left)
        else:
            forward_next = shift(forward[: rows // 2], right)
            backward_next = shift(backward[rows // 2 :], left)
        acc, total, top = pl.pallas_call(
            functools.partial(step_kernel, step=step, count=count, q_heads=q_heads, kv_heads=kv_heads),
            out_shape=(state, state, state),
            in_specs=[smem] + [vmem] * 6,
            out_specs=(vmem, vmem, vmem),
            input_output_aliases={4: 0, 5: 1, 6: 2},
            compiler_params=params,
            cost_estimate=cost(2 * rows),
        )(place, query, forward, backward, acc, total, top)
        forward, backward = forward_next, backward_next
    _, _, _, normed = pl.pallas_call(
        functools.partial(last_kernel, step=half, q_heads=q_heads, kv_heads=kv_heads),
        out_shape=(state, state, state, jax.ShapeDtypeStruct((rows, width), jnp.bfloat16)),
        in_specs=[smem] + [vmem] * 8,
        out_specs=(vmem, vmem, vmem, vmem),
        input_output_aliases={6: 0, 7: 1, 8: 2},
        compiler_params=params,
        cost_estimate=cost(rows),
        name="last",
    )(place, query, forward, backward, residual[0], norm_gain.reshape(1, width), acc, total, top)
    return normed[None]


def solution(mesh):
    placed = P(("groups", "vocab", "batch"), "seq", None)
    return jax.shard_map(
        layer,
        mesh=mesh,
        in_specs=(placed, placed, placed, placed, P()),
        out_specs=placed,
        check_vma=False,
    )
```

time: 372 us -> 174 us (0.47)
  the two profiles are of different devices: /device:TPU:72 before, /device:TPU:94 now
where the time goes in v1:
time: 174 us; the launch traced here: 173 us
  starting transfers between devices  128 us (74%)
  waiting for transfers between devices  30 us (17%)
  local copies, waits for them, and re-layouts  7.3 us (4%)
  Pallas kernels  6.98 us (4%)
    ppermute x16, starting transfers between devices, shift(): return lax.ppermute(array, 'seq', pairs)  128 us
    ppermute x16, waiting for transfers between devices, shift(): return lax.ppermute(array, 'seq', pairs)  30 us
    unnamed x16, local copies, waits for them, and re-layouts  6.54 us
    pallas_call x1, Pallas kernels, layer(): pl.pallas_call(functools.partial(first_kernel, q_heads=q_heads, kv_heads=...  3.82 us
  transfers between devices with their start and end apart: 16, of which 11 were waited for; matrix products, arithmetic and copies ran while one was open for 0% of the time, Pallas kernels for 3%

profile of v1, /device:TPU:94, one launch (start us, length us, event | category | flops | bytes accessed | tf_op | source)
XLA Modules:
  0.0 173.5 jit_solution(12701705531851279954)
XLA Ops:
  1.1 44.0 %collective-permute-start.8 = (bf16[192,1024]{1,0:T(8,128)(2,1)S(1)}, bf16[192,1024]{1,0:T(8,128)(2,1)S(1)}, u32[]{:S(2)}, u32[]{:S(2)}) collective-permute-start(bf16[192,1024]{1,0:T(8,128)(2,1)S(1)} %pad_maximum_fusion.kv_ref), channel_id=1, source_target_pairs={{0,240},{16,0},{32,16},{48,32},{64,48},{80,64},{96,80},{112,96},{1... | collective-permute-start | bytes 1179656 | tf_op jit(solution)/shard_map/ppermute | solution.py:114
  45.1 2.0 %collective-permute-start = (bf16[192,1024]{1,0:T(8,128)(2,1)S(1)}, bf16[192,1024]{1,0:T(8,128)(2,1)S(1)}, u32[]{:S(2)}, u32[]{:S(2)}) collective-permute-start(bf16[192,1024]{1,0:T(8,128)(2,1)S(1)} %pad_maximum_fusion.kv_ref), channel_id=1, source_target_pairs={{0,16},{16,32},{32,48},{48,64},{64,80},{80,96},{96,112},{112,128},... | collective-permute-start | bytes 1179656 | tf_op jit(solution)/shard_map/ppermute | solution.py:114
  47.1 6.5 %collective-permute-done.8.b_ref = bf16[192,1024]{1,0:T(8,128)(2,1)S(1)} collective-permute-done((bf16[192,1024]{1,0:T(8,128)(2,1)S(1)}, bf16[192,1024]{1,0:T(8,128)(2,1)S(1)}, u32[]{:S(2)}, u32[]{:S(2)}) %collective-permute-start.8) | collective-permute-done | bytes 393248 | tf_op jit(solution)/shard_map/ppermute | solution.py:114
  53.5 5.6 %collective-permute-start.9 = (bf16[192,1024]{1,0:T(8,128)(2,1)S(1)}, bf16[192,1024]{1,0:T(8,128)(2,1)S(1)}, u32[]{:S(2)}, u32[]{:S(2)}) collective-permute-start(bf16[192,1024]{1,0:T(8,128)(2,1)S(1)} %collective-permute-done.8.b_ref), channel_id=1, source_target_pairs={{0,240},{16,0},{32,16},{48,32},{64,48},{80,64},{96,80},{112,96},{1... | collective-permute-start | bytes 1179656 | tf_op jit(solution)/shard_map/ppermute | solution.py:114
  59.9 1.9 %collective-permute-start.1 = (bf16[192,1024]{1,0:T(8,128)(2,1)S(1)}, bf16[192,1024]{1,0:T(8,128)(2,1)S(1)}, u32[]{:S(2)}, u32[]{:S(2)}) collective-permute-start(bf16[192,1024]{1,0:T(8,128)(2,1)S(1)} %collective-permute-done.f_ref), channel_id=1, source_target_pairs={{0,16},{16,32},{32,48},{48,64},{64,80},{80,96},{96,112},{112,128},... | collective-permute-start | bytes 1179656 | tf_op jit(solution)/shard_map/ppermute | solution.py:114
  62.6 4.1 %collective-permute-done.9.b_ref = bf16[192,1024]{1,0:T(8,128)(2,1)S(1)} collective-permute-done((bf16[192,1024]{1,0:T(8,128)(2,1)S(1)}, bf16[192,1024]{1,0:T(8,128)(2,1)S(1)}, u32[]{:S(2)}, u32[]{:S(2)}) %collective-permute-start.9) | collective-permute-done | bytes 393248 | tf_op jit(solution)/shard_map/ppermute | solution.py:114
  66.7 5.6 %collective-permute-start.10 = (bf16[192,1024]{1,0:T(8,128)(2,1)S(1)}, bf16[192,1024]{1,0:T(8,128)(2,1)S(1)}, u32[]{:S(2)}, u32[]{:S(2)}) collective-permute-start(bf16[192,1024]{1,0:T(8,128)(2,1)S(1)} %collective-permute-done.9.b_ref), channel_id=1, source_target_pairs={{0,240},{16,0},{32,16},{48,32},{64,48},{80,64},{96,80},{112,96},{1... | collective-permute-start | bytes 1179656 | tf_op jit(solution)/shard_map/ppermute | solution.py:114
  72.8 1.9 %collective-permute-start.2 = (bf16[192,1024]{1,0:T(8,128)(2,1)S(1)}, bf16[192,1024]{1,0:T(8,128)(2,1)S(1)}, u32[]{:S(2)}, u32[]{:S(2)}) collective-permute-start(bf16[192,1024]{1,0:T(8,128)(2,1)S(1)} %collective-permute-done.1.f_ref), channel_id=1, source_target_pairs={{0,16},{16,32},{32,48},{48,64},{64,80},{80,96},{96,112},{112,128},... | collective-permute-start | bytes 1179656 | tf_op jit(solution)/shard_map/ppermute | solution.py:114
  74.8 4.3 %collective-permute-done.10.b_ref = bf16[192,1024]{1,0:T(8,128)(2,1)S(1)} collective-permute-done((bf16[192,1024]{1,0:T(8,128)(2,1)S(1)}, bf16[192,1024]{1,0:T(8,128)(2,1)S(1)}, u32[]{:S(2)}, u32[]{:S(2)}) %collective-permute-start.10) | collective-permute-done | bytes 393248 | tf_op jit(solution)/shard_map/ppermute | solution.py:114
  79.0 5.6 %collective-permute-start.11 = (bf16[192,1024]{1,0:T(8,128)(2,1)S(1)}, bf16[192,1024]{1,0:T(8,128)(2,1)S(1)}, u32[]{:S(2)}, u32[]{:S(2)}) collective-permute-start(bf16[192,1024]{1,0:T(8,128)(2,1)S(1)} %collective-permute-done.10.b_ref), channel_id=1, source_target_pairs={{0,240},{16,0},{32,16},{48,32},{64,48},{80,64},{96,80},{112,96},{1... | collective-permute-start | bytes 1179656 | tf_op jit(solution)/shard_map/ppermute | solution.py:114
  84.9 1.9 %collective-permute-start.3 = (bf16[192,1024]{1,0:T(8,128)(2,1)S(1)}, bf16[192,1024]{1,0:T(8,128)(2,1)S(1)}, u32[]{:S(2)}, u32[]{:S(2)}) collective-permute-start(bf16[192,1024]{1,0:T(8,128)(2,1)S(1)} %collective-permute-done.2.f_ref), channel_id=1, source_target_pairs={{0,16},{16,32},{32,48},{48,64},{64,80},{80,96},{96,112},{112,128},... | collective-permute-start | bytes 1179656 | tf_op jit(solution)/shard_map/ppermute | solution.py:114
  86.8 3.7 %collective-permute-done.11.b_ref = bf16[192,1024]{1,0:T(8,128)(2,1)S(1)} collective-permute-done((bf16[192,1024]{1,0:T(8,128)(2,1)S(1)}, bf16[192,1024]{1,0:T(8,128)(2,1)S(1)}, u32[]{:S(2)}, u32[]{:S(2)}) %collective-permute-start.11) | collective-permute-done | bytes 393248 | tf_op jit(solution)/shard_map/ppermute | solution.py:114
  90.5 5.6 %collective-permute-start.12 = (bf16[192,1024]{1,0:T(8,128)(2,1)S(1)}, bf16[192,1024]{1,0:T(8,128)(2,1)S(1)}, u32[]{:S(2)}, u32[]{:S(2)}) collective-permute-start(bf16[192,1024]{1,0:T(8,128)(2,1)S(1)} %collective-permute-done.11.b_ref), channel_id=1, source_target_pairs={{0,240},{16,0},{32,16},{48,32},{64,48},{80,64},{96,80},{112,96},{1... | collective-permute-start | bytes 1179656 | tf_op jit(solution)/shard_map/ppermute | solution.py:114
  96.1 2.0 %collective-permute-start.4 = (bf16[192,1024]{1,0:T(8,128)(2,1)S(1)}, bf16[192,1024]{1,0:T(8,128)(2,1)}, u32[]{:S(2)}, u32[]{:S(2)}) collective-permute-start(bf16[192,1024]{1,0:T(8,128)(2,1)S(1)} %collective-permute-done.3.f_ref), channel_id=1, source_target_pairs={{0,16},{16,32},{32,48},{48,64},{64,80},{80,96},{96,112},{112,128},... | collective-permute-start | bytes 1179656 | tf_op jit(solution)/shard_map/ppermute | solution.py:114
  98.9 2.6 %collective-permute-done.12.b_ref = bf16[192,1024]{1,0:T(8,128)(2,1)S(1)} collective-permute-done((bf16[192,1024]{1,0:T(8,128)(2,1)S(1)}, bf16[192,1024]{1,0:T(8,128)(2,1)S(1)}, u32[]{:S(2)}, u32[]{:S(2)}) %collective-permute-start.12) | collective-permute-done | bytes 393248 | tf_op jit(solution)/shard_map/ppermute | solution.py:114
  101.4 5.6 %collective-permute-start.13 = (bf16[192,1024]{1,0:T(8,128)(2,1)S(1)}, bf16[192,1024]{1,0:T(8,128)(2,1)S(1)}, u32[]{:S(2)}, u32[]{:S(2)}) collective-permute-start(bf16[192,1024]{1,0:T(8,128)(2,1)S(1)} %collective-permute-done.12.b_ref), channel_id=1, source_target_pairs={{0,240},{16,0},{32,16},{48,32},{64,48},{80,64},{96,80},{112,96},{1... | collective-permute-start | bytes 1179656 | tf_op jit(solution)/shard_map/ppermute | solution.py:114
  107.2 1.9 %collective-permute-start.5 = (bf16[192,1024]{1,0:T(8,128)(2,1)}, bf16[192,1024]{1,0:T(8,128)(2,1)S(1)}, u32[]{:S(2)}, u32[]{:S(2)}) collective-permute-start(bf16[192,1024]{1,0:T(8,128)(2,1)} %collective-permute-done.4.f_ref), channel_id=1, source_target_pairs={{0,16},{16,32},{32,48},{48,64},{64,80},{80,96},{96,112},{112,128},... | collective-permute-start | bytes 1179656 | tf_op jit(solution)/shard_map/ppermute | solution.py:114
  111.2 3.8 %first.1 = (bf16[192,3584]{1,0:T(8,128)(2,1)S(1)}, f32[28,192,128]{2,1,0:T(8,128)S(1)}, f32[28,192,128]{2,1,0:T(8,128)S(1)}, f32[28,192,128]{2,1,0:T(8,128)S(1)}) custom-call(s32[1]{0:T(128)} %bitcast._place.place_ref, bf16[192,3584]{1,0:T(8,128)(2,1)S(1)} %bitcast.7, bf16[192,1024]{1,0:T(8,128)(2,1)S(1)} %pad_maximum_fusion.kv_ref), custom_call_target="tpu_custom_call" | custom-call | flops 528482304 | bytes 2752512 | tf_op jit(solution)/shard_map/first/pallas_call | solution.py:143
  117.0 11.6 %collective-permute-start.14 = (bf16[192,1024]{1,0:T(8,128)(2,1)S(1)}, bf16[192,1024]{1,0:T(8,128)(2,1)S(1)}, u32[]{:S(2)}, u32[]{:S(2)}) collective-permute-start(bf16[192,1024]{1,0:T(8,128)(2,1)S(1)} %collective-permute-done.13.b_ref), channel_id=1, source_target_pairs={{0,240},{16,0},{32,16},{48,32},{64,48},{80,64},{96,80},{112,96},{1... | collective-permute-start | bytes 1179656 | tf_op jit(solution)/shard_map/ppermute | solution.py:114
  128.6 2.0 %collective-permute-start.6 = (bf16[192,1024]{1,0:T(8,128)(2,1)S(1)}, bf16[192,1024]{1,0:T(8,128)(2,1)S(1)}, u32[]{:S(2)}, u32[]{:S(2)}) collective-permute-start(bf16[192,1024]{1,0:T(8,128)(2,1)S(1)} %collective-permute-done.5.f_ref), channel_id=1, source_target_pairs={{0,16},{16,32},{32,48},{48,64},{64,80},{80,96},{96,112},{112,128},... | collective-permute-start | bytes 1179656 | tf_op jit(solution)/shard_map/ppermute | solution.py:114
  133.9 28.6 %collective-permute-start.15 = (bf16[96,1024]{1,0:T(8,128)(2,1)S(1)}, bf16[96,1024]{1,0:T(8,128)(2,1)S(1)}, u32[]{:S(2)}, u32[]{:S(2)}) collective-permute-start(bf16[96,1024]{1,0:T(8,128)(2,1)S(1)} %slice.9), channel_id=1, source_target_pairs={{0,240},{16,0},{32,16},{48,32},{64,48},{80,64},{96,80},{112,96},{1... | collective-permute-start | bytes 589832 | tf_op jit(solution)/shard_map/ppermute | solution.py:114
  162.6 2.0 %collective-permute-start.7 = (bf16[96,1024]{1,0:T(8,128)(2,1)S(1)}, bf16[96,1024]{1,0:T(8,128)(2,1)S(1)}, u32[]{:S(2)}, u32[]{:S(2)}) collective-permute-start(bf16[96,1024]{1,0:T(8,128)(2,1)S(1)} %slice.8), channel_id=1, source_target_pairs={{0,16},{16,32},{32,48},{48,64},{64,80},{80,96},{96,112},{112,128},... | collective-permute-start | bytes 589832 | tf_op jit(solution)/shard_map/ppermute | solution.py:114
  165.7 5.7 %collective-permute-done.7.f_ref = bf16[96,1024]{1,0:T(8,128)(2,1)S(1)} collective-permute-done((bf16[96,1024]{1,0:T(8,128)(2,1)S(1)}, bf16[96,1024]{1,0:T(8,128)(2,1)S(1)}, u32[]{:S(2)}, u32[]{:S(2)}) %collective-permute-start.7) | collective-permute-done | bytes 196640 | tf_op jit(solution)/shard_map/ppermute | solution.py:114
  171.4 2.1 %last.1 = (f32[28,192,128]{2,1,0:T(8,128)S(1)}, f32[28,192,128]{2,1,0:T(8,128)S(1)}, f32[28,192,128]{2,1,0:T(8,128)S(1)}, bf16[192,3584]{1,0:T(8,128)(2,1)}) custom-call(s32[1]{0:T(128)} %bitcast._place.place_ref, bf16[192,3584]{1,0:T(8,128)(2,1)S(1)} %get-tuple-element.31.q_ref, ...), custom_call_target="tpu_custom_call", output_to_operand_aliasing={{0}: (6, {}), {1}: (7, {}), {2}: (8, {})} | custom-call | flops 528482304 | bytes 2752512 | tf_op jit(solution)/shard_map/last/pallas_call | solution.py:169
  (37 shorter events, 12.7 us)
Async XLA Ops:
  1.1 52.4 %collective-permute-start.8 = (bf16[192,1024]{1,0:T(8,128)(2,1)S(1)}, bf16[192,1024]{1,0:T(8,128)(2,1)S(1)}, u32[]{:S(2)}, u32[]{:S(2)}) collective-permute-start(bf16[192,1024]{1,0:T(8,128)(2,1)S(1)} %pad_maximum_fusion.kv_ref), channel_id=1, source_target_pairs={{0,240},{16,0},{32,16},{48,32},{64,48},{80,64},{96,80},{112,96},{1... | collective-permute-start | bytes 1179656 | tf_op jit(solution)/shard_map/ppermute | solution.py:114
  45.1 14.8 %collective-permute-start = (bf16[192,1024]{1,0:T(8,128)(2,1)S(1)}, bf16[192,1024]{1,0:T(8,128)(2,1)S(1)}, u32[]{:S(2)}, u32[]{:S(2)}) collective-permute-start(bf16[192,1024]{1,0:T(8,128)(2,1)S(1)} %pad_maximum_fusion.kv_ref), channel_id=1, source_target_pairs={{0,16},{16,32},{32,48},{48,64},{64,80},{80,96},{96,112},{112,128},... | collective-permute-start | bytes 1179656 | tf_op jit(solution)/shard_map/ppermute | solution.py:114
  53.5 13.2 %collective-permute-start.9 = (bf16[192,1024]{1,0:T(8,128)(2,1)S(1)}, bf16[192,1024]{1,0:T(8,128)(2,1)S(1)}, u32[]{:S(2)}, u32[]{:S(2)}) collective-permute-start(bf16[192,1024]{1,0:T(8,128)(2,1)S(1)} %collective-permute-done.8.b_ref), channel_id=1, source_target_pairs={{0,240},{16,0},{32,16},{48,32},{64,48},{80,64},{96,80},{112,96},{1... | collective-permute-start | bytes 1179656 | tf_op jit(solution)/shard_map/ppermute | solution.py:114
  59.1 0.8 copy-start.1
  59.9 12.9 %collective-permute-start.1 = (bf16[192,1024]{1,0:T(8,128)(2,1)S(1)}, bf16[192,1024]{1,0:T(8,128)(2,1)S(1)}, u32[]{:S(2)}, u32[]{:S(2)}) collective-permute-start(bf16[192,1024]{1,0:T(8,128)(2,1)S(1)} %collective-permute-done.f_ref), channel_id=1, source_target_pairs={{0,16},{16,32},{32,48},{48,64},{64,80},{80,96},{96,112},{112,128},... | collective-permute-start | bytes 1179656 | tf_op jit(solution)/shard_map/ppermute | solution.py:114
  61.9 0.8 copy-start.5
  66.7 12.3 %collective-permute-start.10 = (bf16[192,1024]{1,0:T(8,128)(2,1)S(1)}, bf16[192,1024]{1,0:T(8,128)(2,1)S(1)}, u32[]{:S(2)}, u32[]{:S(2)}) collective-permute-start(bf16[192,1024]{1,0:T(8,128)(2,1)S(1)} %collective-permute-done.9.b_ref), channel_id=1, source_target_pairs={{0,240},{16,0},{32,16},{48,32},{64,48},{80,64},{96,80},{112,96},{1... | collective-permute-start | bytes 1179656 | tf_op jit(solution)/shard_map/ppermute | solution.py:114
  72.8 12.1 %collective-permute-start.2 = (bf16[192,1024]{1,0:T(8,128)(2,1)S(1)}, bf16[192,1024]{1,0:T(8,128)(2,1)S(1)}, u32[]{:S(2)}, u32[]{:S(2)}) collective-permute-start(bf16[192,1024]{1,0:T(8,128)(2,1)S(1)} %collective-permute-done.1.f_ref), channel_id=1, source_target_pairs={{0,16},{16,32},{32,48},{48,64},{64,80},{80,96},{96,112},{112,128},... | collective-permute-start | bytes 1179656 | tf_op jit(solution)/shard_map/ppermute | solution.py:114
  79.0 11.5 %collective-permute-start.11 = (bf16[192,1024]{1,0:T(8,128)(2,1)S(1)}, bf16[192,1024]{1,0:T(8,128)(2,1)S(1)}, u32[]{:S(2)}, u32[]{:S(2)}) collective-permute-start(bf16[192,1024]{1,0:T(8,128)(2,1)S(1)} %collective-permute-done.10.b_ref), channel_id=1, source_target_pairs={{0,240},{16,0},{32,16},{48,32},{64,48},{80,64},{96,80},{112,96},{1... | collective-permute-start | bytes 1179656 | tf_op jit(solution)/shard_map/ppermute | solution.py:114
  84.9 11.3 %collective-permute-start.3 = (bf16[192,1024]{1,0:T(8,128)(2,1)S(1)}, bf16[192,1024]{1,0:T(8,128)(2,1)S(1)}, u32[]{:S(2)}, u32[]{:S(2)}) collective-permute-start(bf16[192,1024]{1,0:T(8,128)(2,1)S(1)} %collective-permute-done.2.f_ref), channel_id=1, source_target_pairs={{0,16},{16,32},{32,48},{48,64},{64,80},{80,96},{96,112},{112,128},... | collective-permute-start | bytes 1179656 | tf_op jit(solution)/shard_map/ppermute | solution.py:114
  90.5 10.9 %collective-permute-start.12 = (bf16[192,1024]{1,0:T(8,128)(2,1)S(1)}, bf16[192,1024]{1,0:T(8,128)(2,1)S(1)}, u32[]{:S(2)}, u32[]{:S(2)}) collective-permute-start(bf16[192,1024]{1,0:T(8,128)(2,1)S(1)} %collective-permute-done.11.b_ref), channel_id=1, source_target_pairs={{0,240},{16,0},{32,16},{48,32},{64,48},{80,64},{96,80},{112,96},{1... | collective-permute-start | bytes 1179656 | tf_op jit(solution)/shard_map/ppermute | solution.py:114
  96.1 11.0 %collective-permute-start.4 = (bf16[192,1024]{1,0:T(8,128)(2,1)S(1)}, bf16[192,1024]{1,0:T(8,128)(2,1)}, u32[]{:S(2)}, u32[]{:S(2)}) collective-permute-start(bf16[192,1024]{1,0:T(8,128)(2,1)S(1)} %collective-permute-done.3.f_ref), channel_id=1, source_target_pairs={{0,16},{16,32},{32,48},{48,64},{64,80},{80,96},{96,112},{112,128},... | collective-permute-start | bytes 1179656 | tf_op jit(solution)/shard_map/ppermute | solution.py:114
  98.1 0.7 copy-start.3
  101.4 15.6 %collective-permute-start.13 = (bf16[192,1024]{1,0:T(8,128)(2,1)S(1)}, bf16[192,1024]{1,0:T(8,128)(2,1)S(1)}, u32[]{:S(2)}, u32[]{:S(2)}) collective-permute-start(bf16[192,1024]{1,0:T(8,128)(2,1)S(1)} %collective-permute-done.12.b_ref), channel_id=1, source_target_pairs={{0,240},{16,0},{32,16},{48,32},{64,48},{80,64},{96,80},{112,96},{1... | collective-permute-start | bytes 1179656 | tf_op jit(solution)/shard_map/ppermute | solution.py:114
  107.2 21.5 %collective-permute-start.5 = (bf16[192,1024]{1,0:T(8,128)(2,1)}, bf16[192,1024]{1,0:T(8,128)(2,1)S(1)}, u32[]{:S(2)}, u32[]{:S(2)}) collective-permute-start(bf16[192,1024]{1,0:T(8,128)(2,1)} %collective-permute-done.4.f_ref), channel_id=1, source_target_pairs={{0,16},{16,32},{32,48},{48,64},{64,80},{80,96},{96,112},{112,128},... | collective-permute-start | bytes 1179656 | tf_op jit(solution)/shard_map/ppermute | solution.py:114
  109.9 1.3 copy-start.7
  115.0 1.0 copy-start.2
  116.0 1.0 copy-start.6
  117.0 16.9 %collective-permute-start.14 = (bf16[192,1024]{1,0:T(8,128)(2,1)S(1)}, bf16[192,1024]{1,0:T(8,128)(2,1)S(1)}, u32[]{:S(2)}, u32[]{:S(2)}) collective-permute-start(bf16[192,1024]{1,0:T(8,128)(2,1)S(1)} %collective-permute-done.13.b_ref), channel_id=1, source_target_pairs={{0,240},{16,0},{32,16},{48,32},{64,48},{80,64},{96,80},{112,96},{1... | collective-permute-start | bytes 1179656 | tf_op jit(solution)/shard_map/ppermute | solution.py:114
  128.6 33.9 %collective-permute-start.6 = (bf16[192,1024]{1,0:T(8,128)(2,1)S(1)}, bf16[192,1024]{1,0:T(8,128)(2,1)S(1)}, u32[]{:S(2)}, u32[]{:S(2)}) collective-permute-start(bf16[192,1024]{1,0:T(8,128)(2,1)S(1)} %collective-permute-done.5.f_ref), channel_id=1, source_target_pairs={{0,16},{16,32},{32,48},{48,64},{64,80},{80,96},{96,112},{112,128},... | collective-permute-start | bytes 1179656 | tf_op jit(solution)/shard_map/ppermute | solution.py:114
  130.6 1.0 copy-start.4
  133.9 31.8 %collective-permute-start.15 = (bf16[96,1024]{1,0:T(8,128)(2,1)S(1)}, bf16[96,1024]{1,0:T(8,128)(2,1)S(1)}, u32[]{:S(2)}, u32[]{:S(2)}) collective-permute-start(bf16[96,1024]{1,0:T(8,128)(2,1)S(1)} %slice.9), channel_id=1, source_target_pairs={{0,240},{16,0},{32,16},{48,32},{64,48},{80,64},{96,80},{112,96},{1... | collective-permute-start | bytes 589832 | tf_op jit(solution)/shard_map/ppermute | solution.py:114
  162.6 8.8 %collective-permute-start.7 = (bf16[96,1024]{1,0:T(8,128)(2,1)S(1)}, bf16[96,1024]{1,0:T(8,128)(2,1)S(1)}, u32[]{:S(2)}, u32[]{:S(2)}) collective-permute-start(bf16[96,1024]{1,0:T(8,128)(2,1)S(1)} %slice.8), channel_id=1, source_target_pairs={{0,16},{16,32},{32,48},{48,64},{64,80},{80,96},{96,112},{112,128},... | collective-permute-start | bytes 589832 | tf_op jit(solution)/shard_map/ppermute | solution.py:114
  164.6 6.8 %copy-start = (bf16[1,192,3584]{2,1,0:T(8,128)(2,1)S(1)}, bf16[1,192,3584]{2,1,0:T(8,128)(2,1)}, u32[]{:S(2)}) copy-start(bf16[1,192,3584]{2,1,0:T(8,128)(2,1)} %param.8) | copy-start | bytes 4128772

commit v2 on v1

--- a/solution.py
+++ b/solution.py
@@ -74,27 +74,31 @@
     each_head(q_ref, (kv_ref,), acc_ref, total_ref, top_ref, q_heads, kv_heads, True)
 
 
-def step_kernel(place_ref, q_ref, f_ref, b_ref, _a, _t, _m, acc_ref, total_ref, top_ref, *, step, count, q_heads, kv_heads):
-    place = place_ref[0]
-    wrapped = place + step >= count
-
-    @pl.when(wrapped)
-    def _():
-        each_head(q_ref, (f_ref, b_ref), acc_ref, total_ref, top_ref, q_heads, kv_heads, False)
-
-    @pl.when(jnp.logical_and(place >= step, jnp.logical_not(wrapped)))
-    def _():
-        each_head(q_ref, (f_ref,), acc_ref, total_ref, top_ref, q_heads, kv_heads, False)
-
-
-def last_kernel(
-    place_ref, q_ref, f_ref, b_ref, residual_ref, gain_ref, _a, _t, _m, acc_ref, total_ref, top_ref, out_ref,
-    *, step, q_heads, kv_heads,
-):
-    @pl.when(place_ref[0] >= step)
-    def _():
-        each_head(q_ref, (f_ref, b_ref), acc_ref, total_ref, top_ref, q_heads, kv_heads, False)
-
+def fold(place, step, count, f_ref, b_ref, update):
+    behind = place >= step
+    if b_ref is None:
+        pl.when(behind)(lambda: update((f_ref,)))
+    else:
+        wrapped = place + step >= count
+        pl.when(wrapped)(lambda: update((f_ref, b_ref)))
+        pl.when(jnp.logical_and(behind, jnp.logical_not(wrapped)))(lambda: update((f_ref,)))
+
+
+def step_kernel(place_ref, q_ref, f_ref, *refs, step, count, both, q_heads, kv_heads):
+    b_ref = refs[0] if both else None
+    state = refs[-3:]
+    fold(
+        place_ref[0], step, count, f_ref, b_ref,
+        lambda blocks: each_head(q_ref, blocks, *state, q_heads, kv_heads, False),
+    )
+
+
+def last_kernel(place_ref, q_ref, f_ref, residual_ref, gain_ref, *refs, step, count, q_heads, kv_heads):
+    acc_ref, total_ref, top_ref, out_ref = refs[-4:]
+    fold(
+        place_ref[0], step, count, f_ref, None,
+        lambda blocks: each_head(q_ref, blocks, acc_ref, total_ref, top_ref, q_heads, kv_heads, False),
+    )
     rows, width = out_ref.shape
     square = jnp.zeros((rows, HEAD_WIDTH), jnp.float32)
     for head in range(q_heads):
@@ -110,21 +114,32 @@
         out_ref[:, at] = (acc_ref[head] * inv_rms * gain_ref[:, at]).astype(jnp.bfloat16)
 
 
+def hops(count):
+    backward = count * 3 // 8
+    return count - 1 - backward, backward
+
+
+def forward_pairs(count, step):
+    return [(i, i + 1) for i in range(step - 1, count - 1)]
+
+
+def backward_pairs(count, step, backward):
+    return [(i, (i - 1) % count) for i in range(count) if (i + step - 1) % count < backward]
+
+
 def shift(array, pairs):
     return lax.ppermute(array, "seq", pairs)
 
 
 def layer(queries, keys, values, residual, norm_gain):
     count = lax.axis_size("seq")
-    half = count // 2
+    forward_steps, backward_steps = hops(count)
     query = queries[0]
     rows, width = query.shape
     q_heads = width // HEAD_WIDTH
     kv_heads = keys.shape[2] // HEAD_WIDTH
     place = lax.axis_index("seq").astype(jnp.int32).reshape(1)
     own = jnp.concatenate([keys[0], values[0]], axis=1)
-    right = [(i, (i + 1) % count) for i in range(count)]
-    left = [(i, (i - 1) % count) for i in range(count)]
     state_shape = (q_heads, rows, HEAD_WIDTH)
     state = pltpu.VMEM(state_shape, jnp.float32)
     vmem = pl.BlockSpec(memory_space=pltpu.VMEM)
@@ -138,8 +153,8 @@
             bytes_accessed=4 * rows * width,
         )
 
-    forward = shift(own, right)
-    backward = shift(own, left)
+    forward = shift(own, forward_pairs(count, 1))
+    backward = shift(own, backward_pairs(count, 1, backward_steps))
     query, acc, total, top = pl.pallas_call(
         functools.partial(first_kernel, q_heads=q_heads, kv_heads=kv_heads),
         out_shape=(pltpu.VMEM(query.shape, query.dtype), state, state, state),
@@ -149,33 +164,33 @@
         cost_estimate=cost(rows),
         name="first",
     )(place, query, own)
-    for step in range(1, half):
-        if step + 1 < half:
-            forward_next = shift(forward, right)
-            backward_next = shift(backward, left)
-        else:
-            forward_next = shift(forward[: rows // 2], right)
-            backward_next = shift(backward[rows // 2 :], left)
+    for step in range(1, forward_steps):
+        blocks = (forward, backward) if step <= backward_steps else (forward,)
+        forward = shift(forward, forward_pairs(count, step + 1))
+        if step < backward_steps:
+            backward = shift(backward, backward_pairs(count, step + 1, backward_steps))
+        at = 2 + len(blocks)
         acc, total, top = pl.pallas_call(
-            functools.partial(step_kernel, step=step, count=count, q_heads=q_heads, kv_heads=kv_heads),
+            functools.partial(
+                step_kernel, step=step, count=count, both=len(blocks) == 2, q_heads=q_heads, kv_heads=kv_heads
+            ),
             out_shape=(state, state, state),
-            in_specs=[smem] + [vmem] * 6,
+            in_specs=[smem] + [vmem] * (at + 2),
             out_specs=(vmem, vmem, vmem),
-            input_output_aliases={4: 0, 5: 1, 6: 2},
+            input_output_aliases={at: 0, at + 1: 1, at + 2: 2},
             compiler_params=params,
-            cost_estimate=cost(2 * rows),
-        )(place, query, forward, backward, acc, total, top)
-        forward, backward = forward_next, backward_next
+            cost_estimate=cost(len(blocks) * rows),
+        )(place, query, *blocks, acc, total, top)
     _, _, _, normed = pl.pallas_call(
-        functools.partial(last_kernel, step=half, q_heads=q_heads, kv_heads=kv_heads),
+        functools.partial(last_kernel, step=forward_steps, count=count, q_heads=q_heads, kv_heads=kv_heads),
         out_shape=(state, state, state, jax.ShapeDtypeStruct((rows, width), jnp.bfloat16)),
-        in_specs=[smem] + [vmem] * 8,
+        in_specs=[smem] + [vmem] * 7,
         out_specs=(vmem, vmem, vmem, vmem),
-        input_output_aliases={6: 0, 7: 1, 8: 2},
+        input_output_aliases={5: 0, 6: 1, 7: 2},
         compiler_params=params,
         cost_estimate=cost(rows),
         name="last",
-    )(place, query, forward, backward, residual[0], norm_gain.reshape(1, width), acc, total, top)
+    )(place, query, forward, residual[0], norm_gain.reshape(1, width), acc, total, top)
     return normed[None]
 
 

time: 174 us -> 151 us (0.87)
  the two profiles are of different devices: /device:TPU:94 before, /device:TPU:1622 now
where the time goes in v2:
time: 151 us
  waiting for transfers between devices  51.6 us (34%)
  Pallas kernels  50.9 us (34%)
  starting transfers between devices  41.4 us (27%)
  local copies, waits for them, and re-layouts  5.31 us (4%)
    ppermute x15, waiting for transfers between devices, shift(): return lax.ppermute(array, 'seq', pairs)  51.6 us
    ppermute x15, starting transfers between devices, shift(): return lax.ppermute(array, 'seq', pairs)  41.4 us
    pallas_call x8, Pallas kernels, layer(): pl.pallas_call(functools.partial(step_kernel, step=step, count=count, bot...  41 us
    pallas_call x1, Pallas kernels, layer(): pl.pallas_call(functools.partial(last_kernel, step=forward_steps, count=c...  6.04 us
    unnamed x16, local copies, waits for them, and re-layouts  4.58 us
    pallas_call x1, Pallas kernels, layer(): pl.pallas_call(functools.partial(first_kernel, q_heads=q_heads, kv_heads=...  3.82 us
  transfers between devices with their start and end apart: 15, of which 7 were waited for; matrix products, arithmetic and copies ran while one was open for 0% of the time, Pallas kernels for 30%

profile of v2, /device:TPU:1622, one launch (start us, length us, event | category | flops | bytes accessed | tf_op | source)
XLA Modules:
  0.0 150.6 jit_solution(4433546904858522744)
XLA Ops:
  1.1 5.1 %collective-permute-start = (bf16[192,1024]{1,0:T(8,128)(2,1)S(1)}, bf16[192,1024]{1,0:T(8,128)(2,1)S(1)}, u32[]{:S(2)}, u32[]{:S(2)}) collective-permute-start(bf16[192,1024]{1,0:T(8,128)(2,1)S(1)} %pad_maximum_fusion.kv_ref), channel_id=1, source_target_pairs={{0,16},{16,32},{32,48},{48,64},{64,80},{80,96},{96,112},{112,128},... | collective-permute-start | bytes 1179656 | tf_op jit(solution)/shard_map/ppermute | solution.py:131
  6.2 8.9 %collective-permute-done.f_ref = bf16[192,1024]{1,0:T(8,128)(2,1)S(1)} collective-permute-done((bf16[192,1024]{1,0:T(8,128)(2,1)S(1)}, bf16[192,1024]{1,0:T(8,128)(2,1)S(1)}, u32[]{:S(2)}, u32[]{:S(2)}) %collective-permute-start) | collective-permute-done | bytes 393248 | tf_op jit(solution)/shard_map/ppermute | solution.py:131
  15.1 4.6 %collective-permute-start.1 = (bf16[192,1024]{1,0:T(8,128)(2,1)S(1)}, bf16[192,1024]{1,0:T(8,128)(2,1)S(1)}, u32[]{:S(2)}, u32[]{:S(2)}) collective-permute-start(bf16[192,1024]{1,0:T(8,128)(2,1)S(1)} %collective-permute-done.f_ref), channel_id=1, source_target_pairs={{16,32},{32,48},{48,64},{64,80},{80,96},{96,112},{112,128},{128,14... | collective-permute-start | bytes 1179656 | tf_op jit(solution)/shard_map/ppermute | solution.py:131
  19.7 8.6 %collective-permute-done.1.f_ref = bf16[192,1024]{1,0:T(8,128)(2,1)S(1)} collective-permute-done((bf16[192,1024]{1,0:T(8,128)(2,1)S(1)}, bf16[192,1024]{1,0:T(8,128)(2,1)S(1)}, u32[]{:S(2)}, u32[]{:S(2)}) %collective-permute-start.1) | collective-permute-done | bytes 393248 | tf_op jit(solution)/shard_map/ppermute | solution.py:131
  28.3 4.1 %collective-permute-start.2 = (bf16[192,1024]{1,0:T(8,128)(2,1)S(1)}, bf16[192,1024]{1,0:T(8,128)(2,1)S(1)}, u32[]{:S(2)}, u32[]{:S(2)}) collective-permute-start(bf16[192,1024]{1,0:T(8,128)(2,1)S(1)} %collective-permute-done.1.f_ref), channel_id=1, source_target_pairs={{32,48},{48,64},{64,80},{80,96},{96,112},{112,128},{128,144},{144,... | collective-permute-start | bytes 1179656 | tf_op jit(solution)/shard_map/ppermute | solution.py:131
  33.1 7.5 %collective-permute-done.2.f_ref = bf16[192,1024]{1,0:T(8,128)(2,1)S(1)} collective-permute-done((bf16[192,1024]{1,0:T(8,128)(2,1)S(1)}, bf16[192,1024]{1,0:T(8,128)(2,1)S(1)}, u32[]{:S(2)}, u32[]{:S(2)}) %collective-permute-start.2) | collective-permute-done | bytes 393248 | tf_op jit(solution)/shard_map/ppermute | solution.py:131
  40.6 2.9 %collective-permute-start.3 = (bf16[192,1024]{1,0:T(8,128)(2,1)S(1)}, bf16[192,1024]{1,0:T(8,128)(2,1)S(1)}, u32[]{:S(2)}, u32[]{:S(2)}) collective-permute-start(bf16[192,1024]{1,0:T(8,128)(2,1)S(1)} %collective-permute-done.2.f_ref), channel_id=1, source_target_pairs={{48,64},{64,80},{80,96},{96,112},{112,128},{128,144},{144,160},{16... | collective-permute-start | bytes 1179656 | tf_op jit(solution)/shard_map/ppermute | solution.py:131
  45.0 7.1 %collective-permute-done.3.f_ref = bf16[192,1024]{1,0:T(8,128)(2,1)S(1)} collective-permute-done((bf16[192,1024]{1,0:T(8,128)(2,1)S(1)}, bf16[192,1024]{1,0:T(8,128)(2,1)S(1)}, u32[]{:S(2)}, u32[]{:S(2)}) %collective-permute-start.3) | collective-permute-done | bytes 393248 | tf_op jit(solution)/shard_map/ppermute | solution.py:131
  55.5 7.5 %collective-permute-done.4.f_ref = bf16[192,1024]{1,0:T(8,128)(2,1)S(1)} collective-permute-done((bf16[192,1024]{1,0:T(8,128)(2,1)S(1)}, bf16[192,1024]{1,0:T(8,128)(2,1)S(1)}, u32[]{:S(2)}, u32[]{:S(2)}) %collective-permute-start.4) | collective-permute-done | bytes 393248 | tf_op jit(solution)/shard_map/ppermute | solution.py:131
  67.0 7.0 %collective-permute-done.5.f_ref = bf16[192,1024]{1,0:T(8,128)(2,1)S(1)} collective-permute-done((bf16[192,1024]{1,0:T(8,128)(2,1)S(1)}, bf16[192,1024]{1,0:T(8,128)(2,1)S(1)}, u32[]{:S(2)}, u32[]{:S(2)}) %collective-permute-start.5) | collective-permute-done | bytes 393248 | tf_op jit(solution)/shard_map/ppermute | solution.py:131
  76.0 5.2 %collective-permute-start.13 = (bf16[192,1024]{1,0:T(8,128)(2,1)}, bf16[192,1024]{1,0:T(8,128)(2,1)}, u32[]{:S(2)}, u32[]{:S(2)}) collective-permute-start(bf16[192,1024]{1,0:T(8,128)(2,1)} %collective-permute-done.12.refs_0_), channel_id=1, source_target_pairs={{0,240},{16,0},{192,176},{208,192},{224,208},{240,224},{1,241},{17... | collective-permute-start | bytes 1179656 | tf_op jit(solution)/shard_map/ppermute | solution.py:131
  81.1 5.0 %collective-permute-done.6.f_ref = bf16[192,1024]{1,0:T(8,128)(2,1)S(1)} collective-permute-done((bf16[192,1024]{1,0:T(8,128)(2,1)S(1)}, bf16[192,1024]{1,0:T(8,128)(2,1)S(1)}, u32[]{:S(2)}, u32[]{:S(2)}) %collective-permute-start.6) | collective-permute-done | bytes 393248 | tf_op jit(solution)/shard_map/ppermute | solution.py:131
  90.2 3.8 %first.1 = (bf16[192,3584]{1,0:T(8,128)(2,1)S(1)}, f32[28,192,128]{2,1,0:T(8,128)S(1)}, f32[28,192,128]{2,1,0:T(8,128)S(1)}, f32[28,192,128]{2,1,0:T(8,128)S(1)}) custom-call(s32[1]{0:T(128)} %bitcast._place.place_ref, bf16[192,3584]{1,0:T(8,128)(2,1)S(1)} %bitcast.7, bf16[192,1024]{1,0:T(8,128)(2,1)S(1)} %pad_maximum_fusion.kv_ref), custom_call_target="tpu_custom_call" | custom-call | flops 528482304 | bytes 2752512 | tf_op jit(solution)/shard_map/first/pallas_call | solution.py:158
  95.0 4.0 %shard_map.55 = (f32[28,192,128]{2,1,0:T(8,128)S(1)}, f32[28,192,128]{2,1,0:T(8,128)S(1)}, f32[28,192,128]{2,1,0:T(8,128)S(1)}) custom-call(s32[1]{0:T(128)} %bitcast._place.place_ref, bf16[192,3584]{1,0:T(8,128)(2,1)S(1)} %get-tuple-element.34.q_ref, ...), custom_call_target="tpu_custom_call", output_to_operand_aliasing={{0}: (4, {}), {1}: (5, {}), {2}: (6, {})} | custom-call | flops 1056964608 | bytes 2752512 | tf_op jit(solution)/shard_map/pallas_call | solution.py:173
  99.0 5.2 %collective-permute-start.14 = (bf16[192,1024]{1,0:T(8,128)(2,1)}, bf16[192,1024]{1,0:T(8,128)(2,1)S(1)}, u32[]{:S(2)}, u32[]{:S(2)}) collective-permute-start(bf16[192,1024]{1,0:T(8,128)(2,1)} %collective-permute-done.13.refs_0_), channel_id=1, source_target_pairs={{0,240},{176,160},{192,176},{208,192},{224,208},{240,224},{1,241},... | collective-permute-start | bytes 1179656 | tf_op jit(solution)/shard_map/ppermute | solution.py:131
  104.2 4.0 %shard_map.56 = (f32[28,192,128]{2,1,0:T(8,128)S(1)}, f32[28,192,128]{2,1,0:T(8,128)S(1)}, f32[28,192,128]{2,1,0:T(8,128)S(1)}) custom-call(s32[1]{0:T(128)} %bitcast._place.place_ref, bf16[192,3584]{1,0:T(8,128)(2,1)S(1)} %get-tuple-element.34.q_ref, ...), custom_call_target="tpu_custom_call", output_to_operand_aliasing={{0}: (4, {}), {1}: (5, {}), {2}: (6, {})} | custom-call | flops 1056964608 | bytes 2752512 | tf_op jit(solution)/shard_map/pallas_call | solution.py:173
  108.2 4.0 %shard_map.57 = (f32[28,192,128]{2,1,0:T(8,128)S(1)}, f32[28,192,128]{2,1,0:T(8,128)S(1)}, f32[28,192,128]{2,1,0:T(8,128)S(1)}) custom-call(s32[1]{0:T(128)} %bitcast._place.place_ref, bf16[192,3584]{1,0:T(8,128)(2,1)S(1)} %get-tuple-element.34.q_ref, ...), custom_call_target="tpu_custom_call", output_to_operand_aliasing={{0}: (4, {}), {1}: (5, {}), {2}: (6, {})} | custom-call | flops 1056964608 | bytes 2752512 | tf_op jit(solution)/shard_map/pallas_call | solution.py:173
  112.1 3.2 %collective-permute-start.8 = (bf16[192,1024]{1,0:T(8,128)(2,1)S(1)}, bf16[192,1024]{1,0:T(8,128)(2,1)S(1)}, u32[]{:S(2)}, u32[]{:S(2)}) collective-permute-start(bf16[192,1024]{1,0:T(8,128)(2,1)S(1)} %collective-permute-done.7.f_ref), channel_id=1, source_target_pairs={{128,144},{144,160},{160,176},{176,192},{192,208},{208,224},{224,2... | collective-permute-start | bytes 1179656 | tf_op jit(solution)/shard_map/ppermute | solution.py:131
  115.4 7.4 %shard_map.58 = (f32[28,192,128]{2,1,0:T(8,128)S(1)}, f32[28,192,128]{2,1,0:T(8,128)S(1)}, f32[28,192,128]{2,1,0:T(8,128)S(1)}) custom-call(s32[1]{0:T(128)} %bitcast._place.place_ref, bf16[192,3584]{1,0:T(8,128)(2,1)S(1)} %get-tuple-element.34.q_ref, ...), custom_call_target="tpu_custom_call", output_to_operand_aliasing={{0}: (4, {}), {1}: (5, {}), {2}: (6, {})} | custom-call | flops 1056964608 | bytes 2752512 | tf_op jit(solution)/shard_map/pallas_call | solution.py:173
  122.8 7.4 %shard_map.59 = (f32[28,192,128]{2,1,0:T(8,128)S(1)}, f32[28,192,128]{2,1,0:T(8,128)S(1)}, f32[28,192,128]{2,1,0:T(8,128)S(1)}) custom-call(s32[1]{0:T(128)} %bitcast._place.place_ref, bf16[192,3584]{1,0:T(8,128)(2,1)S(1)} %get-tuple-element.34.q_ref, ...), custom_call_target="tpu_custom_call", output_to_operand_aliasing={{0}: (4, {}), {1}: (5, {}), {2}: (6, {})} | custom-call | flops 1056964608 | bytes 2752512 | tf_op jit(solution)/shard_map/pallas_call | solution.py:173
  130.2 6.4 %shard_map.60 = (f32[28,192,128]{2,1,0:T(8,128)S(1)}, f32[28,192,128]{2,1,0:T(8,128)S(1)}, f32[28,192,128]{2,1,0:T(8,128)S(1)}) custom-call(s32[1]{0:T(128)} %bitcast._place.place_ref, bf16[192,3584]{1,0:T(8,128)(2,1)S(1)} %get-tuple-element.34.q_ref, ...), custom_call_target="tpu_custom_call", output_to_operand_aliasing={{0}: (4, {}), {1}: (5, {}), {2}: (6, {})} | custom-call | flops 1056964608 | bytes 2752512 | tf_op jit(solution)/shard_map/pallas_call | solution.py:173
  136.6 4.0 %shard_map.61 = (f32[28,192,128]{2,1,0:T(8,128)S(1)}, f32[28,192,128]{2,1,0:T(8,128)S(1)}, f32[28,192,128]{2,1,0:T(8,128)S(1)}) custom-call(s32[1]{0:T(128)} %bitcast._place.place_ref, bf16[192,3584]{1,0:T(8,128)(2,1)S(1)} %get-tuple-element.34.q_ref, ...), custom_call_target="tpu_custom_call", output_to_operand_aliasing={{0}: (3, {}), {1}: (4, {}), {2}: (5, {})} | custom-call | flops 528482304 | bytes 2752512 | tf_op jit(solution)/shard_map/pallas_call | solution.py:173
  140.6 4.0 %shard_map.62 = (f32[28,192,128]{2,1,0:T(8,128)S(1)}, f32[28,192,128]{2,1,0:T(8,128)S(1)}, f32[28,192,128]{2,1,0:T(8,128)S(1)}) custom-call(s32[1]{0:T(128)} %bitcast._place.place_ref, bf16[192,3584]{1,0:T(8,128)(2,1)S(1)} %get-tuple-element.34.q_ref, ...), custom_call_target="tpu_custom_call", output_to_operand_aliasing={{0}: (3, {}), {1}: (4, {}), {2}: (5, {})} | custom-call | flops 528482304 | bytes 2752512 | tf_op jit(solution)/shard_map/pallas_call | solution.py:173
  144.6 6.0 %last.1 = (f32[28,192,128]{2,1,0:T(8,128)S(1)}, f32[28,192,128]{2,1,0:T(8,128)S(1)}, f32[28,192,128]{2,1,0:T(8,128)S(1)}, bf16[192,3584]{1,0:T(8,128)(2,1)}) custom-call(s32[1]{0:T(128)} %bitcast._place.place_ref, bf16[192,3584]{1,0:T(8,128)(2,1)S(1)} %get-tuple-element.34.q_ref, ...), custom_call_target="tpu_custom_call", output_to_operand_aliasing={{0}: (5, {}), {1}: (6, {}), {2}: (7, {})} | custom-call | flops 528482304 | bytes 2752512 | tf_op jit(solution)/shard_map/last/pallas_call | solution.py:184
  (34 shorter events, 17.5 us)
Async XLA Ops:
  1.1 14.1 %collective-permute-start = (bf16[192,1024]{1,0:T(8,128)(2,1)S(1)}, bf16[192,1024]{1,0:T(8,128)(2,1)S(1)}, u32[]{:S(2)}, u32[]{:S(2)}) collective-permute-start(bf16[192,1024]{1,0:T(8,128)(2,1)S(1)} %pad_maximum_fusion.kv_ref), channel_id=1, source_target_pairs={{0,16},{16,32},{32,48},{48,64},{64,80},{80,96},{96,112},{112,128},... | collective-permute-start | bytes 1179656 | tf_op jit(solution)/shard_map/ppermute | solution.py:131
  15.1 13.2 %collective-permute-start.1 = (bf16[192,1024]{1,0:T(8,128)(2,1)S(1)}, bf16[192,1024]{1,0:T(8,128)(2,1)S(1)}, u32[]{:S(2)}, u32[]{:S(2)}) collective-permute-start(bf16[192,1024]{1,0:T(8,128)(2,1)S(1)} %collective-permute-done.f_ref), channel_id=1, source_target_pairs={{16,32},{32,48},{48,64},{64,80},{80,96},{96,112},{112,128},{128,14... | collective-permute-start | bytes 1179656 | tf_op jit(solution)/shard_map/ppermute | solution.py:131
  28.3 12.3 %collective-permute-start.2 = (bf16[192,1024]{1,0:T(8,128)(2,1)S(1)}, bf16[192,1024]{1,0:T(8,128)(2,1)S(1)}, u32[]{:S(2)}, u32[]{:S(2)}) collective-permute-start(bf16[192,1024]{1,0:T(8,128)(2,1)S(1)} %collective-permute-done.1.f_ref), channel_id=1, source_target_pairs={{32,48},{48,64},{64,80},{80,96},{96,112},{112,128},{128,144},{144,... | collective-permute-start | bytes 1179656 | tf_op jit(solution)/shard_map/ppermute | solution.py:131
  32.4 11.1 %collective-permute-start.9 = (bf16[192,1024]{1,0:T(8,128)(2,1)S(1)}, bf16[192,1024]{1,0:T(8,128)(2,1)S(1)}, u32[]{:S(2)}, u32[]{:S(2)}) collective-permute-start(bf16[192,1024]{1,0:T(8,128)(2,1)S(1)} %pad_maximum_fusion.kv_ref), channel_id=1, source_target_pairs={{0,240},{16,0},{32,16},{48,32},{64,48},{80,64},{1,241},{17,1},{33,... | collective-permute-start | bytes 1179656 | tf_op jit(solution)/shard_map/ppermute | solution.py:131
  40.6 11.5 %collective-permute-start.3 = (bf16[192,1024]{1,0:T(8,128)(2,1)S(1)}, bf16[192,1024]{1,0:T(8,128)(2,1)S(1)}, u32[]{:S(2)}, u32[]{:S(2)}) collective-permute-start(bf16[192,1024]{1,0:T(8,128)(2,1)S(1)} %collective-permute-done.2.f_ref), channel_id=1, source_target_pairs={{48,64},{64,80},{80,96},{96,112},{112,128},{128,144},{144,160},{16... | collective-permute-start | bytes 1179656 | tf_op jit(solution)/shard_map/ppermute | solution.py:131
  43.6 10.5 %collective-permute-start.10 = (bf16[192,1024]{1,0:T(8,128)(2,1)S(1)}, bf16[192,1024]{1,0:T(8,128)(2,1)S(1)}, u32[]{:S(2)}, u32[]{:S(2)}) collective-permute-start(bf16[192,1024]{1,0:T(8,128)(2,1)S(1)} %collective-permute-done.9.refs_0_), channel_id=1, source_target_pairs={{0,240},{16,0},{32,16},{48,32},{64,48},{240,224},{1,241},{17,1},{3... | collective-permute-start | bytes 1179656 | tf_op jit(solution)/shard_map/ppermute | solution.py:131
  44.3 0.8 copy-start.3
  52.1 10.9 %collective-permute-start.4 = (bf16[192,1024]{1,0:T(8,128)(2,1)S(1)}, bf16[192,1024]{1,0:T(8,128)(2,1)S(1)}, u32[]{:S(2)}, u32[]{:S(2)}) collective-permute-start(bf16[192,1024]{1,0:T(8,128)(2,1)S(1)} %collective-permute-done.3.f_ref), channel_id=1, source_target_pairs={{64,80},{80,96},{96,112},{112,128},{128,144},{144,160},{160,176},{... | collective-permute-start | bytes 1179656 | tf_op jit(solution)/shard_map/ppermute | solution.py:131
  54.1 10.9 %collective-permute-start.11 = (bf16[192,1024]{1,0:T(8,128)(2,1)S(1)}, bf16[192,1024]{1,0:T(8,128)(2,1)S(1)}, u32[]{:S(2)}, u32[]{:S(2)}) collective-permute-start(bf16[192,1024]{1,0:T(8,128)(2,1)S(1)} %collective-permute-done.10.refs_0_), channel_id=1, source_target_pairs={{0,240},{16,0},{32,16},{48,32},{224,208},{240,224},{1,241},{17,1},... | collective-permute-start | bytes 1179656 | tf_op jit(solution)/shard_map/ppermute | solution.py:131
  54.8 0.8 copy-start.1
  63.0 11.0 %collective-permute-start.5 = (bf16[192,1024]{1,0:T(8,128)(2,1)S(1)}, bf16[192,1024]{1,0:T(8,128)(2,1)S(1)}, u32[]{:S(2)}, u32[]{:S(2)}) collective-permute-start(bf16[192,1024]{1,0:T(8,128)(2,1)S(1)} %collective-permute-done.4.f_ref), channel_id=1, source_target_pairs={{80,96},{96,112},{112,128},{128,144},{144,160},{160,176},{176,192}... | collective-permute-start | bytes 1179656 | tf_op jit(solution)/shard_map/ppermute | solution.py:131
  65.0 11.0 %collective-permute-start.12 = (bf16[192,1024]{1,0:T(8,128)(2,1)S(1)}, bf16[192,1024]{1,0:T(8,128)(2,1)}, u32[]{:S(2)}, u32[]{:S(2)}) collective-permute-start(bf16[192,1024]{1,0:T(8,128)(2,1)S(1)} %collective-permute-done.11.refs_0_), channel_id=1, source_target_pairs={{0,240},{16,0},{32,16},{208,192},{224,208},{240,224},{1,241},{17,1... | collective-permute-start | bytes 1179656 | tf_op jit(solution)/shard_map/ppermute | solution.py:131
  66.3 0.7 copy-start.5
  74.0 12.1 %collective-permute-start.6 = (bf16[192,1024]{1,0:T(8,128)(2,1)S(1)}, bf16[192,1024]{1,0:T(8,128)(2,1)S(1)}, u32[]{:S(2)}, u32[]{:S(2)}) collective-permute-start(bf16[192,1024]{1,0:T(8,128)(2,1)S(1)} %collective-permute-done.5.f_ref), channel_id=1, source_target_pairs={{96,112},{112,128},{128,144},{144,160},{160,176},{176,192},{192,20... | collective-permute-start | bytes 1179656 | tf_op jit(solution)/shard_map/ppermute | solution.py:131
  76.0 23.0 %collective-permute-start.13 = (bf16[192,1024]{1,0:T(8,128)(2,1)}, bf16[192,1024]{1,0:T(8,128)(2,1)}, u32[]{:S(2)}, u32[]{:S(2)}) collective-permute-start(bf16[192,1024]{1,0:T(8,128)(2,1)} %collective-permute-done.12.refs_0_), channel_id=1, source_target_pairs={{0,240},{16,0},{192,176},{208,192},{224,208},{240,224},{1,241},{17... | collective-permute-start | bytes 1179656 | tf_op jit(solution)/shard_map/ppermute | solution.py:131
  86.2 26.0 %collective-permute-start.7 = (bf16[192,1024]{1,0:T(8,128)(2,1)S(1)}, bf16[192,1024]{1,0:T(8,128)(2,1)S(1)}, u32[]{:S(2)}, u32[]{:S(2)}) collective-permute-start(bf16[192,1024]{1,0:T(8,128)(2,1)S(1)} %collective-permute-done.6.f_ref), channel_id=1, source_target_pairs={{112,128},{128,144},{144,160},{160,176},{176,192},{192,208},{208,2... | collective-permute-start | bytes 1179656 | tf_op jit(solution)/shard_map/ppermute | solution.py:131
  88.9 1.3 copy-start.7
  94.0 1.0 copy-start.4
  95.0 9.1 %copy-start.2 = (bf16[192,1024]{1,0:T(8,128)(2,1)S(1)}, bf16[192,1024]{1,0:T(8,128)(2,1)}, u32[]{:S(2)}) copy-start(bf16[192,1024]{1,0:T(8,128)(2,1)} %copy-done.1) | copy-start | bytes 1179652
  99.0 31.2 %collective-permute-start.14 = (bf16[192,1024]{1,0:T(8,128)(2,1)}, bf16[192,1024]{1,0:T(8,128)(2,1)S(1)}, u32[]{:S(2)}, u32[]{:S(2)}) collective-permute-start(bf16[192,1024]{1,0:T(8,128)(2,1)} %collective-permute-done.13.refs_0_), channel_id=1, source_target_pairs={{0,240},{176,160},{192,176},{208,192},{224,208},{240,224},{1,241},... | collective-permute-start | bytes 1179656 | tf_op jit(solution)/shard_map/ppermute | solution.py:131
  104.2 4.0 %copy-start.6 = (bf16[192,1024]{1,0:T(8,128)(2,1)S(1)}, bf16[192,1024]{1,0:T(8,128)(2,1)}, u32[]{:S(2)}) copy-start(bf16[192,1024]{1,0:T(8,128)(2,1)} %copy-done.5) | copy-start | bytes 1179652
  112.1 32.4 %collective-permute-start.8 = (bf16[192,1024]{1,0:T(8,128)(2,1)S(1)}, bf16[192,1024]{1,0:T(8,128)(2,1)S(1)}, u32[]{:S(2)}, u32[]{:S(2)}) collective-permute-start(bf16[192,1024]{1,0:T(8,128)(2,1)S(1)} %collective-permute-done.7.f_ref), channel_id=1, source_target_pairs={{128,144},{144,160},{160,176},{176,192},{192,208},{208,224},{224,2... | collective-permute-start | bytes 1179656 | tf_op jit(solution)/shard_map/ppermute | solution.py:131
  140.6 4.0 %copy-start = (bf16[1,192,3584]{2,1,0:T(8,128)(2,1)S(1)}, bf16[1,192,3584]{2,1,0:T(8,128)(2,1)}, u32[]{:S(2)}) copy-start(bf16[1,192,3584]{2,1,0:T(8,128)(2,1)} %param.8) | copy-start | bytes 4128772

commit v3 on v2

v3 whole, which is shorter than its diff:
```python
import functools
import math

import jax
import jax.numpy as jnp
from jax import lax
from jax.experimental import pallas as pl
from jax.experimental.pallas import tpu as pltpu
from jax.sharding import PartitionSpec as P


HEAD_WIDTH = 128
NORM_EPS = 1e-06
SCALE = math.log2(math.e) / math.sqrt(HEAD_WIDTH)
VMEM_LIMIT = 12 * 1024 * 1024


def lanes(col, width):
    reps = -(-width // HEAD_WIDTH)
    wide = jnp.concatenate([col] * reps, axis=1) if reps > 1 else col
    return wide[:, :width]


def lane_sums(weights):
    width = weights.shape[1]
    whole = width - width % HEAD_WIDTH
    part = weights[:, :HEAD_WIDTH]
    for at in range(HEAD_WIDTH, whole, HEAD_WIDTH):
        part = part + weights[:, at : at + HEAD_WIDTH]
    if whole < width:
        rest = weights[:, whole:]
        fill = jnp.zeros((rest.shape[0], HEAD_WIDTH - rest.shape[1]), jnp.float32)
        part = part + jnp.concatenate([rest, fill], axis=1)
    return part


def each_head(q_ref, keys, values, acc_ref, total_ref, top_ref, q_heads, kv_heads, first):
    per_group = q_heads // kv_heads

    def column(ref, start, group):
        return ref[:, pl.ds(pl.multiple_of(start + group * HEAD_WIDTH, HEAD_WIDTH), HEAD_WIDTH)]

    def one_group(group, carry):
        key = jnp.concatenate([column(ref, start, group) for ref, start in keys], axis=0)
        value = jnp.concatenate([column(ref, start, group) for ref, start in values], axis=0)

        def score(i):
            query = column(q_ref, 0, group * per_group + i)
            scores = lax.dot_general(query, key, (((1,), (1,)), ((), ())), preferred_element_type=jnp.float32)
            if first:
                row = lax.broadcasted_iota(jnp.int32, scores.shape, 0)
                col = lax.broadcasted_iota(jnp.int32, scores.shape, 1)
                scores = jnp.where(col <= row, scores, -jnp.inf)
            return scores

        def weigh(i, scores):
            head = group * per_group + i
            rows, width = scores.shape
            top_here = jnp.max(scores, axis=1, keepdims=True) * SCALE
            if first:
                top, fade = jnp.broadcast_to(top_here, (rows, HEAD_WIDTH)), None
            else:
                top = jnp.maximum(top_ref[head], top_here)
                fade = jnp.exp2(top_ref[head] - top)
            top_ref[head] = top
            return jnp.exp2(scores * SCALE - lanes(top, width)), fade

        def add(i, weights, fade):
            head = group * per_group + i
            acc = jnp.dot(weights.astype(jnp.bfloat16), value, preferred_element_type=jnp.float32)
            total = lane_sums(weights)
            acc_ref[head] = acc if first else acc_ref[head] * fade + acc
            total_ref[head] = total if first else total_ref[head] * fade + total

        scores = [score(0), score(1)]
        waiting = None
        for i in range(per_group):
            if i + 2 < per_group:
                scores.append(score(i + 2))
            weighed = weigh(i, scores[i])
            scores[i] = None
            if waiting is not None:
                add(*waiting)
            waiting = (i, *weighed)
        add(*waiting)
        return carry

    lax.fori_loop(0, kv_heads, one_group, 0)


def first_kernel(_place, q_ref, k_ref, v_ref, q_out, acc_ref, total_ref, top_ref, *, q_heads, kv_heads):
    q_out[...] = q_ref[...]
    each_head(q_ref, ((k_ref, 0),), ((v_ref, 0),), acc_ref, total_ref, top_ref, q_heads, kv_heads, True)


def fold(place, step, count, k_ref, v_ref, b_ref, update):
    behind = place >= step
    keys, values = ((k_ref, 0),), ((v_ref, 0),)
    if b_ref is None:
        pl.when(behind)(lambda: update(keys, values))
    else:
        wrapped = place + step >= count
        wide = b_ref.shape[1] // 2
        pl.when(wrapped)(lambda: update(keys + ((b_ref, 0),), values + ((b_ref, wide),)))
        pl.when(jnp.logical_and(behind, jnp.logical_not(wrapped)))(lambda: update(keys, values))


def step_kernel(place_ref, q_ref, k_ref, v_ref, *refs, step, count, both, q_heads, kv_heads):
    b_ref = refs[0] if both else None
    state = refs[-3:]
    fold(
        place_ref[0], step, count, k_ref, v_ref, b_ref,
        lambda keys, values: each_head(q_ref, keys, values, *state, q_heads, kv_heads, False),
    )


def last_kernel(place_ref, q_ref, k_ref, v_ref, residual_ref, gain_ref, *refs, step, count, q_heads, kv_heads):
    acc_ref, total_ref, top_ref, out_ref = refs[-4:]
    fold(
        place_ref[0], step, count, k_ref, v_ref, None,
        lambda keys, values: each_head(
            q_ref, keys, values, acc_ref, total_ref, top_ref, q_heads, kv_heads, False
        ),
    )
    rows, width = out_ref.shape
    square = jnp.zeros((rows, HEAD_WIDTH), jnp.float32)
    for head in range(q_heads):
        at = slice(head * HEAD_WIDTH, (head + 1) * HEAD_WIDTH)
        total = jnp.sum(total_ref[head], axis=1, keepdims=True)
        attended = (acc_ref[head] / total).astype(jnp.bfloat16).astype(jnp.float32)
        hidden = residual_ref[:, at].astype(jnp.float32) + attended
        acc_ref[head] = hidden
        square = square + hidden * hidden
    inv_rms = lax.rsqrt(jnp.sum(square, axis=1, keepdims=True) / width + NORM_EPS)
    inv_rms = jnp.broadcast_to(inv_rms, (rows, HEAD_WIDTH))
    for head in range(q_heads):
        at = slice(head * HEAD_WIDTH, (head + 1) * HEAD_WIDTH)
        out_ref[:, at] = (acc_ref[head] * inv_rms * gain_ref[:, at]).astype(jnp.bfloat16)


def hops(count):
    backward = count * 3 // 8
    return count - 1 - backward, backward


def forward_pairs(count, step):
    return [(i, i + 1) for i in range(step - 1, count - 1)]


def backward_pairs(count, step, backward):
    return [(i, (i - 1) % count) for i in range(count) if (i + step - 1) % count < backward]


def shift(array, pairs):
    return lax.ppermute(array, "seq", pairs)


def layer(queries, keys, values, residual, norm_gain):
    count = lax.axis_size("seq")
    forward_steps, backward_steps = hops(count)
    query = queries[0]
    rows, width = query.shape
    q_heads = width // HEAD_WIDTH
    kv_heads = keys.shape[2] // HEAD_WIDTH
    place = lax.axis_index("seq").astype(jnp.int32).reshape(1)
    key, value = keys[0], values[0]
    own = jnp.concatenate([key, value], axis=1)
    state_shape = (q_heads, rows, HEAD_WIDTH)
    state = pltpu.VMEM(state_shape, jnp.float32)
    vmem = pl.BlockSpec(memory_space=pltpu.VMEM)
    smem = pl.BlockSpec(memory_space=pltpu.SMEM)
    params = pltpu.CompilerParams(vmem_limit_bytes=VMEM_LIMIT)

    def cost(keys_seen):
        return pl.CostEstimate(
            flops=4 * q_heads * rows * keys_seen * HEAD_WIDTH,
            transcendentals=q_heads * rows * keys_seen,
            bytes_accessed=4 * rows * width,
        )

    key_here = shift(key, forward_pairs(count, 1))
    value_here = shift(value, forward_pairs(count, 1))
    backward = shift(own, backward_pairs(count, 1, backward_steps))
    query, acc, total, top = pl.pallas_call(
        functools.partial(first_kernel, q_heads=q_heads, kv_heads=kv_heads),
        out_shape=(pltpu.VMEM(query.shape, query.dtype), state, state, state),
        in_specs=[smem, vmem, vmem, vmem],
        out_specs=(vmem, vmem, vmem, vmem),
        compiler_params=params,
        cost_estimate=cost(rows),
        name="first",
    )(place, query, key, value)
    for step in range(1, forward_steps):
        blocks = (key_here, value_here, backward) if step <= backward_steps else (key_here, value_here)
        key_here = shift(key_here, forward_pairs(count, step + 1))
        value_here = shift(value_here, forward_pairs(count, step + 1))
        if step < backward_steps:
            backward = shift(backward, backward_pairs(count, step + 1, backward_steps))
        at = 2 + len(blocks)
        acc, total, top = pl.pallas_call(
            functools.partial(
                step_kernel, step=step, count=count, both=len(blocks) == 3, q_heads=q_heads, kv_heads=kv_heads
            ),
            out_shape=(state, state, state),
            in_specs=[smem] + [vmem] * (at + 2),
            out_specs=(vmem, vmem, vmem),
            input_output_aliases={at: 0, at + 1: 1, at + 2: 2},
            compiler_params=params,
            cost_estimate=cost((len(blocks) - 1) * rows),
        )(place, query, *blocks, acc, total, top)
    _, _, _, normed = pl.pallas_call(
        functools.partial(last_kernel, step=forward_steps, count=count, q_heads=q_heads, kv_heads=kv_heads),
        out_shape=(state, state, state, jax.ShapeDtypeStruct((rows, width), jnp.bfloat16)),
        in_specs=[smem] + [vmem] * 8,
        out_specs=(vmem, vmem, vmem, vmem),
        input_output_aliases={6: 0, 7: 1, 8: 2},
        compiler_params=params,
        cost_estimate=cost(rows),
        name="last",
    )(place, query, key_here, value_here, residual[0], norm_gain.reshape(1, width), acc, total, top)
    return normed[None]


def solution(mesh):
    placed = P(("groups", "vocab", "batch"), "seq", None)
    return jax.shard_map(
        layer,
        mesh=mesh,
        in_specs=(placed, placed, placed, placed, P()),
        out_specs=placed,
        check_vma=False,
    )
```

time: 151 us -> 155 us (1.026)
  the two profiles are of different devices: /device:TPU:1622 before, /device:TPU:1356 now
where the time goes in v3:
time: 155 us; the launch traced here: 154 us
  starting transfers between devices  105 us (68%)
  Pallas kernels  38.6 us (25%)
  local copies, waits for them, and re-layouts  8.47 us (5%)
    ppermute x24, starting transfers between devices, shift(): return lax.ppermute(array, 'seq', pairs)  105 us
    pallas_call x8, Pallas kernels, layer(): pl.pallas_call(functools.partial(step_kernel, step=step, count=count, bot...  29.9 us
    unnamed x24, local copies, waits for them, and re-layouts  7.74 us
    pallas_call x1, Pallas kernels, layer(): pl.pallas_call(functools.partial(last_kernel, step=forward_steps, count=c...  5.78 us
  transfers between devices with their start and end apart: 24, of which 0 were waited for; matrix products, arithmetic and copies ran while one was open for 0% of the time, Pallas kernels for 21%

profile of v3, /device:TPU:1356, one launch (start us, length us, event | category | flops | bytes accessed | tf_op | source)
XLA Modules:
  0.0 154.0 jit_solution(1798801293826591410)
XLA Ops:
  2.5 5.1 %collective-permute-start.9 = (bf16[192,512]{1,0:T(8,128)(2,1)}, bf16[192,512]{1,0:T(8,128)(2,1)S(1)}, u32[]{:S(2)}, u32[]{:S(2)}) collective-permute-start(bf16[192,512]{1,0:T(8,128)(2,1)} %bitcast.11), channel_id=1, source_target_pairs={{0,16},{16,32},{32,48},{48,64},{64,80},{80,96},{96,112},{112,128},... | collective-permute-start | bytes 589832 | tf_op jit(solution)/shard_map/ppermute | solution.py:155
  7.6 5.1 %collective-permute-start = (bf16[192,512]{1,0:T(8,128)(2,1)}, bf16[192,512]{1,0:T(8,128)(2,1)S(1)}, u32[]{:S(2)}, u32[]{:S(2)}) collective-permute-start(bf16[192,512]{1,0:T(8,128)(2,1)} %bitcast.8), channel_id=1, source_target_pairs={{0,16},{16,32},{32,48},{48,64},{64,80},{80,96},{96,112},{112,128},... | collective-permute-start | bytes 589832 | tf_op jit(solution)/shard_map/ppermute | solution.py:155
  12.7 5.1 %collective-permute-start.10 = (bf16[192,512]{1,0:T(8,128)(2,1)S(1)}, bf16[192,512]{1,0:T(8,128)(2,1)S(1)}, u32[]{:S(2)}, u32[]{:S(2)}) collective-permute-start(bf16[192,512]{1,0:T(8,128)(2,1)S(1)} %collective-permute-done.9.v_ref), channel_id=1, source_target_pairs={{16,32},{32,48},{48,64},{64,80},{80,96},{96,112},{112,128},{128,14... | collective-permute-start | bytes 589832 | tf_op jit(solution)/shard_map/ppermute | solution.py:155
  18.6 5.7 %collective-permute-start.1 = (bf16[192,512]{1,0:T(8,128)(2,1)S(1)}, bf16[192,512]{1,0:T(8,128)(2,1)S(1)}, u32[]{:S(2)}, u32[]{:S(2)}) collective-permute-start(bf16[192,512]{1,0:T(8,128)(2,1)S(1)} %collective-permute-done.k_ref), channel_id=1, source_target_pairs={{16,32},{32,48},{48,64},{64,80},{80,96},{96,112},{112,128},{128,14... | collective-permute-start | bytes 589832 | tf_op jit(solution)/shard_map/ppermute | solution.py:155
  25.7 19.1 %collective-permute-start.11 = (bf16[192,512]{1,0:T(8,128)(2,1)S(1)}, bf16[192,512]{1,0:T(8,128)(2,1)S(1)}, u32[]{:S(2)}, u32[]{:S(2)}) collective-permute-start(bf16[192,512]{1,0:T(8,128)(2,1)S(1)} %collective-permute-done.10.v_ref), channel_id=1, source_target_pairs={{32,48},{48,64},{64,80},{80,96},{96,112},{112,128},{128,144},{144,... | collective-permute-start | bytes 589832 | tf_op jit(solution)/shard_map/ppermute | solution.py:155
  44.8 5.6 %collective-permute-start.2 = (bf16[192,512]{1,0:T(8,128)(2,1)S(1)}, bf16[192,512]{1,0:T(8,128)(2,1)S(1)}, u32[]{:S(2)}, u32[]{:S(2)}) collective-permute-start(bf16[192,512]{1,0:T(8,128)(2,1)S(1)} %collective-permute-done.1.k_ref), channel_id=1, source_target_pairs={{32,48},{48,64},{64,80},{80,96},{96,112},{112,128},{128,144},{144,... | collective-permute-start | bytes 589832 | tf_op jit(solution)/shard_map/ppermute | solution.py:155
  50.4 4.9 %collective-permute-start.12 = (bf16[192,512]{1,0:T(8,128)(2,1)S(1)}, bf16[192,512]{1,0:T(8,128)(2,1)S(1)}, u32[]{:S(2)}, u32[]{:S(2)}) collective-permute-start(bf16[192,512]{1,0:T(8,128)(2,1)S(1)} %collective-permute-done.11.v_ref), channel_id=1, source_target_pairs={{48,64},{64,80},{80,96},{96,112},{112,128},{128,144},{144,160},{16... | collective-permute-start | bytes 589832 | tf_op jit(solution)/shard_map/ppermute | solution.py:155
  55.4 5.4 %collective-permute-start.3 = (bf16[192,512]{1,0:T(8,128)(2,1)S(1)}, bf16[192,512]{1,0:T(8,128)(2,1)S(1)}, u32[]{:S(2)}, u32[]{:S(2)}) collective-permute-start(bf16[192,512]{1,0:T(8,128)(2,1)S(1)} %collective-permute-done.2.k_ref), channel_id=1, source_target_pairs={{48,64},{64,80},{80,96},{96,112},{112,128},{128,144},{144,160},{16... | collective-permute-start | bytes 589832 | tf_op jit(solution)/shard_map/ppermute | solution.py:155
  62.1 4.2 %collective-permute-start.13 = (bf16[192,512]{1,0:T(8,128)(2,1)S(1)}, bf16[192,512]{1,0:T(8,128)(2,1)S(1)}, u32[]{:S(2)}, u32[]{:S(2)}) collective-permute-start(bf16[192,512]{1,0:T(8,128)(2,1)S(1)} %collective-permute-done.12.v_ref), channel_id=1, source_target_pairs={{64,80},{80,96},{96,112},{112,128},{128,144},{144,160},{160,176},{... | collective-permute-start | bytes 589832 | tf_op jit(solution)/shard_map/ppermute | solution.py:155
  66.3 4.5 %collective-permute-start.4 = (bf16[192,512]{1,0:T(8,128)(2,1)S(1)}, bf16[192,512]{1,0:T(8,128)(2,1)S(1)}, u32[]{:S(2)}, u32[]{:S(2)}) collective-permute-start(bf16[192,512]{1,0:T(8,128)(2,1)S(1)} %collective-permute-done.3.k_ref), channel_id=1, source_target_pairs={{64,80},{80,96},{96,112},{112,128},{128,144},{144,160},{160,176},{... | collective-permute-start | bytes 589832 | tf_op jit(solution)/shard_map/ppermute | solution.py:155
  70.8 4.6 %collective-permute-start.14 = (bf16[192,512]{1,0:T(8,128)(2,1)S(1)}, bf16[192,512]{1,0:T(8,128)(2,1)}, u32[]{:S(2)}, u32[]{:S(2)}) collective-permute-start(bf16[192,512]{1,0:T(8,128)(2,1)S(1)} %collective-permute-done.13.v_ref), channel_id=1, source_target_pairs={{80,96},{96,112},{112,128},{128,144},{144,160},{160,176},{176,192}... | collective-permute-start | bytes 589832 | tf_op jit(solution)/shard_map/ppermute | solution.py:155
  75.5 4.7 %collective-permute-start.5 = (bf16[192,512]{1,0:T(8,128)(2,1)S(1)}, bf16[192,512]{1,0:T(8,128)(2,1)}, u32[]{:S(2)}, u32[]{:S(2)}) collective-permute-start(bf16[192,512]{1,0:T(8,128)(2,1)S(1)} %collective-permute-done.4.k_ref), channel_id=1, source_target_pairs={{80,96},{96,112},{112,128},{128,144},{144,160},{160,176},{176,192}... | collective-permute-start | bytes 589832 | tf_op jit(solution)/shard_map/ppermute | solution.py:155
  81.6 6.3 %collective-permute-start.15 = (bf16[192,512]{1,0:T(8,128)(2,1)}, bf16[192,512]{1,0:T(8,128)(2,1)S(1)}, u32[]{:S(2)}, u32[]{:S(2)}) collective-permute-start(bf16[192,512]{1,0:T(8,128)(2,1)} %collective-permute-done.14.v_ref), channel_id=1, source_target_pairs={{96,112},{112,128},{128,144},{144,160},{160,176},{176,192},{192,20... | collective-permute-start | bytes 589832 | tf_op jit(solution)/shard_map/ppermute | solution.py:155
  87.9 5.8 %collective-permute-start.6 = (bf16[192,512]{1,0:T(8,128)(2,1)}, bf16[192,512]{1,0:T(8,128)(2,1)S(1)}, u32[]{:S(2)}, u32[]{:S(2)}) collective-permute-start(bf16[192,512]{1,0:T(8,128)(2,1)} %collective-permute-done.5.k_ref), channel_id=1, source_target_pairs={{96,112},{112,128},{128,144},{144,160},{160,176},{176,192},{192,20... | collective-permute-start | bytes 589832 | tf_op jit(solution)/shard_map/ppermute | solution.py:155
  112.4 3.5 %shard_map.56 = (f32[28,192,128]{2,1,0:T(8,128)S(1)}, f32[28,192,128]{2,1,0:T(8,128)S(1)}, f32[28,192,128]{2,1,0:T(8,128)S(1)}) custom-call(s32[1]{0:T(128)} %bitcast._place.place_ref, bf16[192,3584]{1,0:T(8,128)(2,1)S(1)} %get-tuple-element.34.q_ref, ...), custom_call_target="tpu_custom_call", output_to_operand_aliasing={{0}: (5, {}), {1}: (6, {}), {2}: (7, {})} | custom-call | flops 1056964608 | bytes 2752512 | tf_op jit(solution)/shard_map/pallas_call | solution.py:200
  115.9 3.5 %shard_map.57 = (f32[28,192,128]{2,1,0:T(8,128)S(1)}, f32[28,192,128]{2,1,0:T(8,128)S(1)}, f32[28,192,128]{2,1,0:T(8,128)S(1)}) custom-call(s32[1]{0:T(128)} %bitcast._place.place_ref, bf16[192,3584]{1,0:T(8,128)(2,1)S(1)} %get-tuple-element.34.q_ref, bf16[192,512]{1,0:T(8,128)(2,1)S(1)} %copy-done.4, ...), custom_call_target="tpu_custom_call", output_to_operand_aliasing={{0}: (5, {}), {1}: (6, {}), {2}: (7, {})} | custom-call | flops 1056964608 | bytes 2752512 | tf_op jit(solution)/shard_map/pallas_call | solution.py:200
  119.4 4.6 %collective-permute-start.17 = (bf16[192,512]{1,0:T(8,128)(2,1)S(1)}, bf16[192,512]{1,0:T(8,128)(2,1)S(1)}, u32[]{:S(2)}, u32[]{:S(2)}) collective-permute-start(bf16[192,512]{1,0:T(8,128)(2,1)S(1)} %collective-permute-done.16.v_ref), channel_id=1, source_target_pairs={{128,144},{144,160},{160,176},{176,192},{192,208},{208,224},{224,2... | collective-permute-start | bytes 589832 | tf_op jit(solution)/shard_map/ppermute | solution.py:155
  124.0 4.5 %collective-permute-start.8 = (bf16[192,512]{1,0:T(8,128)(2,1)S(1)}, bf16[192,512]{1,0:T(8,128)(2,1)S(1)}, u32[]{:S(2)}, u32[]{:S(2)}) collective-permute-start(bf16[192,512]{1,0:T(8,128)(2,1)S(1)} %collective-permute-done.7.k_ref), channel_id=1, source_target_pairs={{128,144},{144,160},{160,176},{176,192},{192,208},{208,224},{224,2... | collective-permute-start | bytes 589832 | tf_op jit(solution)/shard_map/ppermute | solution.py:155
  128.6 3.5 %shard_map.58 = (f32[28,192,128]{2,1,0:T(8,128)S(1)}, f32[28,192,128]{2,1,0:T(8,128)S(1)}, f32[28,192,128]{2,1,0:T(8,128)S(1)}) custom-call(s32[1]{0:T(128)} %bitcast._place.place_ref, bf16[192,3584]{1,0:T(8,128)(2,1)S(1)} %get-tuple-element.34.q_ref, ...), custom_call_target="tpu_custom_call", output_to_operand_aliasing={{0}: (5, {}), {1}: (6, {}), {2}: (7, {})} | custom-call | flops 1056964608 | bytes 2752512 | tf_op jit(solution)/shard_map/pallas_call | solution.py:200
  132.1 3.7 %shard_map.59 = (f32[28,192,128]{2,1,0:T(8,128)S(1)}, f32[28,192,128]{2,1,0:T(8,128)S(1)}, f32[28,192,128]{2,1,0:T(8,128)S(1)}) custom-call(s32[1]{0:T(128)} %bitcast._place.place_ref, bf16[192,3584]{1,0:T(8,128)(2,1)S(1)} %get-tuple-element.34.q_ref, bf16[192,512]{1,0:T(8,128)(2,1)S(1)} %copy-done.6, ...), custom_call_target="tpu_custom_call", output_to_operand_aliasing={{0}: (5, {}), {1}: (6, {}), {2}: (7, {})} | custom-call | flops 1056964608 | bytes 2752512 | tf_op jit(solution)/shard_map/pallas_call | solution.py:200
  135.8 5.4 %shard_map.60 = (f32[28,192,128]{2,1,0:T(8,128)S(1)}, f32[28,192,128]{2,1,0:T(8,128)S(1)}, f32[28,192,128]{2,1,0:T(8,128)S(1)}) custom-call(s32[1]{0:T(128)} %bitcast._place.place_ref, bf16[192,3584]{1,0:T(8,128)(2,1)S(1)} %get-tuple-element.34.q_ref, ...), custom_call_target="tpu_custom_call", output_to_operand_aliasing={{0}: (5, {}), {1}: (6, {}), {2}: (7, {})} | custom-call | flops 1056964608 | bytes 2752512 | tf_op jit(solution)/shard_map/pallas_call | solution.py:200
  141.2 3.5 %shard_map.61 = (f32[28,192,128]{2,1,0:T(8,128)S(1)}, f32[28,192,128]{2,1,0:T(8,128)S(1)}, f32[28,192,128]{2,1,0:T(8,128)S(1)}) custom-call(s32[1]{0:T(128)} %bitcast._place.place_ref, bf16[192,3584]{1,0:T(8,128)(2,1)S(1)} %get-tuple-element.34.q_ref, ...), custom_call_target="tpu_custom_call", output_to_operand_aliasing={{0}: (4, {}), {1}: (5, {}), {2}: (6, {})} | custom-call | flops 528482304 | bytes 2752512 | tf_op jit(solution)/shard_map/pallas_call | solution.py:200
  144.7 3.5 %shard_map.62 = (f32[28,192,128]{2,1,0:T(8,128)S(1)}, f32[28,192,128]{2,1,0:T(8,128)S(1)}, f32[28,192,128]{2,1,0:T(8,128)S(1)}) custom-call(s32[1]{0:T(128)} %bitcast._place.place_ref, bf16[192,3584]{1,0:T(8,128)(2,1)S(1)} %get-tuple-element.34.q_ref, ...), custom_call_target="tpu_custom_call", output_to_operand_aliasing={{0}: (4, {}), {1}: (5, {}), {2}: (6, {})} | custom-call | flops 528482304 | bytes 2752512 | tf_op jit(solution)/shard_map/pallas_call | solution.py:200
  148.2 5.8 %last.1 = (f32[28,192,128]{2,1,0:T(8,128)S(1)}, f32[28,192,128]{2,1,0:T(8,128)S(1)}, f32[28,192,128]{2,1,0:T(8,128)S(1)}, bf16[192,3584]{1,0:T(8,128)(2,1)}) custom-call(s32[1]{0:T(128)} %bitcast._place.place_ref, bf16[192,3584]{1,0:T(8,128)(2,1)S(1)} %get-tuple-element.34.q_ref, ...), custom_call_target="tpu_custom_call", output_to_operand_aliasing={{0}: (6, {}), {1}: (7, {}), {2}: (8, {})} | custom-call | flops 528482304 | bytes 2752512 | tf_op jit(solution)/shard_map/last/pallas_call | solution.py:211
  (60 shorter events, 25.9 us)
Async XLA Ops:
  1.1 0.7 collective-permute-start.18
  1.8 23.2 %collective-permute-start.19 = (bf16[192,1024]{1,0:T(8,128)(2,1)S(1)}, bf16[192,1024]{1,0:T(8,128)(2,1)S(1)}, u32[]{:S(2)}, u32[]{:S(2)}) collective-permute-start(bf16[192,1024]{1,0:T(8,128)(2,1)S(1)} %collective-permute-done.18.refs_0_), channel_id=1, source_target_pairs={{0,240},{16,0},{32,16},{48,32},{64,48},{240,224},{1,241},{17,1},{3... | collective-permute-start | bytes 1179656 | tf_op jit(solution)/shard_map/ppermute | solution.py:155
  2.5 10.3 %collective-permute-start.9 = (bf16[192,512]{1,0:T(8,128)(2,1)}, bf16[192,512]{1,0:T(8,128)(2,1)S(1)}, u32[]{:S(2)}, u32[]{:S(2)}) collective-permute-start(bf16[192,512]{1,0:T(8,128)(2,1)} %bitcast.11), channel_id=1, source_target_pairs={{0,16},{16,32},{32,48},{48,64},{64,80},{80,96},{96,112},{112,128},... | collective-permute-start | bytes 589832 | tf_op jit(solution)/shard_map/ppermute | solution.py:155
  7.6 11.0 %collective-permute-start = (bf16[192,512]{1,0:T(8,128)(2,1)}, bf16[192,512]{1,0:T(8,128)(2,1)S(1)}, u32[]{:S(2)}, u32[]{:S(2)}) collective-permute-start(bf16[192,512]{1,0:T(8,128)(2,1)} %bitcast.8), channel_id=1, source_target_pairs={{0,16},{16,32},{32,48},{48,64},{64,80},{80,96},{96,112},{112,128},... | collective-permute-start | bytes 589832 | tf_op jit(solution)/shard_map/ppermute | solution.py:155
  12.7 12.9 %collective-permute-start.10 = (bf16[192,512]{1,0:T(8,128)(2,1)S(1)}, bf16[192,512]{1,0:T(8,128)(2,1)S(1)}, u32[]{:S(2)}, u32[]{:S(2)}) collective-permute-start(bf16[192,512]{1,0:T(8,128)(2,1)S(1)} %collective-permute-done.9.v_ref), channel_id=1, source_target_pairs={{16,32},{32,48},{48,64},{64,80},{80,96},{96,112},{112,128},{128,14... | collective-permute-start | bytes 589832 | tf_op jit(solution)/shard_map/ppermute | solution.py:155
  18.6 26.3 %collective-permute-start.1 = (bf16[192,512]{1,0:T(8,128)(2,1)S(1)}, bf16[192,512]{1,0:T(8,128)(2,1)S(1)}, u32[]{:S(2)}, u32[]{:S(2)}) collective-permute-start(bf16[192,512]{1,0:T(8,128)(2,1)S(1)} %collective-permute-done.k_ref), channel_id=1, source_target_pairs={{16,32},{32,48},{48,64},{64,80},{80,96},{96,112},{112,128},{128,14... | collective-permute-start | bytes 589832 | tf_op jit(solution)/shard_map/ppermute | solution.py:155
  25.0 36.4 %collective-permute-start.20 = (bf16[192,1024]{1,0:T(8,128)(2,1)S(1)}, bf16[192,1024]{1,0:T(8,128)(2,1)S(1)}, u32[]{:S(2)}, u32[]{:S(2)}) collective-permute-start(bf16[192,1024]{1,0:T(8,128)(2,1)S(1)} %collective-permute-done.19.refs_0_), channel_id=1, source_target_pairs={{0,240},{16,0},{32,16},{48,32},{224,208},{240,224},{1,241},{17,1},... | collective-permute-start | bytes 1179656 | tf_op jit(solution)/shard_map/ppermute | solution.py:155
  25.7 24.7 %collective-permute-start.11 = (bf16[192,512]{1,0:T(8,128)(2,1)S(1)}, bf16[192,512]{1,0:T(8,128)(2,1)S(1)}, u32[]{:S(2)}, u32[]{:S(2)}) collective-permute-start(bf16[192,512]{1,0:T(8,128)(2,1)S(1)} %collective-permute-done.10.v_ref), channel_id=1, source_target_pairs={{32,48},{48,64},{64,80},{80,96},{96,112},{112,128},{128,144},{144,... | collective-permute-start | bytes 589832 | tf_op jit(solution)/shard_map/ppermute | solution.py:155
  44.8 10.5 %collective-permute-start.2 = (bf16[192,512]{1,0:T(8,128)(2,1)S(1)}, bf16[192,512]{1,0:T(8,128)(2,1)S(1)}, u32[]{:S(2)}, u32[]{:S(2)}) collective-permute-start(bf16[192,512]{1,0:T(8,128)(2,1)S(1)} %collective-permute-done.1.k_ref), channel_id=1, source_target_pairs={{32,48},{48,64},{64,80},{80,96},{96,112},{112,128},{128,144},{144,... | collective-permute-start | bytes 589832 | tf_op jit(solution)/shard_map/ppermute | solution.py:155
  50.4 11.7 %collective-permute-start.12 = (bf16[192,512]{1,0:T(8,128)(2,1)S(1)}, bf16[192,512]{1,0:T(8,128)(2,1)S(1)}, u32[]{:S(2)}, u32[]{:S(2)}) collective-permute-start(bf16[192,512]{1,0:T(8,128)(2,1)S(1)} %collective-permute-done.11.v_ref), channel_id=1, source_target_pairs={{48,64},{64,80},{80,96},{96,112},{112,128},{128,144},{144,160},{16... | collective-permute-start | bytes 589832 | tf_op jit(solution)/shard_map/ppermute | solution.py:155
  55.4 10.9 %collective-permute-start.3 = (bf16[192,512]{1,0:T(8,128)(2,1)S(1)}, bf16[192,512]{1,0:T(8,128)(2,1)S(1)}, u32[]{:S(2)}, u32[]{:S(2)}) collective-permute-start(bf16[192,512]{1,0:T(8,128)(2,1)S(1)} %collective-permute-done.2.k_ref), channel_id=1, source_target_pairs={{48,64},{64,80},{80,96},{96,112},{112,128},{128,144},{144,160},{16... | collective-permute-start | bytes 589832 | tf_op jit(solution)/shard_map/ppermute | solution.py:155
  61.4 19.5 %collective-permute-start.21 = (bf16[192,1024]{1,0:T(8,128)(2,1)S(1)}, bf16[192,1024]{1,0:T(8,128)(2,1)S(1)}, u32[]{:S(2)}, u32[]{:S(2)}) collective-permute-start(bf16[192,1024]{1,0:T(8,128)(2,1)S(1)} %collective-permute-done.20.refs_0_), channel_id=1, source_target_pairs={{0,240},{16,0},{32,16},{208,192},{224,208},{240,224},{1,241},{17,1... | collective-permute-start | bytes 1179656 | tf_op jit(solution)/shard_map/ppermute | solution.py:155
  62.1 8.7 %collective-permute-start.13 = (bf16[192,512]{1,0:T(8,128)(2,1)S(1)}, bf16[192,512]{1,0:T(8,128)(2,1)S(1)}, u32[]{:S(2)}, u32[]{:S(2)}) collective-permute-start(bf16[192,512]{1,0:T(8,128)(2,1)S(1)} %collective-permute-done.12.v_ref), channel_id=1, source_target_pairs={{64,80},{80,96},{96,112},{112,128},{128,144},{144,160},{160,176},{... | collective-permute-start | bytes 589832 | tf_op jit(solution)/shard_map/ppermute | solution.py:155
  66.3 9.1 %collective-permute-start.4 = (bf16[192,512]{1,0:T(8,128)(2,1)S(1)}, bf16[192,512]{1,0:T(8,128)(2,1)S(1)}, u32[]{:S(2)}, u32[]{:S(2)}) collective-permute-start(bf16[192,512]{1,0:T(8,128)(2,1)S(1)} %collective-permute-done.3.k_ref), channel_id=1, source_target_pairs={{64,80},{80,96},{96,112},{112,128},{128,144},{144,160},{160,176},{... | collective-permute-start | bytes 589832 | tf_op jit(solution)/shard_map/ppermute | solution.py:155
  70.8 10.7 %collective-permute-start.14 = (bf16[192,512]{1,0:T(8,128)(2,1)S(1)}, bf16[192,512]{1,0:T(8,128)(2,1)}, u32[]{:S(2)}, u32[]{:S(2)}) collective-permute-start(bf16[192,512]{1,0:T(8,128)(2,1)S(1)} %collective-permute-done.13.v_ref), channel_id=1, source_target_pairs={{80,96},{96,112},{112,128},{128,144},{144,160},{160,176},{176,192}... | collective-permute-start | bytes 589832 | tf_op jit(solution)/shard_map/ppermute | solution.py:155
  75.5 12.4 %collective-permute-start.5 = (bf16[192,512]{1,0:T(8,128)(2,1)S(1)}, bf16[192,512]{1,0:T(8,128)(2,1)}, u32[]{:S(2)}, u32[]{:S(2)}) collective-permute-start(bf16[192,512]{1,0:T(8,128)(2,1)S(1)} %collective-permute-done.4.k_ref), channel_id=1, source_target_pairs={{80,96},{96,112},{112,128},{128,144},{144,160},{160,176},{176,192}... | collective-permute-start | bytes 589832 | tf_op jit(solution)/shard_map/ppermute | solution.py:155
  80.9 30.2 %collective-permute-start.22 = (bf16[192,1024]{1,0:T(8,128)(2,1)S(1)}, bf16[192,1024]{1,0:T(8,128)(2,1)S(1)}, u32[]{:S(2)}, u32[]{:S(2)}) collective-permute-start(bf16[192,1024]{1,0:T(8,128)(2,1)S(1)} %collective-permute-done.21.refs_0_), channel_id=1, source_target_pairs={{0,240},{16,0},{192,176},{208,192},{224,208},{240,224},{1,241},{17... | collective-permute-start | bytes 1179656 | tf_op jit(solution)/shard_map/ppermute | solution.py:155
  81.6 24.2 %collective-permute-start.15 = (bf16[192,512]{1,0:T(8,128)(2,1)}, bf16[192,512]{1,0:T(8,128)(2,1)S(1)}, u32[]{:S(2)}, u32[]{:S(2)}) collective-permute-start(bf16[192,512]{1,0:T(8,128)(2,1)} %collective-permute-done.14.v_ref), channel_id=1, source_target_pairs={{96,112},{112,128},{128,144},{144,160},{160,176},{176,192},{192,20... | collective-permute-start | bytes 589832 | tf_op jit(solution)/shard_map/ppermute | solution.py:155
  87.9 20.8 %collective-permute-start.6 = (bf16[192,512]{1,0:T(8,128)(2,1)}, bf16[192,512]{1,0:T(8,128)(2,1)S(1)}, u32[]{:S(2)}, u32[]{:S(2)}) collective-permute-start(bf16[192,512]{1,0:T(8,128)(2,1)} %collective-permute-done.5.k_ref), channel_id=1, source_target_pairs={{96,112},{112,128},{128,144},{144,160},{160,176},{176,192},{192,20... | collective-permute-start | bytes 589832 | tf_op jit(solution)/shard_map/ppermute | solution.py:155
  105.8 13.6 %collective-permute-start.16 = (bf16[192,512]{1,0:T(8,128)(2,1)S(1)}, bf16[192,512]{1,0:T(8,128)(2,1)S(1)}, u32[]{:S(2)}, u32[]{:S(2)}) collective-permute-start(bf16[192,512]{1,0:T(8,128)(2,1)S(1)} %collective-permute-done.15.v_ref), channel_id=1, source_target_pairs={{112,128},{128,144},{144,160},{160,176},{176,192},{192,208},{208,2... | collective-permute-start | bytes 589832 | tf_op jit(solution)/shard_map/ppermute | solution.py:155
  108.6 15.4 %collective-permute-start.7 = (bf16[192,512]{1,0:T(8,128)(2,1)S(1)}, bf16[192,512]{1,0:T(8,128)(2,1)S(1)}, u32[]{:S(2)}, u32[]{:S(2)}) collective-permute-start(bf16[192,512]{1,0:T(8,128)(2,1)S(1)} %collective-permute-done.6.k_ref), channel_id=1, source_target_pairs={{112,128},{128,144},{144,160},{160,176},{176,192},{192,208},{208,2... | collective-permute-start | bytes 589832 | tf_op jit(solution)/shard_map/ppermute | solution.py:155
  111.1 24.6 %collective-permute-start.23 = (bf16[192,1024]{1,0:T(8,128)(2,1)S(1)}, bf16[192,1024]{1,0:T(8,128)(2,1)S(1)}, u32[]{:S(2)}, u32[]{:S(2)}) collective-permute-start(bf16[192,1024]{1,0:T(8,128)(2,1)S(1)} %collective-permute-done.22.refs_0_), channel_id=1, source_target_pairs={{0,240},{176,160},{192,176},{208,192},{224,208},{240,224},{1,241},... | collective-permute-start | bytes 1179656 | tf_op jit(solution)/shard_map/ppermute | solution.py:155
  119.4 28.7 %collective-permute-start.17 = (bf16[192,512]{1,0:T(8,128)(2,1)S(1)}, bf16[192,512]{1,0:T(8,128)(2,1)S(1)}, u32[]{:S(2)}, u32[]{:S(2)}) collective-permute-start(bf16[192,512]{1,0:T(8,128)(2,1)S(1)} %collective-permute-done.16.v_ref), channel_id=1, source_target_pairs={{128,144},{144,160},{160,176},{176,192},{192,208},{208,224},{224,2... | collective-permute-start | bytes 589832 | tf_op jit(solution)/shard_map/ppermute | solution.py:155
  124.0 24.1 %collective-permute-start.8 = (bf16[192,512]{1,0:T(8,128)(2,1)S(1)}, bf16[192,512]{1,0:T(8,128)(2,1)S(1)}, u32[]{:S(2)}, u32[]{:S(2)}) collective-permute-start(bf16[192,512]{1,0:T(8,128)(2,1)S(1)} %collective-permute-done.7.k_ref), channel_id=1, source_target_pairs={{128,144},{144,160},{160,176},{176,192},{192,208},{208,224},{224,2... | collective-permute-start | bytes 589832 | tf_op jit(solution)/shard_map/ppermute | solution.py:155
  (12 other events, 18.3 us)

commit v4 on v3

--- a/solution.py
+++ b/solution.py
@@ -88,36 +88,49 @@
     lax.fori_loop(0, kv_heads, one_group, 0)
 
 
-def first_kernel(_place, q_ref, k_ref, v_ref, q_out, acc_ref, total_ref, top_ref, *, q_heads, kv_heads):
+def first_kernel(_place, q_ref, own_ref, q_out, acc_ref, total_ref, top_ref, *, q_heads, kv_heads):
     q_out[...] = q_ref[...]
-    each_head(q_ref, ((k_ref, 0),), ((v_ref, 0),), acc_ref, total_ref, top_ref, q_heads, kv_heads, True)
-
-
-def fold(place, step, count, k_ref, v_ref, b_ref, update):
+    wide = own_ref.shape[1] // 2
+    each_head(q_ref, ((own_ref, 0),), ((own_ref, wide),), acc_ref, total_ref, top_ref, q_heads, kv_heads, True)
+
+
+def fold(place, step, turn, count, f_ref, b_ref, update):
     behind = place >= step
-    keys, values = ((k_ref, 0),), ((v_ref, 0),)
+    wide = f_ref.shape[1] // 2
+    keys, values = ((f_ref, 0),), ((f_ref, wide),)
     if b_ref is None:
         pl.when(behind)(lambda: update(keys, values))
     else:
-        wrapped = place + step >= count
-        wide = b_ref.shape[1] // 2
+        wrapped = place + turn >= count
         pl.when(wrapped)(lambda: update(keys + ((b_ref, 0),), values + ((b_ref, wide),)))
         pl.when(jnp.logical_and(behind, jnp.logical_not(wrapped)))(lambda: update(keys, values))
 
 
-def step_kernel(place_ref, q_ref, k_ref, v_ref, *refs, step, count, both, q_heads, kv_heads):
-    b_ref = refs[0] if both else None
+def merge_kernel(place_ref, direct_ref, passed_ref, out_ref, *, count):
+    last = place_ref[0] == count - 1
+
+    @pl.when(last)
+    def _():
+        out_ref[...] = direct_ref[...]
+
+    @pl.when(jnp.logical_not(last))
+    def _():
+        out_ref[...] = passed_ref[...]
+
+
+def step_kernel(place_ref, q_ref, f_ref, *refs, step, turn, count, q_heads, kv_heads):
+    b_ref = refs[0] if turn else None
     state = refs[-3:]
     fold(
-        place_ref[0], step, count, k_ref, v_ref, b_ref,
+        place_ref[0], step, turn, count, f_ref, b_ref,
         lambda keys, values: each_head(q_ref, keys, values, *state, q_heads, kv_heads, False),
     )
 
 
-def last_kernel(place_ref, q_ref, k_ref, v_ref, residual_ref, gain_ref, *refs, step, count, q_heads, kv_heads):
+def last_kernel(place_ref, q_ref, f_ref, residual_ref, gain_ref, *refs, step, count, q_heads, kv_heads):
     acc_ref, total_ref, top_ref, out_ref = refs[-4:]
     fold(
-        place_ref[0], step, count, k_ref, v_ref, None,
+        place_ref[0], step, None, count, f_ref, None,
         lambda keys, values: each_head(
             q_ref, keys, values, acc_ref, total_ref, top_ref, q_heads, kv_heads, False
         ),
@@ -138,17 +151,19 @@
         out_ref[:, at] = (acc_ref[head] * inv_rms * gain_ref[:, at]).astype(jnp.bfloat16)
 
 
-def hops(count):
-    backward = count * 3 // 8
-    return count - 1 - backward, backward
+def plan(count):
+    wrapped = count * 6 // 16
+    forward = count - 1 - wrapped
+    folds = [min(2 * turn, forward - 1 - (wrapped - turn)) for turn in range(1, wrapped + 1)]
+    return forward, wrapped, folds
 
 
 def forward_pairs(count, step):
     return [(i, i + 1) for i in range(step - 1, count - 1)]
 
 
-def backward_pairs(count, step, backward):
-    return [(i, (i - 1) % count) for i in range(count) if (i + step - 1) % count < backward]
+def pass_pairs(count, turn):
+    return [(count - 1 - i, count - 2 - i) for i in range(turn)]
 
 
 def shift(array, pairs):
@@ -157,14 +172,13 @@
 
 def layer(queries, keys, values, residual, norm_gain):
     count = lax.axis_size("seq")
-    forward_steps, backward_steps = hops(count)
+    forward_steps, wrapped_blocks, folds = plan(count)
     query = queries[0]
     rows, width = query.shape
     q_heads = width // HEAD_WIDTH
     kv_heads = keys.shape[2] // HEAD_WIDTH
     place = lax.axis_index("seq").astype(jnp.int32).reshape(1)
-    key, value = keys[0], values[0]
-    own = jnp.concatenate([key, value], axis=1)
+    own = jnp.concatenate([keys[0], values[0]], axis=1)
     state_shape = (q_heads, rows, HEAD_WIDTH)
     state = pltpu.VMEM(state_shape, jnp.float32)
     vmem = pl.BlockSpec(memory_space=pltpu.VMEM)
@@ -178,46 +192,60 @@
             bytes_accessed=4 * rows * width,
         )
 
-    key_here = shift(key, forward_pairs(count, 1))
-    value_here = shift(value, forward_pairs(count, 1))
-    backward = shift(own, backward_pairs(count, 1, backward_steps))
+    forward = shift(own, forward_pairs(count, 1))
+    direct = [shift(own, [(0, count - 1)])]
     query, acc, total, top = pl.pallas_call(
         functools.partial(first_kernel, q_heads=q_heads, kv_heads=kv_heads),
         out_shape=(pltpu.VMEM(query.shape, query.dtype), state, state, state),
-        in_specs=[smem, vmem, vmem, vmem],
+        in_specs=[smem, vmem, vmem],
         out_specs=(vmem, vmem, vmem, vmem),
         compiler_params=params,
         cost_estimate=cost(rows),
         name="first",
-    )(place, query, key, value)
+    )(place, query, own)
+    passed = None
     for step in range(1, forward_steps):
-        blocks = (key_here, value_here, backward) if step <= backward_steps else (key_here, value_here)
-        key_here = shift(key_here, forward_pairs(count, step + 1))
-        value_here = shift(value_here, forward_pairs(count, step + 1))
-        if step < backward_steps:
-            backward = shift(backward, backward_pairs(count, step + 1, backward_steps))
+        blocks = (forward,)
+        forward = shift(forward, forward_pairs(count, step + 1))
+        if step < wrapped_blocks:
+            direct.append(shift(own, [(step, count - 1)]))
+        turn = folds.index(step) + 1 if step in folds else None
+        if turn:
+            merged = direct[turn - 1]
+            if passed is not None:
+                merged = pl.pallas_call(
+                    functools.partial(merge_kernel, count=count),
+                    out_shape=pltpu.VMEM(own.shape, own.dtype),
+                    in_specs=[smem, vmem, vmem],
+                    out_specs=vmem,
+                    compiler_params=params,
+                    cost_estimate=pl.CostEstimate(flops=own.size, transcendentals=0, bytes_accessed=4 * own.size),
+                )(place, merged, passed)
+            if turn < wrapped_blocks:
+                passed = shift(merged, pass_pairs(count, turn))
+            blocks = blocks + (merged,)
         at = 2 + len(blocks)
         acc, total, top = pl.pallas_call(
             functools.partial(
-                step_kernel, step=step, count=count, both=len(blocks) == 3, q_heads=q_heads, kv_heads=kv_heads
+                step_kernel, step=step, turn=turn, count=count, q_heads=q_heads, kv_heads=kv_heads
             ),
             out_shape=(state, state, state),
             in_specs=[smem] + [vmem] * (at + 2),
             out_specs=(vmem, vmem, vmem),
             input_output_aliases={at: 0, at + 1: 1, at + 2: 2},
             compiler_params=params,
-            cost_estimate=cost((len(blocks) - 1) * rows),
+            cost_estimate=cost(len(blocks) * rows),
         )(place, query, *blocks, acc, total, top)
     _, _, _, normed = pl.pallas_call(
         functools.partial(last_kernel, step=forward_steps, count=count, q_heads=q_heads, kv_heads=kv_heads),
         out_shape=(state, state, state, jax.ShapeDtypeStruct((rows, width), jnp.bfloat16)),
-        in_specs=[smem] + [vmem] * 8,
+        in_specs=[smem] + [vmem] * 7,
         out_specs=(vmem, vmem, vmem, vmem),
-        input_output_aliases={6: 0, 7: 1, 8: 2},
+        input_output_aliases={5: 0, 6: 1, 7: 2},
         compiler_params=params,
         cost_estimate=cost(rows),
         name="last",
-    )(place, query, key_here, value_here, residual[0], norm_gain.reshape(1, width), acc, total, top)
+    )(place, query, forward, residual[0], norm_gain.reshape(1, width), acc, total, top)
     return normed[None]
 
 

time: 155 us -> 139 us (0.90)
  the two profiles are of different devices: /device:TPU:1356 before, /device:TPU:1486 now
where the time goes in v4:
time: 139 us
  starting transfers between devices  59.9 us (43%)
  Pallas kernels  39.5 us (28%)
  waiting for transfers between devices  37.8 us (27%)
    ppermute x20, starting transfers between devices, shift(): return lax.ppermute(array, 'seq', pairs)  59.9 us
    ppermute x20, waiting for transfers between devices, shift(): return lax.ppermute(array, 'seq', pairs)  37.8 us
    pallas_call x8, Pallas kernels, layer(): pl.pallas_call(functools.partial(step_kernel, step=step, turn=turn, count...  30.7 us
    pallas_call x1, Pallas kernels, layer(): pl.pallas_call(functools.partial(last_kernel, step=forward_steps, count=c...  5.76 us
    pallas_call x1, Pallas kernels, layer(): pl.pallas_call(functools.partial(first_kernel, q_heads=q_heads, kv_heads=...  2.87 us
  transfers between devices with their start and end apart: 20, of which 7 were waited for; matrix products, arithmetic and copies ran while one was open for 0% of the time, Pallas kernels for 24%

profile of v4, /device:TPU:1486, one launch (start us, length us, event | category | flops | bytes accessed | tf_op | source)
XLA Modules:
  0.0 138.7 jit_solution(1305437105135348488)
XLA Ops:
  1.1 5.1 %collective-permute-start = (bf16[192,1024]{1,0:T(8,128)(2,1)S(1)}, bf16[192,1024]{1,0:T(8,128)(2,1)S(1)}, u32[]{:S(2)}, u32[]{:S(2)}) collective-permute-start(bf16[192,1024]{1,0:T(8,128)(2,1)S(1)} %pad_maximum_fusion.own_ref), channel_id=1, source_target_pairs={{0,16},{16,32},{32,48},{48,64},{64,80},{80,96},{96,112},{112,128},... | collective-permute-start | bytes 1179656 | tf_op jit(solution)/shard_map/ppermute | solution.py:170
  6.2 8.4 %collective-permute-done.f_ref = bf16[192,1024]{1,0:T(8,128)(2,1)S(1)} collective-permute-done((bf16[192,1024]{1,0:T(8,128)(2,1)S(1)}, bf16[192,1024]{1,0:T(8,128)(2,1)S(1)}, u32[]{:S(2)}, u32[]{:S(2)}) %collective-permute-start) | collective-permute-done | bytes 393248 | tf_op jit(solution)/shard_map/ppermute | solution.py:170
  14.6 5.6 %collective-permute-start.1 = (bf16[192,1024]{1,0:T(8,128)(2,1)S(1)}, bf16[192,1024]{1,0:T(8,128)(2,1)S(1)}, u32[]{:S(2)}, u32[]{:S(2)}) collective-permute-start(bf16[192,1024]{1,0:T(8,128)(2,1)S(1)} %collective-permute-done.f_ref), channel_id=1, source_target_pairs={{16,32},{32,48},{48,64},{64,80},{80,96},{96,112},{112,128},{128,14... | collective-permute-start | bytes 1179656 | tf_op jit(solution)/shard_map/ppermute | solution.py:170
  20.3 7.6 %collective-permute-done.1.f_ref = bf16[192,1024]{1,0:T(8,128)(2,1)S(1)} collective-permute-done((bf16[192,1024]{1,0:T(8,128)(2,1)S(1)}, bf16[192,1024]{1,0:T(8,128)(2,1)S(1)}, u32[]{:S(2)}, u32[]{:S(2)}) %collective-permute-start.1) | collective-permute-done | bytes 393248 | tf_op jit(solution)/shard_map/ppermute | solution.py:170
  27.8 5.6 %collective-permute-start.2 = (bf16[192,1024]{1,0:T(8,128)(2,1)S(1)}, bf16[192,1024]{1,0:T(8,128)(2,1)S(1)}, u32[]{:S(2)}, u32[]{:S(2)}) collective-permute-start(bf16[192,1024]{1,0:T(8,128)(2,1)S(1)} %collective-permute-done.1.f_ref), channel_id=1, source_target_pairs={{32,48},{48,64},{64,80},{80,96},{96,112},{112,128},{128,144},{144,... | collective-permute-start | bytes 1179656 | tf_op jit(solution)/shard_map/ppermute | solution.py:170
  34.9 5.3 %collective-permute-done.2.f_ref = bf16[192,1024]{1,0:T(8,128)(2,1)S(1)} collective-permute-done((bf16[192,1024]{1,0:T(8,128)(2,1)S(1)}, bf16[192,1024]{1,0:T(8,128)(2,1)S(1)}, u32[]{:S(2)}, u32[]{:S(2)}) %collective-permute-start.2) | collective-permute-done | bytes 393248 | tf_op jit(solution)/shard_map/ppermute | solution.py:170
  40.2 5.6 %collective-permute-start.3 = (bf16[192,1024]{1,0:T(8,128)(2,1)S(1)}, bf16[192,1024]{1,0:T(8,128)(2,1)S(1)}, u32[]{:S(2)}, u32[]{:S(2)}) collective-permute-start(bf16[192,1024]{1,0:T(8,128)(2,1)S(1)} %collective-permute-done.2.f_ref), channel_id=1, source_target_pairs={{48,64},{64,80},{80,96},{96,112},{112,128},{128,144},{144,160},{16... | collective-permute-start | bytes 1179656 | tf_op jit(solution)/shard_map/ppermute | solution.py:170
  47.2 4.5 %collective-permute-done.3.f_ref = bf16[192,1024]{1,0:T(8,128)(2,1)S(1)} collective-permute-done((bf16[192,1024]{1,0:T(8,128)(2,1)S(1)}, bf16[192,1024]{1,0:T(8,128)(2,1)S(1)}, u32[]{:S(2)}, u32[]{:S(2)}) %collective-permute-start.3) | collective-permute-done | bytes 393248 | tf_op jit(solution)/shard_map/ppermute | solution.py:170
  51.6 5.6 %collective-permute-start.4 = (bf16[192,1024]{1,0:T(8,128)(2,1)S(1)}, bf16[192,1024]{1,0:T(8,128)(2,1)S(1)}, u32[]{:S(2)}, u32[]{:S(2)}) collective-permute-start(bf16[192,1024]{1,0:T(8,128)(2,1)S(1)} %collective-permute-done.3.f_ref), channel_id=1, source_target_pairs={{64,80},{80,96},{96,112},{112,128},{128,144},{144,160},{160,176},{... | collective-permute-start | bytes 1179656 | tf_op jit(solution)/shard_map/ppermute | solution.py:170
  58.9 3.7 %collective-permute-done.4.f_ref = bf16[192,1024]{1,0:T(8,128)(2,1)S(1)} collective-permute-done((bf16[192,1024]{1,0:T(8,128)(2,1)S(1)}, bf16[192,1024]{1,0:T(8,128)(2,1)S(1)}, u32[]{:S(2)}, u32[]{:S(2)}) %collective-permute-start.4) | collective-permute-done | bytes 393248 | tf_op jit(solution)/shard_map/ppermute | solution.py:170
  62.5 5.6 %collective-permute-start.5 = (bf16[192,1024]{1,0:T(8,128)(2,1)S(1)}, bf16[192,1024]{1,0:T(8,128)(2,1)S(1)}, u32[]{:S(2)}, u32[]{:S(2)}) collective-permute-start(bf16[192,1024]{1,0:T(8,128)(2,1)S(1)} %collective-permute-done.4.f_ref), channel_id=1, source_target_pairs={{80,96},{96,112},{112,128},{128,144},{144,160},{160,176},{176,192}... | collective-permute-start | bytes 1179656 | tf_op jit(solution)/shard_map/ppermute | solution.py:170
  69.6 3.9 %collective-permute-done.5.f_ref = bf16[192,1024]{1,0:T(8,128)(2,1)S(1)} collective-permute-done((bf16[192,1024]{1,0:T(8,128)(2,1)S(1)}, bf16[192,1024]{1,0:T(8,128)(2,1)S(1)}, u32[]{:S(2)}, u32[]{:S(2)}) %collective-permute-start.5) | collective-permute-done | bytes 393248 | tf_op jit(solution)/shard_map/ppermute | solution.py:170
  73.5 5.6 %collective-permute-start.6 = (bf16[192,1024]{1,0:T(8,128)(2,1)S(1)}, bf16[192,1024]{1,0:T(8,128)(2,1)S(1)}, u32[]{:S(2)}, u32[]{:S(2)}) collective-permute-start(bf16[192,1024]{1,0:T(8,128)(2,1)S(1)} %collective-permute-done.5.f_ref), channel_id=1, source_target_pairs={{96,112},{112,128},{128,144},{144,160},{160,176},{176,192},{192,20... | collective-permute-start | bytes 1179656 | tf_op jit(solution)/shard_map/ppermute | solution.py:170
  81.2 4.4 %collective-permute-done.6.f_ref = bf16[192,1024]{1,0:T(8,128)(2,1)S(1)} collective-permute-done((bf16[192,1024]{1,0:T(8,128)(2,1)S(1)}, bf16[192,1024]{1,0:T(8,128)(2,1)S(1)}, u32[]{:S(2)}, u32[]{:S(2)}) %collective-permute-start.6) | collective-permute-done | bytes 393248 | tf_op jit(solution)/shard_map/ppermute | solution.py:170
  85.7 5.6 %collective-permute-start.7 = (bf16[192,1024]{1,0:T(8,128)(2,1)S(1)}, bf16[192,1024]{1,0:T(8,128)(2,1)S(1)}, u32[]{:S(2)}, u32[]{:S(2)}) collective-permute-start(bf16[192,1024]{1,0:T(8,128)(2,1)S(1)} %collective-permute-done.6.f_ref), channel_id=1, source_target_pairs={{112,128},{128,144},{144,160},{160,176},{176,192},{192,208},{208,2... | collective-permute-start | bytes 1179656 | tf_op jit(solution)/shard_map/ppermute | solution.py:170
  96.9 3.5 %shard_map.60 = (f32[28,192,128]{2,1,0:T(8,128)S(1)}, f32[28,192,128]{2,1,0:T(8,128)S(1)}, f32[28,192,128]{2,1,0:T(8,128)S(1)}) custom-call(s32[1]{0:T(128)} %bitcast._place.place_ref, bf16[192,3584]{1,0:T(8,128)(2,1)S(1)} %get-tuple-element.34.q_ref, ...), custom_call_target="tpu_custom_call", output_to_operand_aliasing={{0}: (3, {}), {1}: (4, {}), {2}: (5, {})} | custom-call | flops 528482304 | bytes 2752512 | tf_op jit(solution)/shard_map/pallas_call | solution.py:228
  100.4 4.5 %shard_map.61 = (f32[28,192,128]{2,1,0:T(8,128)S(1)}, f32[28,192,128]{2,1,0:T(8,128)S(1)}, f32[28,192,128]{2,1,0:T(8,128)S(1)}) custom-call(s32[1]{0:T(128)} %bitcast._place.place_ref, bf16[192,3584]{1,0:T(8,128)(2,1)S(1)} %get-tuple-element.34.q_ref, ...), custom_call_target="tpu_custom_call", output_to_operand_aliasing={{0}: (4, {}), {1}: (5, {}), {2}: (6, {})} | custom-call | flops 1056964608 | bytes 2752512 | tf_op jit(solution)/shard_map/pallas_call | solution.py:228
  104.9 3.5 %shard_map.62 = (f32[28,192,128]{2,1,0:T(8,128)S(1)}, f32[28,192,128]{2,1,0:T(8,128)S(1)}, f32[28,192,128]{2,1,0:T(8,128)S(1)}) custom-call(s32[1]{0:T(128)} %bitcast._place.place_ref, bf16[192,3584]{1,0:T(8,128)(2,1)S(1)} %get-tuple-element.34.q_ref, ...), custom_call_target="tpu_custom_call", output_to_operand_aliasing={{0}: (3, {}), {1}: (4, {}), {2}: (5, {})} | custom-call | flops 528482304 | bytes 2752512 | tf_op jit(solution)/shard_map/pallas_call | solution.py:228
  108.4 3.5 %shard_map.63 = (f32[28,192,128]{2,1,0:T(8,128)S(1)}, f32[28,192,128]{2,1,0:T(8,128)S(1)}, f32[28,192,128]{2,1,0:T(8,128)S(1)}) custom-call(s32[1]{0:T(128)} %bitcast._place.place_ref, bf16[192,3584]{1,0:T(8,128)(2,1)S(1)} %get-tuple-element.34.q_ref, ...), custom_call_target="tpu_custom_call", output_to_operand_aliasing={{0}: (4, {}), {1}: (5, {}), {2}: (6, {})} | custom-call | flops 1056964608 | bytes 2752512 | tf_op jit(solution)/shard_map/pallas_call | solution.py:228
  111.9 5.1 %collective-permute-start.8 = (bf16[192,1024]{1,0:T(8,128)(2,1)S(1)}, bf16[192,1024]{1,0:T(8,128)(2,1)S(1)}, u32[]{:S(2)}, u32[]{:S(2)}) collective-permute-start(bf16[192,1024]{1,0:T(8,128)(2,1)S(1)} %collective-permute-done.7.f_ref), channel_id=1, source_target_pairs={{128,144},{144,160},{160,176},{176,192},{192,208},{208,224},{224,2... | collective-permute-start | bytes 1179656 | tf_op jit(solution)/shard_map/ppermute | solution.py:170
  120.6 3.7 %shard_map.65 = (f32[28,192,128]{2,1,0:T(8,128)S(1)}, f32[28,192,128]{2,1,0:T(8,128)S(1)}, f32[28,192,128]{2,1,0:T(8,128)S(1)}) custom-call(s32[1]{0:T(128)} %bitcast._place.place_ref, bf16[192,3584]{1,0:T(8,128)(2,1)S(1)} %get-tuple-element.34.q_ref, ...), custom_call_target="tpu_custom_call", output_to_operand_aliasing={{0}: (4, {}), {1}: (5, {}), {2}: (6, {})} | custom-call | flops 1056964608 | bytes 2752512 | tf_op jit(solution)/shard_map/pallas_call | solution.py:228
  124.3 4.3 %shard_map.66 = (f32[28,192,128]{2,1,0:T(8,128)S(1)}, f32[28,192,128]{2,1,0:T(8,128)S(1)}, f32[28,192,128]{2,1,0:T(8,128)S(1)}) custom-call(s32[1]{0:T(128)} %bitcast._place.place_ref, bf16[192,3584]{1,0:T(8,128)(2,1)S(1)} %get-tuple-element.34.q_ref, ...), custom_call_target="tpu_custom_call", output_to_operand_aliasing={{0}: (4, {}), {1}: (5, {}), {2}: (6, {})} | custom-call | flops 1056964608 | bytes 2752512 | tf_op jit(solution)/shard_map/pallas_call | solution.py:228
  128.6 4.3 %shard_map.67 = (f32[28,192,128]{2,1,0:T(8,128)S(1)}, f32[28,192,128]{2,1,0:T(8,128)S(1)}, f32[28,192,128]{2,1,0:T(8,128)S(1)}) custom-call(s32[1]{0:T(128)} %bitcast._place.place_ref, bf16[192,3584]{1,0:T(8,128)(2,1)S(1)} %get-tuple-element.34.q_ref, ...), custom_call_target="tpu_custom_call", output_to_operand_aliasing={{0}: (4, {}), {1}: (5, {}), {2}: (6, {})} | custom-call | flops 1056964608 | bytes 2752512 | tf_op jit(solution)/shard_map/pallas_call | solution.py:228
  132.9 5.8 %last.1 = (f32[28,192,128]{2,1,0:T(8,128)S(1)}, f32[28,192,128]{2,1,0:T(8,128)S(1)}, f32[28,192,128]{2,1,0:T(8,128)S(1)}, bf16[192,3584]{1,0:T(8,128)(2,1)}) custom-call(s32[1]{0:T(128)} %bitcast._place.place_ref, bf16[192,3584]{1,0:T(8,128)(2,1)S(1)} %get-tuple-element.34.q_ref, ...), custom_call_target="tpu_custom_call", output_to_operand_aliasing={{0}: (5, {}), {1}: (6, {}), {2}: (7, {})} | custom-call | flops 528482304 | bytes 2752512 | tf_op jit(solution)/shard_map/last/pallas_call | solution.py:239
  (39 shorter events, 18.0 us)
Async XLA Ops:
  0.0 92.0 %copy-start.2 = (f32[3584]{0:T(1024)S(1)}, f32[3584]{0:T(1024)}, u32[]{:S(2)}) copy-start(f32[3584]{0:T(1024)} %param.9) | copy-start | bytes 43012
  1.1 13.6 %collective-permute-start = (bf16[192,1024]{1,0:T(8,128)(2,1)S(1)}, bf16[192,1024]{1,0:T(8,128)(2,1)S(1)}, u32[]{:S(2)}, u32[]{:S(2)}) collective-permute-start(bf16[192,1024]{1,0:T(8,128)(2,1)S(1)} %pad_maximum_fusion.own_ref), channel_id=1, source_target_pairs={{0,16},{16,32},{32,48},{48,64},{64,80},{80,96},{96,112},{112,128},... | collective-permute-start | bytes 1179656 | tf_op jit(solution)/shard_map/ppermute | solution.py:170
  14.6 13.2 %collective-permute-start.1 = (bf16[192,1024]{1,0:T(8,128)(2,1)S(1)}, bf16[192,1024]{1,0:T(8,128)(2,1)S(1)}, u32[]{:S(2)}, u32[]{:S(2)}) collective-permute-start(bf16[192,1024]{1,0:T(8,128)(2,1)S(1)} %collective-permute-done.f_ref), channel_id=1, source_target_pairs={{16,32},{32,48},{48,64},{64,80},{80,96},{96,112},{112,128},{128,14... | collective-permute-start | bytes 1179656 | tf_op jit(solution)/shard_map/ppermute | solution.py:170
  27.8 12.3 %collective-permute-start.2 = (bf16[192,1024]{1,0:T(8,128)(2,1)S(1)}, bf16[192,1024]{1,0:T(8,128)(2,1)S(1)}, u32[]{:S(2)}, u32[]{:S(2)}) collective-permute-start(bf16[192,1024]{1,0:T(8,128)(2,1)S(1)} %collective-permute-done.1.f_ref), channel_id=1, source_target_pairs={{32,48},{48,64},{64,80},{80,96},{96,112},{112,128},{128,144},{144,... | collective-permute-start | bytes 1179656 | tf_op jit(solution)/shard_map/ppermute | solution.py:170
  33.5 13.0 %collective-permute-start.14 = (bf16[192,1024]{1,0:T(8,128)(2,1)S(1)}, bf16[192,1024]{1,0:T(8,128)(2,1)}, u32[]{:S(2)}, u32[]{:S(2)}) collective-permute-start(bf16[192,1024]{1,0:T(8,128)(2,1)S(1)} %pad_maximum_fusion.own_ref), channel_id=1, source_target_pairs={{0,240},{1,241},{2,242},{3,243},{4,244},{5,245},{6,246},{7,247},{8... | collective-permute-start | bytes 1179656 | tf_op jit(solution)/shard_map/ppermute | solution.py:170
  40.2 11.5 %collective-permute-start.3 = (bf16[192,1024]{1,0:T(8,128)(2,1)S(1)}, bf16[192,1024]{1,0:T(8,128)(2,1)S(1)}, u32[]{:S(2)}, u32[]{:S(2)}) collective-permute-start(bf16[192,1024]{1,0:T(8,128)(2,1)S(1)} %collective-permute-done.2.f_ref), channel_id=1, source_target_pairs={{48,64},{64,80},{80,96},{96,112},{112,128},{128,144},{144,160},{16... | collective-permute-start | bytes 1179656 | tf_op jit(solution)/shard_map/ppermute | solution.py:170
  45.8 12.2 %collective-permute-start.13 = (bf16[192,1024]{1,0:T(8,128)(2,1)S(1)}, bf16[192,1024]{1,0:T(8,128)(2,1)S(1)}, u32[]{:S(2)}, u32[]{:S(2)}) collective-permute-start(bf16[192,1024]{1,0:T(8,128)(2,1)S(1)} %pad_maximum_fusion.own_ref), channel_id=1, source_target_pairs={{16,240},{17,241},{18,242},{19,243},{20,244},{21,245},{22,246},{23... | collective-permute-start | bytes 1179656 | tf_op jit(solution)/shard_map/ppermute | solution.py:170
  46.5 11.5 %collective-permute-start.15 = (bf16[192,1024]{1,0:T(8,128)(2,1)}, bf16[192,1024]{1,0:T(8,128)(2,1)S(1)}, u32[]{:S(2)}, u32[]{:S(2)}) collective-permute-start(bf16[192,1024]{1,0:T(8,128)(2,1)} %collective-permute-done.14.refs_0_), channel_id=1, source_target_pairs={{240,224},{241,225},{242,226},{243,227},{244,228},{245,229},{246,2... | collective-permute-start | bytes 1179656 | tf_op jit(solution)/shard_map/ppermute | solution.py:170
  51.6 10.9 %collective-permute-start.4 = (bf16[192,1024]{1,0:T(8,128)(2,1)S(1)}, bf16[192,1024]{1,0:T(8,128)(2,1)S(1)}, u32[]{:S(2)}, u32[]{:S(2)}) collective-permute-start(bf16[192,1024]{1,0:T(8,128)(2,1)S(1)} %collective-permute-done.3.f_ref), channel_id=1, source_target_pairs={{64,80},{80,96},{96,112},{112,128},{128,144},{144,160},{160,176},{... | collective-permute-start | bytes 1179656 | tf_op jit(solution)/shard_map/ppermute | solution.py:170
  57.3 11.6 %collective-permute-start.12 = (bf16[192,1024]{1,0:T(8,128)(2,1)S(1)}, bf16[192,1024]{1,0:T(8,128)(2,1)S(1)}, u32[]{:S(2)}, u32[]{:S(2)}) collective-permute-start(bf16[192,1024]{1,0:T(8,128)(2,1)S(1)} %pad_maximum_fusion.own_ref), channel_id=1, source_target_pairs={{32,240},{33,241},{34,242},{35,243},{36,244},{37,245},{38,246},{39... | collective-permute-start | bytes 1179656 | tf_op jit(solution)/shard_map/ppermute | solution.py:170
  58.0 34.1 %copy-start.1 = (bf16[1,192,3584]{2,1,0:T(8,128)(2,1)S(1)}, bf16[1,192,3584]{2,1,0:T(8,128)(2,1)}, u32[]{:S(2)}) copy-start(bf16[1,192,3584]{2,1,0:T(8,128)(2,1)} %param.5) | copy-start | bytes 4128772
  58.0 10.8 %collective-permute-start.16 = (bf16[192,1024]{1,0:T(8,128)(2,1)S(1)}, bf16[192,1024]{1,0:T(8,128)(2,1)S(1)}, u32[]{:S(2)}, u32[]{:S(2)}) collective-permute-start(bf16[192,1024]{1,0:T(8,128)(2,1)S(1)} %shard_map.55.refs_0_), channel_id=1, source_target_pairs={{240,224},{224,208},{241,225},{225,209},{242,226},{226,210},{243,2... | collective-permute-start | bytes 1179656 | tf_op jit(solution)/shard_map/ppermute | solution.py:170
  62.5 11.0 %collective-permute-start.5 = (bf16[192,1024]{1,0:T(8,128)(2,1)S(1)}, bf16[192,1024]{1,0:T(8,128)(2,1)S(1)}, u32[]{:S(2)}, u32[]{:S(2)}) collective-permute-start(bf16[192,1024]{1,0:T(8,128)(2,1)S(1)} %collective-permute-done.4.f_ref), channel_id=1, source_target_pairs={{80,96},{96,112},{112,128},{128,144},{144,160},{160,176},{176,192}... | collective-permute-start | bytes 1179656 | tf_op jit(solution)/shard_map/ppermute | solution.py:170
  68.2 11.7 %collective-permute-start.11 = (bf16[192,1024]{1,0:T(8,128)(2,1)S(1)}, bf16[192,1024]{1,0:T(8,128)(2,1)S(1)}, u32[]{:S(2)}, u32[]{:S(2)}) collective-permute-start(bf16[192,1024]{1,0:T(8,128)(2,1)S(1)} %pad_maximum_fusion.own_ref), channel_id=1, source_target_pairs={{48,240},{49,241},{50,242},{51,243},{52,244},{53,245},{54,246},{55... | collective-permute-start | bytes 1179656 | tf_op jit(solution)/shard_map/ppermute | solution.py:170
  68.9 10.9 %collective-permute-start.17 = (bf16[192,1024]{1,0:T(8,128)(2,1)S(1)}, bf16[192,1024]{1,0:T(8,128)(2,1)S(1)}, u32[]{:S(2)}, u32[]{:S(2)}) collective-permute-start(bf16[192,1024]{1,0:T(8,128)(2,1)S(1)} %shard_map.56.refs_0_), channel_id=1, source_target_pairs={{240,224},{224,208},{208,192},{241,225},{225,209},{209,193},{242,2... | collective-permute-start | bytes 1179656 | tf_op jit(solution)/shard_map/ppermute | solution.py:170
  73.5 12.1 %collective-permute-start.6 = (bf16[192,1024]{1,0:T(8,128)(2,1)S(1)}, bf16[192,1024]{1,0:T(8,128)(2,1)S(1)}, u32[]{:S(2)}, u32[]{:S(2)}) collective-permute-start(bf16[192,1024]{1,0:T(8,128)(2,1)S(1)} %collective-permute-done.5.f_ref), channel_id=1, source_target_pairs={{96,112},{112,128},{128,144},{144,160},{160,176},{176,192},{192,20... | collective-permute-start | bytes 1179656 | tf_op jit(solution)/shard_map/ppermute | solution.py:170
  79.2 15.8 %collective-permute-start.10 = (bf16[192,1024]{1,0:T(8,128)(2,1)S(1)}, bf16[192,1024]{1,0:T(8,128)(2,1)S(1)}, u32[]{:S(2)}, u32[]{:S(2)}) collective-permute-start(bf16[192,1024]{1,0:T(8,128)(2,1)S(1)} %pad_maximum_fusion.own_ref), channel_id=1, source_target_pairs={{64,240},{65,241},{66,242},{67,243},{68,244},{69,245},{70,246},{71... | collective-permute-start | bytes 1179656 | tf_op jit(solution)/shard_map/ppermute | solution.py:170
  79.9 15.0 %collective-permute-start.18 = (bf16[192,1024]{1,0:T(8,128)(2,1)S(1)}, bf16[192,1024]{1,0:T(8,128)(2,1)S(1)}, u32[]{:S(2)}, u32[]{:S(2)}) collective-permute-start(bf16[192,1024]{1,0:T(8,128)(2,1)S(1)} %shard_map.57.refs_0_), channel_id=1, source_target_pairs={{240,224},{224,208},{208,192},{192,176},{241,225},{225,209},{209,1... | collective-permute-start | bytes 1179656 | tf_op jit(solution)/shard_map/ppermute | solution.py:170
  85.7 26.2 %collective-permute-start.7 = (bf16[192,1024]{1,0:T(8,128)(2,1)S(1)}, bf16[192,1024]{1,0:T(8,128)(2,1)S(1)}, u32[]{:S(2)}, u32[]{:S(2)}) collective-permute-start(bf16[192,1024]{1,0:T(8,128)(2,1)S(1)} %collective-permute-done.6.f_ref), channel_id=1, source_target_pairs={{112,128},{128,144},{144,160},{160,176},{176,192},{192,208},{208,2... | collective-permute-start | bytes 1179656 | tf_op jit(solution)/shard_map/ppermute | solution.py:170
  91.3 29.2 %collective-permute-start.9 = (bf16[192,1024]{1,0:T(8,128)(2,1)S(1)}, bf16[192,1024]{1,0:T(8,128)(2,1)S(1)}, u32[]{:S(2)}, u32[]{:S(2)}) collective-permute-start(bf16[192,1024]{1,0:T(8,128)(2,1)S(1)} %pad_maximum_fusion.own_ref), channel_id=1, source_target_pairs={{80,240},{81,241},{82,242},{83,243},{84,244},{85,245},{86,246},{87... | collective-permute-start | bytes 1179656 | tf_op jit(solution)/shard_map/ppermute | solution.py:170
  95.0 25.6 %collective-permute-start.19 = (bf16[192,1024]{1,0:T(8,128)(2,1)S(1)}, bf16[192,1024]{1,0:T(8,128)(2,1)S(1)}, u32[]{:S(2)}, u32[]{:S(2)}) collective-permute-start(bf16[192,1024]{1,0:T(8,128)(2,1)S(1)} %shard_map.58.refs_0_), channel_id=1, source_target_pairs={{240,224},{224,208},{208,192},{192,176},{176,160},{241,225},{225,2... | collective-permute-start | bytes 1179656 | tf_op jit(solution)/shard_map/ppermute | solution.py:170
  111.9 21.0 %collective-permute-start.8 = (bf16[192,1024]{1,0:T(8,128)(2,1)S(1)}, bf16[192,1024]{1,0:T(8,128)(2,1)S(1)}, u32[]{:S(2)}, u32[]{:S(2)}) collective-permute-start(bf16[192,1024]{1,0:T(8,128)(2,1)S(1)} %collective-permute-done.7.f_ref), channel_id=1, source_target_pairs={{128,144},{144,160},{160,176},{176,192},{192,208},{208,224},{224,2... | collective-permute-start | bytes 1179656 | tf_op jit(solution)/shard_map/ppermute | solution.py:170
  128.6 4.4 %copy-start = (bf16[1,192,3584]{2,1,0:T(8,128)(2,1)S(1)}, bf16[1,192,3584]{2,1,0:T(8,128)(2,1)}, u32[]{:S(2)}) copy-start(bf16[1,192,3584]{2,1,0:T(8,128)(2,1)} %param.8) | copy-start | bytes 4128772

commit v5 on v4

--- a/solution.py
+++ b/solution.py
@@ -34,7 +34,7 @@
     return part
 
 
-def each_head(q_ref, keys, values, acc_ref, total_ref, top_ref, q_heads, kv_heads, first):
+def each_head(q_ref, keys, values, acc_ref, total_ref, top_ref, q_heads, kv_heads, first, finish=None):
     per_group = q_heads // kv_heads
 
     def column(ref, start, group):
@@ -62,15 +62,22 @@
             else:
                 top = jnp.maximum(top_ref[head], top_here)
                 fade = jnp.exp2(top_ref[head] - top)
-            top_ref[head] = top
+            if finish is None:
+                top_ref[head] = top
             return jnp.exp2(scores * SCALE - lanes(top, width)), fade
 
         def add(i, weights, fade):
             head = group * per_group + i
             acc = jnp.dot(weights.astype(jnp.bfloat16), value, preferred_element_type=jnp.float32)
             total = lane_sums(weights)
-            acc_ref[head] = acc if first else acc_ref[head] * fade + acc
-            total_ref[head] = total if first else total_ref[head] * fade + total
+            if not first:
+                acc = acc_ref[head] * fade + acc
+                total = total_ref[head] * fade + total
+            if finish is None:
+                acc_ref[head] = acc
+                total_ref[head] = total
+            else:
+                finish(head, acc, total)
 
         scores = [score(0), score(1)]
         waiting = None
@@ -127,23 +134,36 @@
     )
 
 
-def last_kernel(place_ref, q_ref, f_ref, residual_ref, gain_ref, *refs, step, count, q_heads, kv_heads):
-    acc_ref, total_ref, top_ref, out_ref = refs[-4:]
-    fold(
-        place_ref[0], step, None, count, f_ref, None,
-        lambda keys, values: each_head(
-            q_ref, keys, values, acc_ref, total_ref, top_ref, q_heads, kv_heads, False
-        ),
-    )
+def last_kernel(place_ref, q_ref, f_ref, residual_ref, gain_ref, *refs, step, q_heads, kv_heads):
+    acc_ref, total_ref, top_ref, out_ref, square_ref = refs[-5:]
     rows, width = out_ref.shape
-    square = jnp.zeros((rows, HEAD_WIDTH), jnp.float32)
-    for head in range(q_heads):
-        at = slice(head * HEAD_WIDTH, (head + 1) * HEAD_WIDTH)
-        total = jnp.sum(total_ref[head], axis=1, keepdims=True)
-        attended = (acc_ref[head] / total).astype(jnp.bfloat16).astype(jnp.float32)
+    square_ref[...] = jnp.zeros(square_ref.shape, jnp.float32)
+
+    def finish(head, acc, total):
+        attended = (acc / jnp.sum(total, axis=1, keepdims=True)).astype(jnp.bfloat16).astype(jnp.float32)
+        at = pl.ds(pl.multiple_of(head * HEAD_WIDTH, HEAD_WIDTH), HEAD_WIDTH)
         hidden = residual_ref[:, at].astype(jnp.float32) + attended
         acc_ref[head] = hidden
-        square = square + hidden * hidden
+        square_ref[...] = square_ref[...] + hidden * hidden
+
+    wide = f_ref.shape[1] // 2
+    behind = place_ref[0] >= step
+
+    @pl.when(behind)
+    def _():
+        each_head(
+            q_ref, ((f_ref, 0),), ((f_ref, wide),), acc_ref, total_ref, top_ref, q_heads, kv_heads, False, finish
+        )
+
+    @pl.when(jnp.logical_not(behind))
+    def _():
+        def one_head(head, carry):
+            finish(head, acc_ref[head], total_ref[head])
+            return carry
+
+        lax.fori_loop(0, q_heads, one_head, 0)
+
+    square = square_ref[...]
     inv_rms = lax.rsqrt(jnp.sum(square, axis=1, keepdims=True) / width + NORM_EPS)
     inv_rms = jnp.broadcast_to(inv_rms, (rows, HEAD_WIDTH))
     for head in range(q_heads):
@@ -237,10 +257,11 @@
             cost_estimate=cost(len(blocks) * rows),
         )(place, query, *blocks, acc, total, top)
     _, _, _, normed = pl.pallas_call(
-        functools.partial(last_kernel, step=forward_steps, count=count, q_heads=q_heads, kv_heads=kv_heads),
+        functools.partial(last_kernel, step=forward_steps, q_heads=q_heads, kv_heads=kv_heads),
         out_shape=(state, state, state, jax.ShapeDtypeStruct((rows, width), jnp.bfloat16)),
         in_specs=[smem] + [vmem] * 7,
         out_specs=(vmem, vmem, vmem, vmem),
+        scratch_shapes=[pltpu.VMEM((rows, HEAD_WIDTH), jnp.float32)],
         input_output_aliases={5: 0, 6: 1, 7: 2},
         compiler_params=params,
         cost_estimate=cost(rows),

time: 139 us -> 141 us (1.014)
  the two profiles are of different devices: /device:TPU:1486 before, /device:TPU:712 now
where the time goes in v5:
time: 141 us; the launch traced here: 140 us
  starting transfers between devices  78.2 us (55%)
  waiting for transfers between devices  33.2 us (24%)
  Pallas kernels  26.3 us (19%)
    ppermute x20, starting transfers between devices, shift(): return lax.ppermute(array, 'seq', pairs)  78.2 us
    ppermute x20, waiting for transfers between devices, shift(): return lax.ppermute(array, 'seq', pairs)  33.2 us
    pallas_call x8, Pallas kernels, layer(): pl.pallas_call(functools.partial(step_kernel, step=step, turn=turn, count...  18.6 us
    pallas_call x1, Pallas kernels, layer(): pl.pallas_call(functools.partial(last_kernel, step=forward_steps, q_heads...  4.66 us
    pallas_call x1, Pallas kernels, layer(): pl.pallas_call(functools.partial(first_kernel, q_heads=q_heads, kv_heads=...  2.86 us
  transfers between devices with their start and end apart: 20, of which 6 were waited for; matrix products, arithmetic and copies ran while one was open for 0% of the time, Pallas kernels for 15%

profile of v5, /device:TPU:712, one launch (start us, length us, event | category | flops | bytes accessed | tf_op | source)
XLA Modules:
  0.0 140.5 jit_solution(11891069567717969840)
XLA Ops:
  0.0 1.1 pad_maximum_fusion.own_ref
  1.1 6.0 %collective-permute-start = (bf16[192,1024]{1,0:T(8,128)(2,1)S(1)}, bf16[192,1024]{1,0:T(8,128)(2,1)S(1)}, u32[]{:S(2)}, u32[]{:S(2)}) collective-permute-start(bf16[192,1024]{1,0:T(8,128)(2,1)S(1)} %pad_maximum_fusion.own_ref), channel_id=1, source_target_pairs={{0,16},{16,32},{32,48},{48,64},{64,80},{80,96},{96,112},{112,128},... | collective-permute-start | bytes 1179656 | tf_op jit(solution)/shard_map/ppermute | solution.py:190
  7.1 8.4 %collective-permute-done.f_ref = bf16[192,1024]{1,0:T(8,128)(2,1)S(1)} collective-permute-done((bf16[192,1024]{1,0:T(8,128)(2,1)S(1)}, bf16[192,1024]{1,0:T(8,128)(2,1)S(1)}, u32[]{:S(2)}, u32[]{:S(2)}) %collective-permute-start) | collective-permute-done | bytes 393248 | tf_op jit(solution)/shard_map/ppermute | solution.py:190
  15.5 6.0 %collective-permute-start.1 = (bf16[192,1024]{1,0:T(8,128)(2,1)S(1)}, bf16[192,1024]{1,0:T(8,128)(2,1)S(1)}, u32[]{:S(2)}, u32[]{:S(2)}) collective-permute-start(bf16[192,1024]{1,0:T(8,128)(2,1)S(1)} %collective-permute-done.f_ref), channel_id=1, source_target_pairs={{16,32},{32,48},{48,64},{64,80},{80,96},{96,112},{112,128},{128,14... | collective-permute-start | bytes 1179656 | tf_op jit(solution)/shard_map/ppermute | solution.py:190
  21.6 7.6 %collective-permute-done.1.f_ref = bf16[192,1024]{1,0:T(8,128)(2,1)S(1)} collective-permute-done((bf16[192,1024]{1,0:T(8,128)(2,1)S(1)}, bf16[192,1024]{1,0:T(8,128)(2,1)S(1)}, u32[]{:S(2)}, u32[]{:S(2)}) %collective-permute-start.1) | collective-permute-done | bytes 393248 | tf_op jit(solution)/shard_map/ppermute | solution.py:190
  29.1 7.2 %collective-permute-start.2 = (bf16[192,1024]{1,0:T(8,128)(2,1)S(1)}, bf16[192,1024]{1,0:T(8,128)(2,1)S(1)}, u32[]{:S(2)}, u32[]{:S(2)}) collective-permute-start(bf16[192,1024]{1,0:T(8,128)(2,1)S(1)} %collective-permute-done.1.f_ref), channel_id=1, source_target_pairs={{32,48},{48,64},{64,80},{80,96},{96,112},{112,128},{128,144},{144,... | collective-permute-start | bytes 1179656 | tf_op jit(solution)/shard_map/ppermute | solution.py:190
  36.4 1.4 %collective-permute-start.14 = (bf16[192,1024]{1,0:T(8,128)(2,1)S(1)}, bf16[192,1024]{1,0:T(8,128)(2,1)}, u32[]{:S(2)}, u32[]{:S(2)}) collective-permute-start(bf16[192,1024]{1,0:T(8,128)(2,1)S(1)} %pad_maximum_fusion.own_ref), channel_id=1, source_target_pairs={{0,240},{1,241},{2,242},{3,243},{4,244},{5,245},{6,246},{7,247},{8... | collective-permute-start | bytes 1179656 | tf_op jit(solution)/shard_map/ppermute | solution.py:190
  37.8 5.3 %collective-permute-done.2.f_ref = bf16[192,1024]{1,0:T(8,128)(2,1)S(1)} collective-permute-done((bf16[192,1024]{1,0:T(8,128)(2,1)S(1)}, bf16[192,1024]{1,0:T(8,128)(2,1)S(1)}, u32[]{:S(2)}, u32[]{:S(2)}) %collective-permute-start.2) | collective-permute-done | bytes 393248 | tf_op jit(solution)/shard_map/ppermute | solution.py:190
  43.1 5.6 %collective-permute-start.3 = (bf16[192,1024]{1,0:T(8,128)(2,1)S(1)}, bf16[192,1024]{1,0:T(8,128)(2,1)S(1)}, u32[]{:S(2)}, u32[]{:S(2)}) collective-permute-start(bf16[192,1024]{1,0:T(8,128)(2,1)S(1)} %collective-permute-done.2.f_ref), channel_id=1, source_target_pairs={{48,64},{64,80},{80,96},{96,112},{112,128},{128,144},{144,160},{16... | collective-permute-start | bytes 1179656 | tf_op jit(solution)/shard_map/ppermute | solution.py:190
  50.1 4.5 %collective-permute-done.3.f_ref = bf16[192,1024]{1,0:T(8,128)(2,1)S(1)} collective-permute-done((bf16[192,1024]{1,0:T(8,128)(2,1)S(1)}, bf16[192,1024]{1,0:T(8,128)(2,1)S(1)}, u32[]{:S(2)}, u32[]{:S(2)}) %collective-permute-start.3) | collective-permute-done | bytes 393248 | tf_op jit(solution)/shard_map/ppermute | solution.py:190
  54.5 5.6 %collective-permute-start.4 = (bf16[192,1024]{1,0:T(8,128)(2,1)S(1)}, bf16[192,1024]{1,0:T(8,128)(2,1)S(1)}, u32[]{:S(2)}, u32[]{:S(2)}) collective-permute-start(bf16[192,1024]{1,0:T(8,128)(2,1)S(1)} %collective-permute-done.3.f_ref), channel_id=1, source_target_pairs={{64,80},{80,96},{96,112},{112,128},{128,144},{144,160},{160,176},{... | collective-permute-start | bytes 1179656 | tf_op jit(solution)/shard_map/ppermute | solution.py:190
  60.9 0.8 collective-permute-start.16
  61.8 3.7 %collective-permute-done.4.f_ref = bf16[192,1024]{1,0:T(8,128)(2,1)S(1)} collective-permute-done((bf16[192,1024]{1,0:T(8,128)(2,1)S(1)}, bf16[192,1024]{1,0:T(8,128)(2,1)S(1)}, u32[]{:S(2)}, u32[]{:S(2)}) %collective-permute-start.4) | collective-permute-done | bytes 393248 | tf_op jit(solution)/shard_map/ppermute | solution.py:190
  65.4 5.6 %collective-permute-start.5 = (bf16[192,1024]{1,0:T(8,128)(2,1)S(1)}, bf16[192,1024]{1,0:T(8,128)(2,1)S(1)}, u32[]{:S(2)}, u32[]{:S(2)}) collective-permute-start(bf16[192,1024]{1,0:T(8,128)(2,1)S(1)} %collective-permute-done.4.f_ref), channel_id=1, source_target_pairs={{80,96},{96,112},{112,128},{128,144},{144,160},{160,176},{176,192}... | collective-permute-start | bytes 1179656 | tf_op jit(solution)/shard_map/ppermute | solution.py:190
  72.5 3.8 %collective-permute-done.5.f_ref = bf16[192,1024]{1,0:T(8,128)(2,1)S(1)} collective-permute-done((bf16[192,1024]{1,0:T(8,128)(2,1)S(1)}, bf16[192,1024]{1,0:T(8,128)(2,1)S(1)}, u32[]{:S(2)}, u32[]{:S(2)}) %collective-permute-start.5) | collective-permute-done | bytes 393248 | tf_op jit(solution)/shard_map/ppermute | solution.py:190
  79.2 32.2 %collective-permute-start.9 = (bf16[192,1024]{1,0:T(8,128)(2,1)S(1)}, bf16[192,1024]{1,0:T(8,128)(2,1)S(1)}, u32[]{:S(2)}, u32[]{:S(2)}) collective-permute-start(bf16[192,1024]{1,0:T(8,128)(2,1)S(1)} %pad_maximum_fusion.own_ref), channel_id=1, source_target_pairs={{80,240},{81,241},{82,242},{83,243},{84,244},{85,245},{86,246},{87... | collective-permute-start | bytes 1179656 | tf_op jit(solution)/shard_map/ppermute | solution.py:190
  111.5 2.9 %first.1 = (bf16[192,3584]{1,0:T(8,128)(2,1)S(1)}, f32[28,192,128]{2,1,0:T(8,128)S(1)}, f32[28,192,128]{2,1,0:T(8,128)S(1)}, f32[28,192,128]{2,1,0:T(8,128)S(1)}) custom-call(s32[1]{0:T(128)} %bitcast._place.place_ref, bf16[192,3584]{1,0:T(8,128)(2,1)S(1)} %bitcast.7, bf16[192,1024]{1,0:T(8,128)(2,1)S(1)} %pad_maximum_fusion.own_ref), custom_call_target="tpu_custom_call" | custom-call | flops 528482304 | bytes 2752512 | tf_op jit(solution)/shard_map/first/pallas_call | solution.py:217
  115.1 3.5 %shard_map.60 = (f32[28,192,128]{2,1,0:T(8,128)S(1)}, f32[28,192,128]{2,1,0:T(8,128)S(1)}, f32[28,192,128]{2,1,0:T(8,128)S(1)}) custom-call(s32[1]{0:T(128)} %bitcast._place.place_ref, bf16[192,3584]{1,0:T(8,128)(2,1)S(1)} %get-tuple-element.34.q_ref, ...), custom_call_target="tpu_custom_call", output_to_operand_aliasing={{0}: (3, {}), {1}: (4, {}), {2}: (5, {})} | custom-call | flops 528482304 | bytes 2752512 | tf_op jit(solution)/shard_map/pallas_call | solution.py:248
  118.6 4.5 %shard_map.61 = (f32[28,192,128]{2,1,0:T(8,128)S(1)}, f32[28,192,128]{2,1,0:T(8,128)S(1)}, f32[28,192,128]{2,1,0:T(8,128)S(1)}) custom-call(s32[1]{0:T(128)} %bitcast._place.place_ref, bf16[192,3584]{1,0:T(8,128)(2,1)S(1)} %get-tuple-element.34.q_ref, ...), custom_call_target="tpu_custom_call", output_to_operand_aliasing={{0}: (4, {}), {1}: (5, {}), {2}: (6, {})} | custom-call | flops 1056964608 | bytes 2752512 | tf_op jit(solution)/shard_map/pallas_call | solution.py:248
  123.0 3.5 %shard_map.62 = (f32[28,192,128]{2,1,0:T(8,128)S(1)}, f32[28,192,128]{2,1,0:T(8,128)S(1)}, f32[28,192,128]{2,1,0:T(8,128)S(1)}) custom-call(s32[1]{0:T(128)} %bitcast._place.place_ref, bf16[192,3584]{1,0:T(8,128)(2,1)S(1)} %get-tuple-element.34.q_ref, ...), custom_call_target="tpu_custom_call", output_to_operand_aliasing={{0}: (3, {}), {1}: (4, {}), {2}: (5, {})} | custom-call | flops 528482304 | bytes 2752512 | tf_op jit(solution)/shard_map/pallas_call | solution.py:248
  126.5 3.5 %shard_map.63 = (f32[28,192,128]{2,1,0:T(8,128)S(1)}, f32[28,192,128]{2,1,0:T(8,128)S(1)}, f32[28,192,128]{2,1,0:T(8,128)S(1)}) custom-call(s32[1]{0:T(128)} %bitcast._place.place_ref, bf16[192,3584]{1,0:T(8,128)(2,1)S(1)} %get-tuple-element.34.q_ref, ...), custom_call_target="tpu_custom_call", output_to_operand_aliasing={{0}: (4, {}), {1}: (5, {}), {2}: (6, {})} | custom-call | flops 1056964608 | bytes 2752512 | tf_op jit(solution)/shard_map/pallas_call | solution.py:248
  130.7 3.5 %shard_map.64 = (f32[28,192,128]{2,1,0:T(8,128)S(1)}, f32[28,192,128]{2,1,0:T(8,128)S(1)}, f32[28,192,128]{2,1,0:T(8,128)S(1)}) custom-call(s32[1]{0:T(128)} %bitcast._place.place_ref, bf16[192,3584]{1,0:T(8,128)(2,1)S(1)} %get-tuple-element.34.q_ref, ...), custom_call_target="tpu_custom_call", output_to_operand_aliasing={{0}: (4, {}), {1}: (5, {}), {2}: (6, {})} | custom-call | flops 1056964608 | bytes 2752512 | tf_op jit(solution)/shard_map/pallas_call | solution.py:248
  134.5 1.3 copy-done
  135.8 4.7 %last.1 = (f32[28,192,128]{2,1,0:T(8,128)S(1)}, f32[28,192,128]{2,1,0:T(8,128)S(1)}, f32[28,192,128]{2,1,0:T(8,128)S(1)}, bf16[192,3584]{1,0:T(8,128)(2,1)}) custom-call(s32[1]{0:T(128)} %bitcast._place.place_ref, bf16[192,3584]{1,0:T(8,128)(2,1)S(1)} %get-tuple-element.34.q_ref, ...), custom_call_target="tpu_custom_call", output_to_operand_aliasing={{0}: (5, {}), {1}: (6, {}), {2}: (7, {})} | custom-call | flops 528482304 | bytes 2752512 | tf_op jit(solution)/shard_map/last/pallas_call | solution.py:259
  (39 shorter events, 8.0 us)
Async XLA Ops:
  0.0 111.4 %copy-start.2 = (f32[3584]{0:T(1024)S(1)}, f32[3584]{0:T(1024)}, u32[]{:S(2)}) copy-start(f32[3584]{0:T(1024)} %param.9) | copy-start | bytes 43012
  1.1 14.5 %collective-permute-start = (bf16[192,1024]{1,0:T(8,128)(2,1)S(1)}, bf16[192,1024]{1,0:T(8,128)(2,1)S(1)}, u32[]{:S(2)}, u32[]{:S(2)}) collective-permute-start(bf16[192,1024]{1,0:T(8,128)(2,1)S(1)} %pad_maximum_fusion.own_ref), channel_id=1, source_target_pairs={{0,16},{16,32},{32,48},{48,64},{64,80},{80,96},{96,112},{112,128},... | collective-permute-start | bytes 1179656 | tf_op jit(solution)/shard_map/ppermute | solution.py:190
  15.5 13.6 %collective-permute-start.1 = (bf16[192,1024]{1,0:T(8,128)(2,1)S(1)}, bf16[192,1024]{1,0:T(8,128)(2,1)S(1)}, u32[]{:S(2)}, u32[]{:S(2)}) collective-permute-start(bf16[192,1024]{1,0:T(8,128)(2,1)S(1)} %collective-permute-done.f_ref), channel_id=1, source_target_pairs={{16,32},{32,48},{48,64},{64,80},{80,96},{96,112},{112,128},{128,14... | collective-permute-start | bytes 1179656 | tf_op jit(solution)/shard_map/ppermute | solution.py:190
  29.1 13.9 %collective-permute-start.2 = (bf16[192,1024]{1,0:T(8,128)(2,1)S(1)}, bf16[192,1024]{1,0:T(8,128)(2,1)S(1)}, u32[]{:S(2)}, u32[]{:S(2)}) collective-permute-start(bf16[192,1024]{1,0:T(8,128)(2,1)S(1)} %collective-permute-done.1.f_ref), channel_id=1, source_target_pairs={{32,48},{48,64},{64,80},{80,96},{96,112},{112,128},{128,144},{144,... | collective-permute-start | bytes 1179656 | tf_op jit(solution)/shard_map/ppermute | solution.py:190
  36.4 13.0 %collective-permute-start.14 = (bf16[192,1024]{1,0:T(8,128)(2,1)S(1)}, bf16[192,1024]{1,0:T(8,128)(2,1)}, u32[]{:S(2)}, u32[]{:S(2)}) collective-permute-start(bf16[192,1024]{1,0:T(8,128)(2,1)S(1)} %pad_maximum_fusion.own_ref), channel_id=1, source_target_pairs={{0,240},{1,241},{2,242},{3,243},{4,244},{5,245},{6,246},{7,247},{8... | collective-permute-start | bytes 1179656 | tf_op jit(solution)/shard_map/ppermute | solution.py:190
  43.1 11.5 %collective-permute-start.3 = (bf16[192,1024]{1,0:T(8,128)(2,1)S(1)}, bf16[192,1024]{1,0:T(8,128)(2,1)S(1)}, u32[]{:S(2)}, u32[]{:S(2)}) collective-permute-start(bf16[192,1024]{1,0:T(8,128)(2,1)S(1)} %collective-permute-done.2.f_ref), channel_id=1, source_target_pairs={{48,64},{64,80},{80,96},{96,112},{112,128},{128,144},{144,160},{16... | collective-permute-start | bytes 1179656 | tf_op jit(solution)/shard_map/ppermute | solution.py:190
  48.7 12.2 %collective-permute-start.13 = (bf16[192,1024]{1,0:T(8,128)(2,1)S(1)}, bf16[192,1024]{1,0:T(8,128)(2,1)S(1)}, u32[]{:S(2)}, u32[]{:S(2)}) collective-permute-start(bf16[192,1024]{1,0:T(8,128)(2,1)S(1)} %pad_maximum_fusion.own_ref), channel_id=1, source_target_pairs={{16,240},{17,241},{18,242},{19,243},{20,244},{21,245},{22,246},{23... | collective-permute-start | bytes 1179656 | tf_op jit(solution)/shard_map/ppermute | solution.py:190
  49.4 11.5 %collective-permute-start.15 = (bf16[192,1024]{1,0:T(8,128)(2,1)}, bf16[192,1024]{1,0:T(8,128)(2,1)S(1)}, u32[]{:S(2)}, u32[]{:S(2)}) collective-permute-start(bf16[192,1024]{1,0:T(8,128)(2,1)} %collective-permute-done.14.refs_0_), channel_id=1, source_target_pairs={{240,224},{241,225},{242,226},{243,227},{244,228},{245,229},{246,2... | collective-permute-start | bytes 1179656 | tf_op jit(solution)/shard_map/ppermute | solution.py:190
  54.5 10.9 %collective-permute-start.4 = (bf16[192,1024]{1,0:T(8,128)(2,1)S(1)}, bf16[192,1024]{1,0:T(8,128)(2,1)S(1)}, u32[]{:S(2)}, u32[]{:S(2)}) collective-permute-start(bf16[192,1024]{1,0:T(8,128)(2,1)S(1)} %collective-permute-done.3.f_ref), channel_id=1, source_target_pairs={{64,80},{80,96},{96,112},{112,128},{128,144},{144,160},{160,176},{... | collective-permute-start | bytes 1179656 | tf_op jit(solution)/shard_map/ppermute | solution.py:190
  60.2 11.6 %collective-permute-start.12 = (bf16[192,1024]{1,0:T(8,128)(2,1)S(1)}, bf16[192,1024]{1,0:T(8,128)(2,1)S(1)}, u32[]{:S(2)}, u32[]{:S(2)}) collective-permute-start(bf16[192,1024]{1,0:T(8,128)(2,1)S(1)} %pad_maximum_fusion.own_ref), channel_id=1, source_target_pairs={{32,240},{33,241},{34,242},{35,243},{36,244},{37,245},{38,246},{39... | collective-permute-start | bytes 1179656 | tf_op jit(solution)/shard_map/ppermute | solution.py:190
  60.9 50.6 %copy-start.1 = (bf16[1,192,3584]{2,1,0:T(8,128)(2,1)S(1)}, bf16[1,192,3584]{2,1,0:T(8,128)(2,1)}, u32[]{:S(2)}) copy-start(bf16[1,192,3584]{2,1,0:T(8,128)(2,1)} %param.5) | copy-start | bytes 4128772
  60.9 10.9 %collective-permute-start.16 = (bf16[192,1024]{1,0:T(8,128)(2,1)S(1)}, bf16[192,1024]{1,0:T(8,128)(2,1)S(1)}, u32[]{:S(2)}, u32[]{:S(2)}) collective-permute-start(bf16[192,1024]{1,0:T(8,128)(2,1)S(1)} %shard_map.55.refs_0_), channel_id=1, source_target_pairs={{240,224},{224,208},{241,225},{225,209},{242,226},{226,210},{243,2... | collective-permute-start | bytes 1179656 | tf_op jit(solution)/shard_map/ppermute | solution.py:190
  65.4 10.9 %collective-permute-start.5 = (bf16[192,1024]{1,0:T(8,128)(2,1)S(1)}, bf16[192,1024]{1,0:T(8,128)(2,1)S(1)}, u32[]{:S(2)}, u32[]{:S(2)}) collective-permute-start(bf16[192,1024]{1,0:T(8,128)(2,1)S(1)} %collective-permute-done.4.f_ref), channel_id=1, source_target_pairs={{80,96},{96,112},{112,128},{128,144},{144,160},{160,176},{176,192}... | collective-permute-start | bytes 1179656 | tf_op jit(solution)/shard_map/ppermute | solution.py:190
  71.1 6.6 %collective-permute-start.11 = (bf16[192,1024]{1,0:T(8,128)(2,1)S(1)}, bf16[192,1024]{1,0:T(8,128)(2,1)S(1)}, u32[]{:S(2)}, u32[]{:S(2)}) collective-permute-start(bf16[192,1024]{1,0:T(8,128)(2,1)S(1)} %pad_maximum_fusion.own_ref), channel_id=1, source_target_pairs={{48,240},{49,241},{50,242},{51,243},{52,244},{53,245},{54,246},{55... | collective-permute-start | bytes 1179656 | tf_op jit(solution)/shard_map/ppermute | solution.py:190
  71.9 5.9 %collective-permute-start.17 = (bf16[192,1024]{1,0:T(8,128)(2,1)S(1)}, bf16[192,1024]{1,0:T(8,128)(2,1)S(1)}, u32[]{:S(2)}, u32[]{:S(2)}) collective-permute-start(bf16[192,1024]{1,0:T(8,128)(2,1)S(1)} %shard_map.56.refs_0_), channel_id=1, source_target_pairs={{240,224},{224,208},{208,192},{241,225},{225,209},{209,193},{242,2... | collective-permute-start | bytes 1179656 | tf_op jit(solution)/shard_map/ppermute | solution.py:190
  76.3 2.1 %collective-permute-start.6 = (bf16[192,1024]{1,0:T(8,128)(2,1)S(1)}, bf16[192,1024]{1,0:T(8,128)(2,1)S(1)}, u32[]{:S(2)}, u32[]{:S(2)}) collective-permute-start(bf16[192,1024]{1,0:T(8,128)(2,1)S(1)} %collective-permute-done.5.f_ref), channel_id=1, source_target_pairs={{96,112},{112,128},{128,144},{144,160},{160,176},{176,192},{192,20... | collective-permute-start | bytes 1179656 | tf_op jit(solution)/shard_map/ppermute | solution.py:190
  77.0 37.3 %collective-permute-start.10 = (bf16[192,1024]{1,0:T(8,128)(2,1)S(1)}, bf16[192,1024]{1,0:T(8,128)(2,1)S(1)}, u32[]{:S(2)}, u32[]{:S(2)}) collective-permute-start(bf16[192,1024]{1,0:T(8,128)(2,1)S(1)} %pad_maximum_fusion.own_ref), channel_id=1, source_target_pairs={{64,240},{65,241},{66,242},{67,243},{68,244},{69,245},{70,246},{71... | collective-permute-start | bytes 1179656 | tf_op jit(solution)/shard_map/ppermute | solution.py:190
  77.8 36.5 %collective-permute-start.18 = (bf16[192,1024]{1,0:T(8,128)(2,1)S(1)}, bf16[192,1024]{1,0:T(8,128)(2,1)S(1)}, u32[]{:S(2)}, u32[]{:S(2)}) collective-permute-start(bf16[192,1024]{1,0:T(8,128)(2,1)S(1)} %shard_map.57.refs_0_), channel_id=1, source_target_pairs={{240,224},{224,208},{208,192},{192,176},{241,225},{225,209},{209,1... | collective-permute-start | bytes 1179656 | tf_op jit(solution)/shard_map/ppermute | solution.py:190
  78.5 51.5 %collective-permute-start.7 = (bf16[192,1024]{1,0:T(8,128)(2,1)S(1)}, bf16[192,1024]{1,0:T(8,128)(2,1)S(1)}, u32[]{:S(2)}, u32[]{:S(2)}) collective-permute-start(bf16[192,1024]{1,0:T(8,128)(2,1)S(1)} %collective-permute-done.6.f_ref), channel_id=1, source_target_pairs={{112,128},{128,144},{144,160},{160,176},{176,192},{192,208},{208,2... | collective-permute-start | bytes 1179656 | tf_op jit(solution)/shard_map/ppermute | solution.py:190
  79.2 55.0 %collective-permute-start.9 = (bf16[192,1024]{1,0:T(8,128)(2,1)S(1)}, bf16[192,1024]{1,0:T(8,128)(2,1)S(1)}, u32[]{:S(2)}, u32[]{:S(2)}) collective-permute-start(bf16[192,1024]{1,0:T(8,128)(2,1)S(1)} %pad_maximum_fusion.own_ref), channel_id=1, source_target_pairs={{80,240},{81,241},{82,242},{83,243},{84,244},{85,245},{86,246},{87... | collective-permute-start | bytes 1179656 | tf_op jit(solution)/shard_map/ppermute | solution.py:190
  114.4 19.8 %collective-permute-start.19 = (bf16[192,1024]{1,0:T(8,128)(2,1)S(1)}, bf16[192,1024]{1,0:T(8,128)(2,1)S(1)}, u32[]{:S(2)}, u32[]{:S(2)}) collective-permute-start(bf16[192,1024]{1,0:T(8,128)(2,1)S(1)} %shard_map.58.refs_0_), channel_id=1, source_target_pairs={{240,224},{224,208},{208,192},{192,176},{176,160},{241,225},{225,2... | collective-permute-start | bytes 1179656 | tf_op jit(solution)/shard_map/ppermute | solution.py:190
  130.0 4.5 %collective-permute-start.8 = (bf16[192,1024]{1,0:T(8,128)(2,1)S(1)}, bf16[192,1024]{1,0:T(8,128)(2,1)S(1)}, u32[]{:S(2)}, u32[]{:S(2)}) collective-permute-start(bf16[192,1024]{1,0:T(8,128)(2,1)S(1)} %collective-permute-done.7.f_ref), channel_id=1, source_target_pairs={{128,144},{144,160},{160,176},{176,192},{192,208},{208,224},{224,2... | collective-permute-start | bytes 1179656 | tf_op jit(solution)/shard_map/ppermute | solution.py:190
  134.5 1.3 copy-start
